TPU v7x, 512 devices: a 8x2x16 block of a 8x8x16 slice. The times are simulated.
512 devices in a mesh: groups: 2 (over y), users: 16 (over z), routers: 8 (over x), heads: 2 (over core).
Axes of the slice: x: 8, y: 2, z: 16, core: 2. Of those that a mesh axis runs over, the one named last changes fastest.
The devices are a block of a 8x8x16 slice.
Arguments:
- items: bfloat16 [4096, 64, 1024], P(('groups', 'users', 'routers')), parts along dimension 0, may hold values from -6 to 6
- block_owner: int32 [4096, 1], P(('groups', 'users', 'routers')), parts along dimension 0, may hold values from 0 to 15; in each aligned block of 16 rows (0 to 15, 16 to 31, ...) at most 2 rows name the same one
- block_user: int32 [4096], P(('groups', 'users', 'routers')), parts along dimension 0, may hold values from 0 to 1
- block_fill: int32 [4096], P(('groups', 'users', 'routers')), parts along dimension 0, may hold values from 1 to 64
- prefix_keys: bfloat16 [64, 256, 1024], P(('groups', 'users'), None, 'heads'), parts along dimension 0, may hold values from -6 to 6
- prefix_values: bfloat16 [64, 256, 1024], P(('groups', 'users'), None, 'heads'), parts along dimension 0, may hold values from -6 to 6
- w_in: bfloat16 [4, 1024, 1024], P(None, 'routers', 'heads'), may hold values from -0.1875 to 0.1875
- attn_gain: bfloat16 [1024], P('heads'), may hold values from 0.25 to 1.75
- w_o: bfloat16 [1024, 1024], P('heads', 'routers'), may hold values from -0.1875 to 0.1875
- mlp_gain: bfloat16 [1024], replicated, may hold values from 0.25 to 1.75
- w_one: bfloat16 [1024, 256], replicated, may hold values from -0.1875 to 0.1875
- w_two: bfloat16 [256], replicated, may hold values from -0.375 to 0.375
Outputs:
- scores: float32 [4096, 64], P(('groups', 'users', 'routers')), parts along dimension 0
There are 2 independent parts, one for each index of `groups`. A program takes and returns all parts, laid end to end along the dimension named above; an argument that names none is the same for every part. Nothing has to cross between parts.
Inputs may be any that keep to these rules, and one draw needn't show every extreme that they name: `block_owner`: within the rows of one device (aligned blocks of 16 blocks), no owner is named by more than 2 rows, and in every draw some owner is named by exactly 2 rows of some device.
All inputs are finite; a program needn't handle non-finite values.
Results may differ from a plain program's by a relative error of at most 0.005.
Values may be sent and summed in bfloat16 or wider, within the bound.
No kernel may reach another device: no remote copies, remote signals or barrier semaphores. Data moves between devices by JAX's collectives and lax.ppermute only.
A program may use at most 64 MiB of HBM per device.

v0:
```python
import jax
import jax.numpy as jnp
from jax import lax
from jax.sharding import PartitionSpec as P

D = 1024
HEAD_DIM = 128
CAP = 2
HD = 1024


EPSILON = 1e-05


def items_in_groups(x, axis, split_dim, concat_dim, work, item_dim, out_dim):

    def moved(group):
        return lax.all_to_all(group, axis, split_axis=split_dim, concat_axis=concat_dim, tiled=True)

    items = jax.tree.leaves(x)[0].shape[item_dim]
    ends = [items * k // 2 for k in range(2 + 1)] if items % 2 == 0 else [0, items]
    groups = [
        jax.tree.map(lambda a: lax.slice_in_dim(a, low, high, axis=item_dim), x)
        for low, high in zip(ends, ends[1:])
    ]
    arrived = [moved(group) for group in groups]
    made = [work(group) for group in arrived]
    return jax.tree.map(lambda *parts: jnp.concatenate(parts, axis=out_dim), *made)


def in_blocks(x, dim, peers):
    shape = x.shape
    tiles = x.reshape(*shape[:dim], peers, shape[dim] // peers, *shape[dim + 1 :])
    return jnp.moveaxis(tiles, dim, 0)


def sent_and_summed(x, axis, dim):
    tiles = in_blocks(x, dim, lax.axis_size(axis))
    arrived = lax.all_to_all(tiles, axis, split_axis=0, concat_axis=0, tiled=True)
    return arrived.sum(axis=0)


def sent_to_all(x, axis):
    copies = jnp.broadcast_to(x, (lax.axis_size(axis), *x.shape))
    return lax.all_to_all(copies, axis, split_axis=0, concat_axis=0, tiled=True)


def taken_together(x, axis):
    return sent_to_all(x, axis).sum(axis=0)


def prefix_attention(group_queries, group_users, prefix_keys, prefix_values):
    group_size, block_width, half_width = group_queries.shape
    heads_here = half_width // HEAD_DIM
    safe_user = jnp.maximum(group_users, 0)
    user_keys = jnp.take(prefix_keys, safe_user, axis=0)
    user_values = jnp.take(prefix_values, safe_user, axis=0)
    query_heads = group_queries.reshape(group_size, block_width, heads_here, HEAD_DIM)
    key_heads = user_keys.reshape(group_size, -1, heads_here, HEAD_DIM)
    value_heads = user_values.reshape(group_size, -1, heads_here, HEAD_DIM)
    raw_scores = jnp.einsum(
        "gqhd,gkhd->ghqk", query_heads, key_heads, preferred_element_type=jnp.float32
    ) * HEAD_DIM ** (-0.5)
    weights = jax.nn.silu(raw_scores).astype(jnp.bfloat16)
    summed = jnp.einsum("ghqk,gkhd->gqhd", weights, value_heads, preferred_element_type=jnp.float32)
    return summed.reshape(group_size, block_width, half_width).astype(jnp.bfloat16)


def local(
    items,
    block_owner,
    block_user,
    block_fill,
    prefix_keys,
    prefix_values,
    w_in,
    attn_gain,
    w_o,
    mlp_gain,
    w_one,
    w_two,
):
    blocks, block_width, model_width = items.shape
    row_count = blocks * block_width
    half_width = w_in.shape[2]
    heads_here = half_width // HEAD_DIM
    peer_count = lax.axis_size("users")
    slot_count = peer_count * CAP
    score_scale = HEAD_DIM ** (-0.5)
    flat_items = items.reshape(row_count, model_width)
    projected = jnp.einsum(
        "rk,pkc->prc",
        flat_items,
        lax.all_gather(w_in, "routers", axis=1, tiled=True),
        preferred_element_type=jnp.float32,
    )
    activated = jax.nn.silu(projected)
    queries = activated[0].astype(jnp.bfloat16)
    target = block_owner[:, 0]
    earlier = lax.broadcasted_iota(jnp.int32, (blocks, blocks), 1) < lax.broadcasted_iota(
        jnp.int32, (blocks, blocks), 0
    )
    same_target = target[:, None] == target[None, :]
    dest_rank = jnp.sum((same_target & earlier).astype(jnp.int32), axis=1)
    position = target * CAP + dest_rank
    selector = lax.broadcasted_iota(jnp.int32, (slot_count, blocks), 0) == position[None, :]
    block_queries = queries.reshape(blocks, block_width * half_width)
    outgoing = jnp.dot(
        selector.astype(jnp.bfloat16), block_queries, preferred_element_type=jnp.float32
    ).astype(jnp.bfloat16)
    outgoing = outgoing.reshape(peer_count, CAP, block_width, half_width)
    slot_user = jnp.sum(jnp.where(selector, block_user[None, :] + 1, 0), axis=1) - 1
    slot_user = slot_user.reshape(peer_count, CAP)

    def serve_slots(received):
        arrived, arrived_users = received
        sources, per_source = arrived_users.shape
        total_slots = sources * per_source
        flat_queries = arrived.reshape(total_slots, block_width, half_width)
        flat_users = arrived_users.reshape(total_slots)
        packing = jnp.argsort((flat_users < 0).astype(jnp.int32), stable=True)
        used_slots = jnp.sum((flat_users >= 0).astype(jnp.int32))
        packed_queries = jnp.take(flat_queries, packing, axis=0)
        packed_users = jnp.take(flat_users, packing, axis=0)
        needed = (used_slots + 3) // 4

        def attend_group(group_index, buffer):
            first_slot = group_index * 4
            group_queries = lax.dynamic_slice_in_dim(packed_queries, first_slot, 4, 0)
            group_users = lax.dynamic_slice_in_dim(packed_users, first_slot, 4, 0)
            result = prefix_attention(group_queries, group_users, prefix_keys, prefix_values)
            return lax.dynamic_update_slice_in_dim(buffer, result, first_slot, 0)

        packed_out = lax.fori_loop(
            0, needed, attend_group, jnp.zeros((total_slots, block_width, half_width), jnp.bfloat16)
        )
        inverse = jnp.argsort(packing)
        attended_slots = jnp.take(packed_out, inverse, axis=0)
        return lax.all_to_all(
            attended_slots.reshape(sources, per_source, block_width, half_width),
            "users",
            split_axis=0,
            concat_axis=0,
            tiled=True,
        )

    returned = items_in_groups((outgoing, slot_user), "users", 0, 0, serve_slots, 1, 1)
    prefix_part = jnp.take(returned.reshape(slot_count, block_width * half_width), position, axis=0)
    prefix_part = prefix_part.reshape(row_count, heads_here, HEAD_DIM).astype(jnp.float32)
    query_heads = queries.astype(jnp.float32).reshape(row_count, heads_here, HEAD_DIM)
    self_keys = activated[1].reshape(row_count, heads_here, HEAD_DIM)
    self_values = activated[2].reshape(row_count, heads_here, HEAD_DIM)
    own_term = (
        jax.nn.silu(jnp.sum(query_heads * self_keys, axis=-1) * score_scale)[..., None]
        * self_values
    )
    attended = (prefix_part + own_term).reshape(row_count, half_width)
    totals = lax.psum((jnp.sum(attended, axis=1), jnp.sum(attended * attended, axis=1)), "heads")
    row_mean = totals[0] / HD
    row_var = totals[1] / HD - row_mean * row_mean
    gated = (
        (attended - row_mean[:, None])
        * lax.rsqrt(row_var + EPSILON)[:, None]
        * attn_gain.astype(jnp.float32)
        * activated[3]
    ).astype(jnp.bfloat16)
    partial_out = jnp.dot(
        gated,
        lax.all_gather(w_o, "routers", axis=1, tiled=True),
        preferred_element_type=jnp.float32,
    )
    head_share = sent_and_summed(partial_out, "heads", 1)
    share_cols = head_share.shape[1]
    offset = lax.axis_index("heads") * share_cols
    residual = (
        lax.dynamic_slice_in_dim(flat_items, offset, share_cols, 1).astype(jnp.float32) + head_share
    )
    squares = lax.psum(jnp.sum(residual * residual, axis=1), "heads")
    row_scale = lax.rsqrt(squares / D + EPSILON)
    gain_part = lax.dynamic_slice_in_dim(mlp_gain, offset, share_cols, 0)
    normed = (residual * row_scale[:, None] * gain_part.astype(jnp.float32)).astype(jnp.bfloat16)
    weight_part = lax.dynamic_slice_in_dim(w_one, offset, share_cols, 0)
    inner_sum = taken_together(
        jnp.dot(normed, weight_part, preferred_element_type=jnp.float32), "heads"
    )
    hidden = jax.nn.silu(inner_sum).astype(jnp.bfloat16)
    block_scores = jnp.dot(hidden, w_two, preferred_element_type=jnp.float32).reshape(
        blocks, block_width
    )
    is_valid = lax.broadcasted_iota(jnp.int32, (blocks, block_width), 1) < block_fill[:, None]
    return jnp.where(is_valid, block_scores, jnp.zeros_like(block_scores))


def solution(mesh):
    placed = (
        P(("groups", "users", "routers"), None, None),
        P(("groups", "users", "routers"), None),
        P(("groups", "users", "routers")),
        P(("groups", "users", "routers")),
        P(("groups", "users"), None, "heads"),
        P(("groups", "users"), None, "heads"),
        P(None, "routers", "heads"),
        P("heads"),
        P("heads", "routers"),
        P(),
        P(),
        P(),
    )
    return jax.shard_map(
        local,
        mesh=mesh,
        in_specs=placed,
        out_specs=P(("groups", "users", "routers"), None),
        check_vma=False,
    )
```

profile of v0, /device:TPU:78, one launch (start us, length us, event | category | flops | bytes accessed | tf_op | source)
XLA Modules:
  0.0 425.1 jit_solution(11410321025123503344)
XLA Ops:
  6.6 2.1 copy.77
  11.2 43.7 %all-to-all-start.3 = ((s32[16,1,1]{2,1,0:T(1,128)}), s32[16,1,1]{2,1,0:T(1,128)S(1)}, u32[]{:S(2)}, u32[]{:S(2)}) async-start(s32[16,1,1]{2,1,0:T(1,128)} %bitcast.11), calls=%async_computation.3 | async-start | bytes 16384 | tf_op jit(solution)/shard_map/all_to_all | solution.py:18
  54.8 58.0 %all-gather.3.cloned.1.call-done = bf16[4,1024,512]{1,2,0:T(8,128)(2,1)} async-done(((bf16[4,128,512]{1,2,0:T(8,128)(2,1)}), bf16[4,1024,512]{1,2,0:T(8,128)(2,1)}) %all-gather.3.cloned.1.call-update) | async-done | bytes 4194320 | tf_op jit(solution)/shard_map/all_gather | solution.py:94
  112.9 7.8 %bitcast_multiply_fusion = f32[4,1024,512]{1,2,0:T(8,128)S(1)} fusion(bf16[4,1024,512]{1,2,0:T(8,128)(2,1)} %all-gather.3.cloned.1.call-done, bf16[1024,1024,1]{1,0,2:T(8,128)(2,1)} %bitcast.171), kind=kOutput, calls=%fused_computation.54 | convolution fusion | flops 4303355904 | bytes 14680064 | tf_op jit(solution)/shard_map/rk,pkc->prc/dot_general | solution.py:91
  120.7 3.2 copy-done.3
  123.9 1.9 slice_multiply_fusion.1
  128.4 10.5 %all-to-all-start = ((s32[16,1,1]{2,1,0:T(1,128)}), s32[16,1,1]{2,1,0:T(1,128)S(1)}, u32[]{:S(2)}, u32[]{:S(2)}) async-start(s32[16,1,1]{2,1,0:T(1,128)} %bitcast.6), calls=%async_computation | async-start | bytes 16384 | tf_op jit(solution)/shard_map/all_to_all | solution.py:18
  140.4 10.7 %all-to-all-done = s32[16,1,1]{2,1,0:T(1,128)S(1)} async-done(((s32[16,1,1]{2,1,0:T(1,128)}), s32[16,1,1]{2,1,0:T(1,128)S(1)}, u32[]{:S(2)}, u32[]{:S(2)}) %all-to-all-start) | async-done | bytes 96 | tf_op jit(solution)/shard_map/all_to_all | solution.py:18
  151.2 4.1 all-to-all-start.4
  165.2 32.7 %all-to-all-done.4 = bf16[16,1,64,512]{3,2,1,0:T(8,128)(2,1)S(1)} async-done(((bf16[16,1,64,512]{3,2,1,0:T(8,128)(2,1)}), bf16[16,1,64,512]{3,2,1,0:T(8,128)(2,1)S(1)}, u32[]{:S(2)}, u32[]{:S(2)}) %all-to-all-start.4) | async-done | bytes 1048608 | tf_op jit(solution)/shard_map/all_to_all | solution.py:18
  197.9 9.1 %all-to-all-start.1 = ((bf16[16,1,64,512]{3,2,1,0:T(8,128)(2,1)}), bf16[16,1,64,512]{3,2,1,0:T(8,128)(2,1)}, u32[]{:S(2)}, u32[]{:S(2)}) async-start(bf16[16,1,64,512]{3,2,1,0:T(8,128)(2,1)} %get-tuple-element.142), calls=%async_computation.1 | async-start | bytes 2097152 | tf_op jit(solution)/shard_map/all_to_all | solution.py:18
  207.1 1.8 gather_fusion.9
  211.2 1.8 gather_fusion.10
  214.1 40.2 %all-to-all-done.1 = bf16[16,1,64,512]{3,2,1,0:T(8,128)(2,1)} async-done(((bf16[16,1,64,512]{3,2,1,0:T(8,128)(2,1)}), bf16[16,1,64,512]{3,2,1,0:T(8,128)(2,1)}, u32[]{:S(2)}, u32[]{:S(2)}) %all-to-all-start.1) | async-done | bytes 1048608 | tf_op jit(solution)/shard_map/all_to_all | solution.py:18
  254.4 9.1 %all-to-all-start.5 = ((bf16[16,1,64,512]{3,2,1,0:T(8,128)(2,1)}), bf16[16,1,64,512]{3,2,1,0:T(8,128)(2,1)}, u32[]{:S(2)}, u32[]{:S(2)}) async-start(bf16[16,1,64,512]{3,2,1,0:T(8,128)(2,1)} %select_bitcast_fusion.4), calls=%async_computation.5 | async-start | bytes 2097152 | tf_op jit(solution)/shard_map/all_to_all | solution.py:139
  263.5 1.8 gather_fusion.6
  267.6 32.9 %while.20 = (s32[]{:T(128)}, bf16[16,64,512]{2,1,0:T(8,128)(2,1)}, s32[]{:T(128)}, s32[16]{0:T(128)S(1)}, bf16[2,256,512]{2,1,0:T(8,128)(2,1)S(1)}, /*index=5*/b...) while((s32[]{:T(128)}, bf16[16,64,512]{2,1,0:T(8,128)(2,1)}, ...), condition=%wide.region_5.9_spmd, body=%wide.region_4.8_spmd.sunk | while | flops 136971280 | bytes 11538695 | solution.py:134
  268.3 1.6 gather_fusion.1
  269.9 2.8 select_bitcast_fusion.8
  272.7 2.4 fusion.76
  276.5 1.6 gather_fusion.1
  278.1 2.8 select_bitcast_fusion.8
  280.9 2.4 fusion.76
  284.7 1.6 gather_fusion.1
  286.3 2.8 select_bitcast_fusion.8
  289.1 2.4 fusion.76
  293.0 1.6 gather_fusion.1
  294.6 2.8 select_bitcast_fusion.8
  297.4 2.4 fusion.76
  300.5 1.8 gather_fusion.7
  303.5 9.5 %all-to-all-done.5 = bf16[16,1,64,512]{3,2,1,0:T(8,128)(2,1)} async-done(((bf16[16,1,64,512]{3,2,1,0:T(8,128)(2,1)}), bf16[16,1,64,512]{3,2,1,0:T(8,128)(2,1)}, u32[]{:S(2)}, u32[]{:S(2)}) %all-to-all-start.5) | async-done | bytes 1048608 | tf_op jit(solution)/shard_map/all_to_all | solution.py:139
  313.1 8.2 %all-to-all-start.2 = ((bf16[16,1,64,512]{3,2,1,0:T(8,128)(2,1)}), bf16[16,1,64,512]{3,2,1,0:T(8,128)(2,1)}, u32[]{:S(2)}, u32[]{:S(2)}) async-start(bf16[16,1,64,512]{3,2,1,0:T(8,128)(2,1)} %select_bitcast_fusion.5), calls=%async_computation.2 | async-start | bytes 2097152 | tf_op jit(solution)/shard_map/all_to_all | solution.py:139
  322.4 46.5 %all-gather.5.cloned.1.call-done = bf16[512,1024]{1,0:T(8,128)(2,1)} async-done(((bf16[512,128]{1,0:T(8,128)(2,1)}), bf16[512,1024]{1,0:T(8,128)(2,1)}) %all-gather.5.cloned.1.call-update) | async-done | bytes 1048592 | tf_op jit(solution)/shard_map/all_gather | solution.py:169
  368.8 2.3 copy.82
  371.3 1.7 pad_maximum_fusion
  374.3 2.2 gather_fusion.4
  376.5 2.5 gather.19
  381.8 1.5 copy.80
  383.2 2.1 fusion.43
  385.3 2.5 all-reduce
  387.9 2.9 fusion.37
  392.1 8.2 %all_to_all.48 = f32[2,1024,512]{2,1,0:T(8,128)} all-to-all(f32[2,1024,512]{2,1,0:T(8,128)S(1)} %convolution_bitcast_fusion), channel_id=1, replica_groups=mesh['groups'=2,'users'=16,'routers'=8,'heads'=2] {'heads'}, dimensions={0} | all-to-all | bytes 8388608 | tf_op jit(solution)/shard_map/all_to_all | solution.py:39
  400.3 2.9 reduce_sum.100
  403.2 1.6 multiply_reduce_fusion
  404.8 2.5 psum.23
  407.3 1.7 fusion.44
  409.2 5.4 %all_to_all.49 = f32[2,1024,256]{2,1,0:T(8,128)S(1)} all-to-all(f32[2,1024,256]{2,1,0:T(8,128)S(1)} %broadcast_in_dim.74), channel_id=1, replica_groups=mesh['groups'=2,'users'=16,'routers'=8,'heads'=2] {'heads'}, dimensions={0} | all-to-all | bytes 4194304 | tf_op jit(solution)/shard_map/all_to_all | solution.py:45
  415.8 1.6 fusion.49
  (112 shorter events, 36.4 us)
Async XLA Ops:
  6.5 400.7 %copy-start = (bf16[1024,256]{1,0:T(8,128)(2,1)S(1)}, bf16[1024,256]{1,0:T(8,128)(2,1)}, u32[]{:S(2)}) copy-start(bf16[1024,256]{1,0:T(8,128)(2,1)} %param.32) | copy-start | bytes 1572868
  6.6 106.3 %all-gather.3.cloned.1.call-start = ((), (), s32[]{:S(2)}) async-start(), calls=%async_computation.8 | async-start | bytes 4718592 | tf_op jit(solution)/shard_map/all_gather | solution.py:94
  11.2 117.3 %all-to-all-start.3 = ((s32[16,1,1]{2,1,0:T(1,128)}), s32[16,1,1]{2,1,0:T(1,128)S(1)}, u32[]{:S(2)}, u32[]{:S(2)}) async-start(s32[16,1,1]{2,1,0:T(1,128)} %bitcast.11), calls=%async_computation.3 | async-start | bytes 16384 | tf_op jit(solution)/shard_map/all_to_all | solution.py:18
  120.7 3.2 copy-start.3
  128.4 22.7 %all-to-all-start = ((s32[16,1,1]{2,1,0:T(1,128)}), s32[16,1,1]{2,1,0:T(1,128)S(1)}, u32[]{:S(2)}, u32[]{:S(2)}) async-start(s32[16,1,1]{2,1,0:T(1,128)} %bitcast.6), calls=%async_computation | async-start | bytes 16384 | tf_op jit(solution)/shard_map/all_to_all | solution.py:18
  151.2 46.7 %all-to-all-start.4 = ((bf16[16,1,64,512]{3,2,1,0:T(8,128)(2,1)}), bf16[16,1,64,512]{3,2,1,0:T(8,128)(2,1)S(1)}, u32[]{:S(2)}, u32[]{:S(2)}) async-start(bf16[16,1,64,512]{3,2,1,0:T(8,128)(2,1)} %get-tuple-element.143), calls=%async_computation.4 | async-start | bytes 2097152 | tf_op jit(solution)/shard_map/all_to_all | solution.py:18
  197.9 9.2 %copy-start.6 = (bf16[16,1,64,512]{3,2,1,0:T(8,128)(2,1)}, bf16[16,1,64,512]{3,2,1,0:T(8,128)(2,1)S(1)}, u32[]{:S(2)}) copy-start(bf16[16,1,64,512]{3,2,1,0:T(8,128)(2,1)S(1)} %all-to-all-done.4) | copy-start | bytes 3145732
  197.9 56.5 %all-to-all-start.1 = ((bf16[16,1,64,512]{3,2,1,0:T(8,128)(2,1)}), bf16[16,1,64,512]{3,2,1,0:T(8,128)(2,1)}, u32[]{:S(2)}, u32[]{:S(2)}) async-start(bf16[16,1,64,512]{3,2,1,0:T(8,128)(2,1)} %get-tuple-element.142), calls=%async_computation.1 | async-start | bytes 2097152 | tf_op jit(solution)/shard_map/all_to_all | solution.py:18
  208.9 2.3 copy-start.1
  208.9 2.2 copy-start.2
  254.4 58.7 %all-to-all-start.5 = ((bf16[16,1,64,512]{3,2,1,0:T(8,128)(2,1)}), bf16[16,1,64,512]{3,2,1,0:T(8,128)(2,1)}, u32[]{:S(2)}, u32[]{:S(2)}) async-start(bf16[16,1,64,512]{3,2,1,0:T(8,128)(2,1)} %select_bitcast_fusion.4), calls=%async_computation.5 | async-start | bytes 2097152 | tf_op jit(solution)/shard_map/all_to_all | solution.py:139
  302.4 19.7 %copy-start.12 = (bf16[256]{0:T(256)(128)(2,1)S(1)}, bf16[256]{0:T(256)(128)(2,1)}, u32[]{:S(2)}) copy-start(bf16[256]{0:T(256)(128)(2,1)} %param.33) | copy-start | bytes 1540
  302.4 19.7 %copy-start.9 = (bf16[512]{0:T(512)(128)(2,1)S(1)}, bf16[512]{0:T(512)(128)(2,1)}, u32[]{:S(2)}) copy-start(bf16[512]{0:T(512)(128)(2,1)} %param.29) | copy-start | bytes 3076
  302.4 19.7 %copy-start.8 = (s32[16,1]{0,1:T(1,128)S(1)}, s32[16,1]{0,1:T(1,128)}, u32[]{:S(2)}) copy-start(s32[16,1]{0,1:T(1,128)} %param.23) | copy-start | bytes 196
  302.4 19.9 %copy-start.10 = (bf16[1024]{0:T(1024)(128)(2,1)S(1)}, bf16[1024]{0:T(1024)(128)(2,1)}, u32[]{:S(2)}) copy-start(bf16[1024]{0:T(1024)(128)(2,1)} %param.31) | copy-start | bytes 6148
  303.5 67.6 %copy-start.5 = (f32[1,1024,512]{1,2,0:T(8,128)S(1)}, f32[1,1024,512]{1,2,0:T(8,128)}, u32[]{:S(2)}) copy-start(f32[1,1024,512]{1,2,0:T(8,128)} %get-tuple-element.136) | copy-start | bytes 6291460
  313.1 58.3 %all-to-all-start.2 = ((bf16[16,1,64,512]{3,2,1,0:T(8,128)(2,1)}), bf16[16,1,64,512]{3,2,1,0:T(8,128)(2,1)}, u32[]{:S(2)}, u32[]{:S(2)}) async-start(bf16[16,1,64,512]{3,2,1,0:T(8,128)(2,1)} %select_bitcast_fusion.5), calls=%async_computation.2 | async-start | bytes 2097152 | tf_op jit(solution)/shard_map/all_to_all | solution.py:139
  321.2 47.6 %all-gather.5.cloned.1.call-start = ((), (), s32[]{:S(2)}) async-start(), calls=%async_computation.9 | async-start | bytes 1179648 | tf_op jit(solution)/shard_map/all_gather | solution.py:169
  376.5 2.5 copy-start.4
  387.9 2.9 copy-start.7
  415.8 1.7 copy-start.11
Sparse Core Ops, SparseCore 0:
  9.4 103.4 all-gather.2
  324.1 44.6 all-gather.4
where the time goes:
time: 431 us; the launch traced here: 425 us
  waiting for transfers between devices  198 us (46%)
  starting transfers between devices  84.7 us (20%)
  local copies, waits for them, and re-layouts  44.8 us (10%)
  other arithmetic  40.3 us (9%)
  matrix products  22.9 us (5%)
  blocking collectives  18.7 us (4%)
  between operations  15.1 us (4%)
    all_to_all x4, waiting for transfers between devices, moved(): lax.all_to_all(group, axis, split_axis=split_dim, concat_axis=concat_dim,...  83.7 us
    all_to_all x4, starting transfers between devices, moved(): lax.all_to_all(group, axis, split_axis=split_dim, concat_axis=concat_dim,...  67.4 us
    all_gather x1, waiting for transfers between devices, local(): lax.all_gather(w_in, 'routers', axis=1, tiled=True)  58 us
    all_gather x1, waiting for transfers between devices, local(): lax.all_gather(w_o, 'routers', axis=1, tiled=True)  46.5 us
    all_to_all x2, starting transfers between devices, serve_slots(): lax.all_to_all(attended_slots.reshape(sources, per_source, block_width, h...  17.2 us
    while x4, other arithmetic  11.1 us
    dot_general x4, matrix products, prefix_attention(): jnp.einsum('ghqk,gkhd->gqhd', weights, value_heads, preferred_element_typ...  9.6 us
    all_to_all x2, waiting for transfers between devices, serve_slots(): lax.all_to_all(attended_slots.reshape(sources, per_source, block_width, h...  9.54 us
  transfers between devices with their start and end apart: 8, of which 6 were waited for; matrix products, arithmetic and copies ran while one was open for 18% of the time, Pallas kernels for 0%

commit v1 on v0

v1 whole, which is shorter than its diff:
```python
import functools

import jax
import jax.numpy as jnp
from jax import lax
from jax.experimental import pallas as pl
from jax.experimental.pallas import tpu as pltpu
from jax.sharding import PartitionSpec as P

HEAD_DIM = 128
CAP = 2
EPSILON = 1e-05
TILE = 256
CHUNK = 256
ALIGN = 16
USER_CODE = 128


def half_silu(half):
    return half * (1.0 + jnp.tanh(half))


def score_kernel(
    code_ref,
    x_ref,
    kt_own,
    kt_other,
    v_own,
    v_other,
    w_own,
    w_other,
    gain_own,
    gain_other,
    wo_own,
    wo_other,
    mlp_gain_ref,
    w_one_ref,
    w_two_ref,
    out_ref,
    rows_ref,
    query_ref,
    prefix_ref,
    own_ref,
    gate_ref,
    score_ref,
    unit_ref,
    offset_ref,
):
    units, unit_rows, width = x_ref.shape
    half_width = v_own.shape[2]
    scale = HEAD_DIM ** (-0.5)

    def place(user, start):
        def step(unit, position):
            code = code_ref[unit]
            count = code % USER_CODE
            mine = (count > 0) & (code // USER_CODE == user)

            @pl.when(mine)
            def _():
                at = pl.multiple_of(position, ALIGN)
                rows_ref[pl.ds(at, unit_rows), :] = x_ref[unit]
                offset_ref[unit] = position

            padded = (count + ALIGN - 1) // ALIGN * ALIGN
            return position + jnp.where(mine, padded, 0)

        return lax.fori_loop(0, units, step, start)

    boundary = place(0, jnp.int32(0))
    total = place(1, boundary)

    def attend(user, queries, kt_ref, values_ref, low):
        raw = jnp.dot(
            queries, kt_ref[user, low : low + HEAD_DIM, :], preferred_element_type=jnp.float32
        )
        weights = half_silu(raw * (0.5 * scale)).astype(jnp.bfloat16)
        return jnp.dot(
            weights,
            values_ref[user, :, low : low + HEAD_DIM],
            preferred_element_type=jnp.float32,
        ).astype(jnp.bfloat16)

    sides = ((kt_own, v_own, w_own, gain_own, wo_own), (kt_other, v_other, w_other, gain_other, wo_other))

    def tile_step(tile, carry):
        start = pl.multiple_of(tile * TILE, TILE)
        x = rows_ref[pl.ds(start, TILE), :]
        first_user = jnp.where(start < boundary, 0, 1)
        mixed = (start < boundary) & (start + TILE > boundary) & (total > boundary)
        for side, (kt_ref, values_ref, w_ref, _, _) in enumerate(sides):
            for low in range(0, half_width, CHUNK):
                at = side * half_width + low

                def projected(which):
                    weight = w_ref[:, which, :, low : low + CHUNK].reshape(width, CHUNK)
                    return half_silu(jnp.dot(x, weight, preferred_element_type=jnp.float32) * 0.5)

                queries = projected(0).astype(jnp.bfloat16)
                query_ref[:, at : at + CHUNK] = queries
                keys = projected(1)
                values = projected(2)
                gate_ref[:, at : at + CHUNK] = projected(3)
                for inner in range(0, CHUNK, HEAD_DIM):
                    part = slice(inner, inner + HEAD_DIM)
                    place_at = slice(at + inner, at + inner + HEAD_DIM)
                    raw = jnp.sum(
                        queries[:, part].astype(jnp.float32) * keys[:, part], axis=1, keepdims=True
                    )
                    own_ref[:, place_at] = half_silu(raw * (0.5 * scale)) * values[:, part]
                    prefix_ref[:, place_at] = attend(
                        first_user, queries[:, part], kt_ref, values_ref, low + inner
                    )

        @pl.when(mixed)
        def _():
            row = start + lax.broadcasted_iota(jnp.int32, (TILE, HEAD_DIM), 0)
            for side, (kt_ref, values_ref, _, _, _) in enumerate(sides):
                for low in range(0, half_width, HEAD_DIM):
                    place_at = slice(side * half_width + low, side * half_width + low + HEAD_DIM)
                    second = attend(1, query_ref[:, place_at], kt_ref, values_ref, low)
                    prefix_ref[:, place_at] = jnp.where(
                        row < boundary, prefix_ref[:, place_at].astype(jnp.float32), second.astype(jnp.float32)
                    ).astype(jnp.bfloat16)

        attended = prefix_ref[...].astype(jnp.float32) + own_ref[...]
        row_mean = jnp.sum(attended, axis=1, keepdims=True) / width
        row_var = jnp.sum(attended * attended, axis=1, keepdims=True) / width - row_mean * row_mean
        inverse = lax.rsqrt(row_var + EPSILON)
        residual = x.astype(jnp.float32)
        for side, (_, _, _, gain_ref, wo_ref) in enumerate(sides):
            part = slice(side * half_width, (side + 1) * half_width)
            gated = (
                (attended[:, part] - row_mean)
                * inverse
                * gain_ref[...].astype(jnp.float32)
                * gate_ref[:, part]
            ).astype(jnp.bfloat16)
            residual = residual + jnp.dot(gated, wo_ref[...], preferred_element_type=jnp.float32)
        squares = jnp.sum(residual * residual, axis=1, keepdims=True)
        normed = (
            residual * lax.rsqrt(squares / width + EPSILON) * mlp_gain_ref[...].astype(jnp.float32)
        ).astype(jnp.bfloat16)
        inner_sum = jnp.dot(normed, w_one_ref[...], preferred_element_type=jnp.float32)
        hidden = half_silu(inner_sum * 0.5).astype(jnp.bfloat16).astype(jnp.float32)
        scores = jnp.sum(hidden * w_two_ref[...].astype(jnp.float32), axis=1, keepdims=True)
        score_ref[pl.ds(start, TILE), :] = jnp.broadcast_to(scores, (TILE, score_ref.shape[1]))
        return carry

    lax.fori_loop(0, (total + TILE - 1) // TILE, tile_step, 0)

    lanes = score_ref.shape[1]
    unit_row = lax.broadcasted_iota(jnp.int32, (unit_rows, lanes), 0)

    def unplace(unit, carry):
        count = code_ref[unit] % USER_CODE
        to = pl.multiple_of(unit * unit_rows, unit_rows)

        @pl.when(count > 0)
        def _():
            at = pl.multiple_of(offset_ref[unit], ALIGN)
            found = score_ref[pl.ds(at, unit_rows), :]
            unit_ref[pl.ds(to, unit_rows), :] = jnp.where(unit_row < count, found, 0.0)

        @pl.when(count == 0)
        def _():
            unit_ref[pl.ds(to, unit_rows), :] = jnp.zeros((unit_rows, lanes), jnp.float32)

        return carry

    lax.fori_loop(0, units, unplace, 0)
    for block in range(units * unit_rows // lanes):
        out_ref[block : block + 1, :] = unit_ref[block * lanes : (block + 1) * lanes, :].T[0:1, :]


def score_units(codes, x, own, other, mlp_gain, w_one, w_two, interpret=False):
    units, unit_rows, width = x.shape
    kt, values, w, gain, wo = own
    kt2, values2, w2, gain2, wo2 = other
    lanes = 128
    rows = units * unit_rows
    room = (rows + TILE - 1) // TILE * TILE + max(TILE, unit_rows)
    vmem = pl.BlockSpec(memory_space=pltpu.VMEM)
    return pl.pallas_call(
        score_kernel,
        out_shape=jax.ShapeDtypeStruct((rows // lanes, lanes), jnp.float32),
        in_specs=[pl.BlockSpec(memory_space=pltpu.SMEM)] + [vmem] * 14,
        out_specs=vmem,
        scratch_shapes=[
            pltpu.VMEM((room, width), jnp.bfloat16),
            pltpu.VMEM((TILE, width), jnp.bfloat16),
            pltpu.VMEM((TILE, width), jnp.bfloat16),
            pltpu.VMEM((TILE, width), jnp.float32),
            pltpu.VMEM((TILE, width), jnp.float32),
            pltpu.VMEM((room, lanes), jnp.float32),
            pltpu.VMEM((rows, lanes), jnp.float32),
            pltpu.SMEM((units,), jnp.int32),
        ],
        compiler_params=pltpu.CompilerParams(vmem_limit_bytes=56 * 1024 * 1024),
        name="score_units",
        interpret=interpret,
    )(
        codes, x, kt, kt2, values, values2, w, w2, gain, gain2, wo, wo2, mlp_gain, w_one, w_two
    )


INTERPRET = False


def local(
    items,
    block_owner,
    block_user,
    block_fill,
    prefix_keys,
    prefix_values,
    w_in,
    attn_gain,
    w_o,
    mlp_gain,
    w_one,
    w_two,
):
    blocks, block_width, model_width = items.shape
    peers = lax.axis_size("users")
    cores = lax.axis_size("heads")
    core = lax.axis_index("heads")
    slots = peers * CAP
    unit_rows = block_width // cores
    flat_items = items.reshape(blocks * block_width, model_width)

    def swapped(x):
        return lax.ppermute(x, "heads", [(k, cores - 1 - k) for k in range(cores)])

    target = block_owner[:, 0]
    earlier = lax.broadcasted_iota(jnp.int32, (blocks, blocks), 1) < lax.broadcasted_iota(
        jnp.int32, (blocks, blocks), 0
    )
    same_target = target[:, None] == target[None, :]
    position = target * CAP + jnp.sum((same_target & earlier).astype(jnp.int32), axis=1)
    selector = lax.broadcasted_iota(jnp.int32, (slots, blocks), 0) == position[None, :]
    code = block_user * USER_CODE + (block_fill + (cores - 1 - core)) // cores
    codes = jnp.sum(jnp.where(selector, code[None, :], 0), axis=1).reshape(peers, CAP)

    inside = lax.broadcasted_iota(jnp.int32, (blocks, block_width), 1)
    goes_to = jnp.where(
        inside % cores == core, position[:, None] * unit_rows + inside // cores, -1
    ).reshape(1, blocks * block_width)
    pick = lax.broadcasted_iota(jnp.int32, (slots * unit_rows, 1), 0) == goes_to
    outgoing = jnp.dot(
        pick.astype(jnp.bfloat16), flat_items, preferred_element_type=jnp.float32
    ).astype(jnp.bfloat16)
    outgoing = outgoing.reshape(peers, CAP * unit_rows, model_width)

    arrived = lax.all_to_all(outgoing, "users", split_axis=0, concat_axis=0, tiled=True)
    arrived_codes = lax.all_to_all(codes, "users", split_axis=0, concat_axis=0, tiled=True)

    w_all = lax.all_gather(w_in, "routers", axis=0)
    wo_all = lax.all_gather(w_o, "routers", axis=1, tiled=True)
    own = (
        jnp.swapaxes(prefix_keys, 1, 2),
        prefix_values,
        w_all,
        attn_gain[None, :],
        wo_all,
    )
    other = jax.tree.map(swapped, own)
    scores = score_units(
        arrived_codes.reshape(slots),
        arrived.reshape(slots, unit_rows, model_width),
        own,
        other,
        mlp_gain[None, :],
        w_one,
        w_two[None, :],
        interpret=INTERPRET,
    )
    scores = scores.reshape(peers, 1, CAP * unit_rows)
    back = jnp.broadcast_to(scores, (peers, cores, CAP * unit_rows)).reshape(peers * cores, -1)
    returned = lax.all_to_all(back, ("users", "heads"), split_axis=0, concat_axis=0, tiled=True)
    returned = returned.reshape(peers, cores, CAP, unit_rows).transpose(0, 2, 3, 1)
    returned = returned.reshape(slots, block_width)
    block_scores = jnp.sum(jnp.where(selector[:, :, None], returned[:, None, :], 0.0), axis=0)
    is_valid = lax.broadcasted_iota(jnp.int32, (blocks, block_width), 1) < block_fill[:, None]
    return jnp.where(is_valid, block_scores, jnp.zeros_like(block_scores))


def solution(mesh):
    placed = (
        P(("groups", "users", "routers"), None, None),
        P(("groups", "users", "routers"), None),
        P(("groups", "users", "routers")),
        P(("groups", "users", "routers")),
        P(("groups", "users"), None, "heads"),
        P(("groups", "users"), None, "heads"),
        P(None, "routers", "heads"),
        P("heads"),
        P("heads", "routers"),
        P(),
        P(),
        P(),
    )
    return jax.shard_map(
        local,
        mesh=mesh,
        in_specs=placed,
        out_specs=P(("groups", "users", "routers"), None),
        check_vma=False,
    )
```

time: 431 us -> 228 us (0.53)
  waiting for transfers between devices: 198 us -> 99.8 us
  local copies, waits for them, and re-layouts: 44.8 us -> 7.01 us
  other arithmetic: 40.3 us -> 4.67 us
  matrix products: 22.9 us -> 3.66 us
  blocking collectives: 18.7 us -> 0 us
  Pallas kernels: 0 us -> 18.6 us
  starting transfers between devices: 84.7 us -> 78.8 us
    all_to_all x6 -> x3, waiting for transfers between devices: 93.2 us -> 21.5 us  [the longest x1 11.6 us: local(): lax.all_to_all(back, ('users', 'heads'), split_axis=0, concat_axis=0, til...]
    all_gather x2, waiting for transfers between devices: 104 us -> 77.5 us  [the longest x1 46.4 us: local(): wo_all = lax.all_gather(w_o, 'routers', axis=1, tiled=True)]
    gather x19 -> x0, local copies, waits for them, and re-layouts: 26.5 us -> none  [the longest x5 8.97 us: local(): jnp.take(returned.reshape(slot_count, block_width * half_width), position...]
    dot_general x9 -> x1, matrix products: 22.9 us -> 3.66 us  [local(): jnp.dot(pick.astype(jnp.bfloat16), flat_items, preferred_element_type=jnp...]
    pallas_call x0 -> x1, Pallas kernels: none -> 18.6 us  [score_units(): pl.pallas_call(score_kernel, out_shape=jax.ShapeDtypeStruct((rows // lane...]
    all_to_all x6 -> x3, starting transfers between devices: 84.7 us -> 68 us  [the longest x1 43.7 us: local(): lax.all_to_all(codes, 'users', split_axis=0, concat_axis=0, tiled=True)]
    all_to_all x2 -> x0, blocking collectives: 13.6 us -> none  [the longest x1 8.19 us: sent_and_summed(): lax.all_to_all(tiles, axis, split_axis=0, concat_axis=0, tiled=True)]
    while x4 -> x0, other arithmetic: 11.1 us -> none
  transfers between devices with their start and end apart: 8 -> 10, of which waited for: 6 -> 5; matrix products, arithmetic and copies ran while one was open for 18% -> 5% of each run, Pallas kernels for 0% -> 0%
where the time goes in v1:
time: 228 us; the launch traced here: 226 us
  waiting for transfers between devices  99.8 us (44%)
  starting transfers between devices  78.8 us (35%)
  Pallas kernels  18.6 us (8%)
  between operations  13.7 us (6%)
  local copies, waits for them, and re-layouts  7.01 us (3%)
  other arithmetic  4.67 us (2%)
  matrix products  3.66 us (2%)
    all_gather x1, waiting for transfers between devices, local(): wo_all = lax.all_gather(w_o, 'routers', axis=1, tiled=True)  46.4 us
    all_to_all x1, starting transfers between devices, local(): lax.all_to_all(codes, 'users', split_axis=0, concat_axis=0, tiled=True)  43.7 us
    all_gather x1, waiting for transfers between devices, local(): w_all = lax.all_gather(w_in, 'routers', axis=0)  31.1 us
    all_to_all x1, starting transfers between devices, local(): lax.all_to_all(back, ('users', 'heads'), split_axis=0, concat_axis=0, til...  19.4 us
    pallas_call x1, Pallas kernels, score_units(): pl.pallas_call(score_kernel, out_shape=jax.ShapeDtypeStruct((rows // lane...  18.6 us
    all_to_all x1, waiting for transfers between devices, local(): lax.all_to_all(back, ('users', 'heads'), split_axis=0, concat_axis=0, til...  11.6 us
    ppermute x5, starting transfers between devices, swapped(): return lax.ppermute(x, 'heads', [(k, cores - 1 - k) for k in range(cores)])  10.7 us
    all_to_all x1, waiting for transfers between devices, local(): lax.all_to_all(codes, 'users', split_axis=0, concat_axis=0, tiled=True)  7.68 us
  transfers between devices with their start and end apart: 10, of which 5 were waited for; matrix products, arithmetic and copies ran while one was open for 5% of the time, Pallas kernels for 0%

profile of v1, /device:TPU:78, one launch (start us, length us, event | category | flops | bytes accessed | tf_op | source)
XLA Modules:
  0.0 226.2 jit_solution(10874103599611195429)
XLA Ops:
  6.6 0.7 all-gather.6.cloned.1.call-update
  7.3 0.9 convert_reduce_fusion
  8.2 0.7 fusion.7
  8.9 0.1 select_reduce_fusion.1
  9.0 0.7 all_to_all.15
  9.7 43.7 %all-to-all-start = ((s32[16,1,2]{2,1,0:T(1,128)}), s32[16,1,2]{2,1,0:T(1,128)S(1)}, u32[]{:S(2)}, u32[]{:S(2)}) async-start(s32[16,1,2]{2,1,0:T(1,128)} %bitcast.1), calls=%async_computation | async-start | bytes 16384 | tf_op jit(solution)/shard_map/all_to_all | solution.py:256
  53.4 0.7 fusion.6
  54.1 0.1 add_select_fusion
  54.2 0.1 select_n.55
  54.2 3.7 %fusion.2 = bf16[1024,1024]{1,0:T(8,128)(2,1)} fusion(bf16[1024,1024]{1,0:T(8,128)(2,1)S(1)} %bitcast.21, s32[1024]{0:T(1024)S(1)} %select_n.55), kind=kOutput, calls=%fused_computation.3 | convolution fusion | flops 2149580800 | bytes 4198400 | tf_op jit(solution)/shard_map/dot_general | solution.py:250
  57.9 7.7 %all-to-all-done = s32[16,1,2]{2,1,0:T(1,128)S(1)} async-done(((s32[16,1,2]{2,1,0:T(1,128)}), s32[16,1,2]{2,1,0:T(1,128)S(1)}, u32[]{:S(2)}, u32[]{:S(2)}) %all-to-all-start) | async-done | bytes 160 | tf_op jit(solution)/shard_map/all_to_all | solution.py:256
  65.6 5.0 %all-to-all-start.1 = ((bf16[16,64,1024]{2,1,0:T(8,128)(2,1)}), bf16[16,64,1024]{2,1,0:T(8,128)(2,1)}, u32[]{:S(2)}, u32[]{:S(2)}) async-start(bf16[16,64,1024]{2,1,0:T(8,128)(2,1)} %bitcast.26), calls=%async_computation.1 | async-start | bytes 4194304 | tf_op jit(solution)/shard_map/all_to_all | solution.py:255
  70.6 0.1 all-gather.4.cloned.1.call-start
  70.6 31.1 %all-gather.6.cloned.1.call-done = bf16[32,128,512]{2,1,0:T(8,128)(2,1)} async-done(((bf16[4,128,512]{2,1,0:T(8,128)(2,1)}), bf16[32,128,512]{2,1,0:T(8,128)(2,1)}) %all-gather.6.cloned.1.call-update) | async-done | bytes 4194320 | tf_op jit(solution)/shard_map/all_gather | solution.py:258
  101.8 1.9 collective-permute-start.2
  103.7 0.1 all-gather.4.cloned.1.call-update
  103.8 46.4 %all-gather.4.cloned.1.call-done.wo_own = bf16[512,1024]{1,0:T(8,128)(2,1)} async-done(((bf16[512,128]{1,0:T(8,128)(2,1)}), bf16[512,1024]{1,0:T(8,128)(2,1)}) %all-gather.4.cloned.1.call-update) | async-done | bytes 1048592 | tf_op jit(solution)/shard_map/all_gather | solution.py:259
  150.1 1.9 collective-permute-start.4
  152.1 1.2 copy.21
  153.4 2.4 %collective-permute-start = (bf16[2,512,256]{2,1,0:T(8,128)(2,1)S(1)}, bf16[2,512,256]{2,1,0:T(8,128)(2,1)}, u32[]{:S(2)}, u32[]{:S(2)}) collective-permute-start(bf16[2,512,256]{2,1,0:T(8,128)(2,1)S(1)} %bitcast.24), channel_id=1, source_target_pairs={{0,1},{1,0},{2,3},{3,2},{4,5},{5,4},{6,7},{7,6},{8,9},{9,8},{10,11... | collective-permute-start | bytes 1572872 | tf_op jit(solution)/shard_map/ppermute | solution.py:233
  155.8 2.0 collective-permute-start.1
  157.8 2.4 %collective-permute-start.3 = (bf16[1,512]{1,0:T(2,128)(2,1)S(1)}, bf16[1,512]{1,0:T(2,128)(2,1)S(1)}, u32[]{:S(2)}, u32[]{:S(2)}) collective-permute-start(bf16[1,512]{1,0:T(2,128)(2,1)S(1)} %broadcast_in_dim.66.gain_own), channel_id=1, source_target_pairs={{0,1},{1,0},{2,3},{3,2},{4,5},{5,4},{6,7},{7,6},{8,9},{9,8},{10,11... | collective-permute-start | bytes 3080 | tf_op jit(solution)/shard_map/ppermute | solution.py:233
  160.3 0.6 broadcast_in_dim.67.mlp_gain_ref
  160.9 0.6 broadcast_in_dim.68.w_two_ref
  161.4 0.5 broadcast.126
  162.0 0.6 reduce.6
  162.6 0.7 reshape.128.code_ref
  163.3 0.0 collective-permute-done.3.gain_other
  163.3 0.0 collective-permute-done.kt_other
  163.3 0.0 collective-permute-done.1.v_other
  163.3 0.0 collective-permute-done.4.wo_other
  163.3 2.2 all-to-all-done.1
  165.5 0.0 collective-permute-done.2.w_other
  165.6 0.0 copy-start.6
  165.6 18.6 %score_units.1 = f32[8,128]{1,0:T(8,128)} custom-call(s32[32]{0:T(128)} %reshape.128.code_ref, bf16[32,32,1024]{2,1,0:T(8,128)(2,1)} %bitcast.6.x_ref, bf16[2,512,256]{2,1,0:T(8,128)(2,1)} %bitcast.25, bf16[2,512,256]{2,1,0:T(8,128)(2,1)} %collective-permute-done.kt_other, bf16[2,256,512]{2,1,0:T(8,128)(2,1)} %v_own.1, ...), custom_call_target="tpu_custom_call" | custom-call | tf_op jit(solution)/shard_map/score_units/pallas_call | solution.py:184
  184.2 0.7 broadcast_in_dim.69
  184.9 0.6 broadcast_in_dim.70
  185.5 19.4 %all-to-all-start.2 = ((f32[32,1,64]{2,1,0:T(1,128)}), f32[32,1,64]{2,1,0:T(1,128)S(1)}, u32[]{:S(2)}, u32[]{:S(2)}) async-start(f32[32,1,64]{2,1,0:T(1,128)} %bitcast.9), calls=%async_computation.2 | async-start | bytes 32768 | tf_op jit(solution)/shard_map/all_to_all | solution.py:280
  204.9 0.1 iota_compare_fusion.5
  205.0 0.1 copy.19
  205.1 11.6 %all-to-all-done.2 = f32[32,1,64]{2,1,0:T(1,128)S(1)} async-done(((f32[32,1,64]{2,1,0:T(1,128)}), f32[32,1,64]{2,1,0:T(1,128)S(1)}, u32[]{:S(2)}, u32[]{:S(2)}) %all-to-all-start.2) | async-done | bytes 8224 | tf_op jit(solution)/shard_map/all_to_all | solution.py:280
  216.7 0.5 broadcast.127
  217.2 0.7 reduce.7
  217.9 0.1 reshape.132
  218.0 0.3 copy.22
  218.3 0.3 broadcast_in_dim.71
  218.5 0.1 select_reduce_fusion
  218.7 0.7 fusion.3
  (22 shorter events, 0.1 us)
Async XLA Ops:
  6.5 47.7 %copy-start = (bf16[16,64,1024]{2,1,0:T(8,128)(2,1)S(1)}, bf16[16,64,1024]{2,1,0:T(8,128)(2,1)}, u32[]{:S(2)}) copy-start(bf16[16,64,1024]{2,1,0:T(8,128)(2,1)} %param.12) | copy-start | bytes 6291460
  6.6 95.2 %all-gather.6.cloned.1.call-start = ((), (), s32[]{:S(2)}) async-start(), calls=%async_computation.4 | async-start | bytes 4718592 | tf_op jit(solution)/shard_map/all_gather | solution.py:258
  9.7 55.9 %all-to-all-start = ((s32[16,1,2]{2,1,0:T(1,128)}), s32[16,1,2]{2,1,0:T(1,128)S(1)}, u32[]{:S(2)}, u32[]{:S(2)}) async-start(s32[16,1,2]{2,1,0:T(1,128)} %bitcast.1), calls=%async_computation | async-start | bytes 16384 | tf_op jit(solution)/shard_map/all_to_all | solution.py:256
  65.6 90.2 %copy-start.2 = (bf16[2,256,512]{2,1,0:T(8,128)(2,1)S(1)}, bf16[2,256,512]{2,1,0:T(8,128)(2,1)}, u32[]{:S(2)}) copy-start(bf16[2,256,512]{2,1,0:T(8,128)(2,1)} %v_own.1) | copy-start | bytes 1572868
  65.6 92.2 %copy-start.7 = (bf16[512]{0:T(512)(128)(2,1)S(1)}, bf16[512]{0:T(512)(128)(2,1)}, u32[]{:S(2)}) copy-start(bf16[512]{0:T(512)(128)(2,1)} %param.19) | copy-start | bytes 3076
  65.6 94.7 %copy-start.5 = (bf16[1024]{0:T(1024)(128)(2,1)S(1)}, bf16[1024]{0:T(1024)(128)(2,1)}, u32[]{:S(2)}) copy-start(bf16[1024]{0:T(1024)(128)(2,1)} %param.21) | copy-start | bytes 6148
  65.6 95.3 %copy-start.8 = (bf16[256]{0:T(256)(128)(2,1)S(1)}, bf16[256]{0:T(256)(128)(2,1)}, u32[]{:S(2)}) copy-start(bf16[256]{0:T(256)(128)(2,1)} %param.23) | copy-start | bytes 1540
  65.6 99.9 %all-to-all-start.1 = ((bf16[16,64,1024]{2,1,0:T(8,128)(2,1)}), bf16[16,64,1024]{2,1,0:T(8,128)(2,1)}, u32[]{:S(2)}, u32[]{:S(2)}) async-start(bf16[16,64,1024]{2,1,0:T(8,128)(2,1)} %bitcast.26), calls=%async_computation.1 | async-start | bytes 4194304 | tf_op jit(solution)/shard_map/all_to_all | solution.py:255
  70.6 79.6 %all-gather.4.cloned.1.call-start = ((), (), s32[]{:S(2)}) async-start(), calls=%async_computation.3 | async-start | bytes 1179648 | tf_op jit(solution)/shard_map/all_gather | solution.py:259
  101.8 63.8 %collective-permute-start.2 = (bf16[8,4,128,512]{3,2,1,0:T(8,128)(2,1)}, bf16[8,4,128,512]{3,2,1,0:T(8,128)(2,1)}, u32[]{:S(2)}, u32[]{:S(2)}) collective-permute-start(bf16[8,4,128,512]{3,2,1,0:T(8,128)(2,1)} %bitcast.22), channel_id=1, source_target_pairs={{0,1},{1,0},{2,3},{3,2},{4,5},{5,4},{6,7},{7,6},{8,9},{9,8},{10,11... | collective-permute-start | bytes 12582920 | tf_op jit(solution)/shard_map/ppermute | solution.py:233
  150.1 13.2 %collective-permute-start.4 = (bf16[512,1024]{1,0:T(8,128)(2,1)}, bf16[512,1024]{1,0:T(8,128)(2,1)}, u32[]{:S(2)}, u32[]{:S(2)}) collective-permute-start(bf16[512,1024]{1,0:T(8,128)(2,1)} %all-gather.4.cloned.1.call-done.wo_own), channel_id=1, source_target_pairs={{0,1},{1,0},{2,3},{3,2},{4,5},{5,4},{6,7},{7,6},{8,9},{9,8},{10,11... | collective-permute-start | bytes 3145736 | tf_op jit(solution)/shard_map/ppermute | solution.py:233
  153.3 12.2 %copy-start.1 = (bf16[2,256,512]{1,2,0:T(8,128)(2,1)}, bf16[2,256,512]{1,2,0:T(8,128)(2,1)S(1)}, u32[]{:S(2)}) copy-start(bf16[2,256,512]{1,2,0:T(8,128)(2,1)S(1)} %copy.21) | copy-start | bytes 1572868
  153.4 9.9 %collective-permute-start = (bf16[2,512,256]{2,1,0:T(8,128)(2,1)S(1)}, bf16[2,512,256]{2,1,0:T(8,128)(2,1)}, u32[]{:S(2)}, u32[]{:S(2)}) collective-permute-start(bf16[2,512,256]{2,1,0:T(8,128)(2,1)S(1)} %bitcast.24), channel_id=1, source_target_pairs={{0,1},{1,0},{2,3},{3,2},{4,5},{5,4},{6,7},{7,6},{8,9},{9,8},{10,11... | collective-permute-start | bytes 1572872 | tf_op jit(solution)/shard_map/ppermute | solution.py:233
  155.8 7.5 %collective-permute-start.1 = (bf16[2,256,512]{2,1,0:T(8,128)(2,1)S(1)}, bf16[2,256,512]{2,1,0:T(8,128)(2,1)}, u32[]{:S(2)}, u32[]{:S(2)}) collective-permute-start(bf16[2,256,512]{2,1,0:T(8,128)(2,1)S(1)} %copy-done.2), channel_id=1, source_target_pairs={{0,1},{1,0},{2,3},{3,2},{4,5},{5,4},{6,7},{7,6},{8,9},{9,8},{10,11... | collective-permute-start | bytes 1572872 | tf_op jit(solution)/shard_map/ppermute | solution.py:233
  157.8 7.8 %copy-start.3 = (bf16[1,512]{1,0:T(2,128)(2,1)}, bf16[1,512]{1,0:T(2,128)(2,1)S(1)}, u32[]{:S(2)}) copy-start(bf16[1,512]{1,0:T(2,128)(2,1)S(1)} %broadcast_in_dim.66.gain_own) | copy-start | bytes 3076
  157.8 5.5 %collective-permute-start.3 = (bf16[1,512]{1,0:T(2,128)(2,1)S(1)}, bf16[1,512]{1,0:T(2,128)(2,1)S(1)}, u32[]{:S(2)}, u32[]{:S(2)}) collective-permute-start(bf16[1,512]{1,0:T(2,128)(2,1)S(1)} %broadcast_in_dim.66.gain_own), channel_id=1, source_target_pairs={{0,1},{1,0},{2,3},{3,2},{4,5},{5,4},{6,7},{7,6},{8,9},{9,8},{10,11... | collective-permute-start | bytes 3080 | tf_op jit(solution)/shard_map/ppermute | solution.py:233
  163.3 2.3 copy-start.4
  165.6 53.1 %copy-start.6 = (s32[16]{0:T(128)S(1)}, s32[16]{0:T(128)}, u32[]{:S(2)}) copy-start(s32[16]{0:T(128)} %param.15) | copy-start | bytes 196
  185.5 31.1 %all-to-all-start.2 = ((f32[32,1,64]{2,1,0:T(1,128)}), f32[32,1,64]{2,1,0:T(1,128)S(1)}, u32[]{:S(2)}, u32[]{:S(2)}) async-start(f32[32,1,64]{2,1,0:T(1,128)} %bitcast.9), calls=%async_computation.2 | async-start | bytes 32768 | tf_op jit(solution)/shard_map/all_to_all | solution.py:280
Sparse Core Ops, SparseCore 0:
  9.4 92.2 all-gather.5
  103.9 46.2 all-gather.3

commit v2 on v1

v2 whole, which is shorter than its diff:
```python
import functools

import jax
import jax.numpy as jnp
from jax import lax
from jax.experimental import pallas as pl
from jax.experimental.pallas import tpu as pltpu
from jax.sharding import PartitionSpec as P

HEAD_DIM = 128
EPSILON = 1e-05
TILE = 256
CHUNK = 256
ALIGN = 16
CODE = 256


def half_silu(half):
    return half * (1.0 + jnp.tanh(half))


def score_kernel(
    base,
    code_ref,
    core_ref,
    x_ref,
    kt_own,
    kt_other,
    v_own,
    v_other,
    gain_own,
    gain_other,
    w_ref,
    mlp_gain_ref,
    w_one_ref,
    w_two_ref,
    out_ref,
    rows_ref,
    prefix_ref,
    own_ref,
    gate_ref,
    wo_ref,
    user_ref,
    score_ref,
    unit_ref,
    offset_ref,
):
    units, unit_rows, width = x_ref.shape
    routers, cores, _, share, _ = w_ref.shape
    half_width = v_own.shape[2]
    scale = HEAD_DIM ** (-0.5)
    core = core_ref[0]
    lanes = score_ref.shape[1]
    unit_row = lax.broadcasted_iota(jnp.int32, (unit_rows, lanes), 0)

    def rows_here(count):
        return jnp.clip((count + (cores - 1 - core)) // cores - base, 0, unit_rows)

    def place(unit, position):
        code = code_ref[unit]
        count = rows_here(code % CODE)
        first = rows_here(code // CODE)

        @pl.when(count > 0)
        def _():
            at = pl.multiple_of(position, ALIGN)
            rows_ref[pl.ds(at, unit_rows), :] = x_ref[unit]
            user_ref[pl.ds(at, unit_rows), :] = (unit_row >= first).astype(jnp.int32)

        offset_ref[unit] = position
        return position + (count + ALIGN - 1) // ALIGN * ALIGN

    total = lax.fori_loop(0, units, place, jnp.int32(0))

    sides = ((kt_own, v_own, gain_own, core), (kt_other, v_other, gain_other, cores - 1 - core))
    for side, (_, _, _, index) in enumerate(sides):
        for router in range(routers):
            for row in range(0, half_width, share):
                wo_ref[
                    side * half_width + row : side * half_width + row + share,
                    router * share : (router + 1) * share,
                ] = w_ref[router, index, row // share, :, half_width : half_width + share]

    def attend(user, queries, kt_ref, values_ref, low):
        raw = jnp.dot(
            queries, kt_ref[user, low : low + HEAD_DIM, :], preferred_element_type=jnp.float32
        )
        weights = half_silu(raw * (0.5 * scale)).astype(jnp.bfloat16)
        return jnp.dot(
            weights,
            values_ref[user, :, low : low + HEAD_DIM],
            preferred_element_type=jnp.float32,
        )

    def tile_step(tile, carry):
        start = pl.multiple_of(tile * TILE, TILE)
        x = rows_ref[pl.ds(start, TILE), :]
        second = user_ref[pl.ds(start, TILE), :] > 0
        for side, (kt_ref, values_ref, _, index) in enumerate(sides):
            for low in range(0, half_width, CHUNK):
                at = side * half_width + low

                def projected(which):
                    weight = w_ref[:, index, which, :, low : low + CHUNK].reshape(width, CHUNK)
                    return half_silu(jnp.dot(x, weight, preferred_element_type=jnp.float32) * 0.5)

                queries = projected(0).astype(jnp.bfloat16)
                keys = projected(1)
                values = projected(2)
                gate_ref[:, at : at + CHUNK] = projected(3)
                for inner in range(0, CHUNK, HEAD_DIM):
                    part = slice(inner, inner + HEAD_DIM)
                    place_at = slice(at + inner, at + inner + HEAD_DIM)
                    raw = jnp.sum(
                        queries[:, part].astype(jnp.float32) * keys[:, part], axis=1, keepdims=True
                    )
                    own_ref[:, place_at] = half_silu(raw * (0.5 * scale)) * values[:, part]
                    prefix_ref[:, place_at] = jnp.where(
                        second,
                        attend(1, queries[:, part], kt_ref, values_ref, low + inner),
                        attend(0, queries[:, part], kt_ref, values_ref, low + inner),
                    ).astype(jnp.bfloat16)

        attended = prefix_ref[...].astype(jnp.float32) + own_ref[...]
        row_mean = jnp.sum(attended, axis=1, keepdims=True) / width
        row_var = jnp.sum(attended * attended, axis=1, keepdims=True) / width - row_mean * row_mean
        inverse = lax.rsqrt(row_var + EPSILON)
        residual = x.astype(jnp.float32)
        for side, (_, _, gain_ref, _) in enumerate(sides):
            part = slice(side * half_width, (side + 1) * half_width)
            gated = (
                (attended[:, part] - row_mean)
                * inverse
                * gain_ref[...].astype(jnp.float32)
                * gate_ref[:, part]
            ).astype(jnp.bfloat16)
            residual = residual + jnp.dot(
                gated, wo_ref[part, :], preferred_element_type=jnp.float32
            )
        squares = jnp.sum(residual * residual, axis=1, keepdims=True)
        normed = (
            residual * lax.rsqrt(squares / width + EPSILON) * mlp_gain_ref[...].astype(jnp.float32)
        ).astype(jnp.bfloat16)
        inner_sum = jnp.dot(normed, w_one_ref[...], preferred_element_type=jnp.float32)
        hidden = half_silu(inner_sum * 0.5).astype(jnp.bfloat16).astype(jnp.float32)
        scores = jnp.sum(hidden * w_two_ref[...].astype(jnp.float32), axis=1, keepdims=True)
        score_ref[pl.ds(start, TILE), :] = jnp.broadcast_to(scores, (TILE, lanes))
        return carry

    lax.fori_loop(0, (total + TILE - 1) // TILE, tile_step, 0)

    def unplace(unit, carry):
        count = rows_here(code_ref[unit] % CODE)
        to = pl.multiple_of(unit * unit_rows, unit_rows)

        @pl.when(count > 0)
        def _():
            at = pl.multiple_of(offset_ref[unit], ALIGN)
            found = score_ref[pl.ds(at, unit_rows), :]
            unit_ref[pl.ds(to, unit_rows), :] = jnp.where(unit_row < count, found, 0.0)

        @pl.when(count == 0)
        def _():
            unit_ref[pl.ds(to, unit_rows), :] = jnp.zeros((unit_rows, lanes), jnp.float32)

        return carry

    lax.fori_loop(0, units, unplace, 0)
    for block in range(units * unit_rows // lanes):
        out_ref[block : block + 1, :] = unit_ref[block * lanes : (block + 1) * lanes, :].T[0:1, :]


def score_units(base, codes, core, x, own, other, w_all, mlp_gain, w_one, w_two):
    units, unit_rows, width = x.shape
    kt, values, gain = own
    kt2, values2, gain2 = other
    lanes = 128
    rows = units * unit_rows
    room = (rows + TILE - 1) // TILE * TILE + max(TILE, unit_rows)
    smem = pl.BlockSpec(memory_space=pltpu.SMEM)
    vmem = pl.BlockSpec(memory_space=pltpu.VMEM)
    return pl.pallas_call(
        functools.partial(score_kernel, base),
        out_shape=jax.ShapeDtypeStruct((rows // lanes, lanes), jnp.float32),
        in_specs=[smem] * 2 + [vmem] * 11,
        out_specs=vmem,
        scratch_shapes=[
            pltpu.VMEM((room, width), jnp.bfloat16),
            pltpu.VMEM((TILE, width), jnp.bfloat16),
            pltpu.VMEM((TILE, width), jnp.float32),
            pltpu.VMEM((TILE, width), jnp.float32),
            pltpu.VMEM((2 * values.shape[2], width), jnp.bfloat16),
            pltpu.VMEM((room, lanes), jnp.int32),
            pltpu.VMEM((room, lanes), jnp.float32),
            pltpu.VMEM((rows, lanes), jnp.float32),
            pltpu.SMEM((units,), jnp.int32),
        ],
        compiler_params=pltpu.CompilerParams(vmem_limit_bytes=VMEM_LIMIT),
        name="score_units",
        interpret=INTERPRET,
    )(codes, core, x, kt, kt2, values, values2, gain, gain2, w_all, mlp_gain, w_one, w_two)


INTERPRET = False
VMEM_LIMIT = 28 * 1024 * 1024


def local(
    items,
    block_owner,
    block_user,
    block_fill,
    prefix_keys,
    prefix_values,
    w_in,
    attn_gain,
    w_o,
    mlp_gain,
    w_one,
    w_two,
):
    blocks, block_width, model_width = items.shape
    peers = lax.axis_size("users")
    cores = lax.axis_size("heads")
    routers = lax.axis_size("routers")
    core = lax.axis_index("heads")
    unit_rows = block_width // cores
    flat_items = items.reshape(blocks * block_width, model_width)

    def swapped(x):
        return lax.ppermute(x, "heads", [(k, cores - 1 - k) for k in range(cores)])

    matrices, share, half_width = w_in.shape
    w_local = jnp.concatenate([w_in, w_o.reshape(matrices, share, share)], axis=2)
    w_all = lax.all_gather(w_local, ("routers", "heads"), axis=0)
    w_all = w_all.reshape(routers, cores, matrices, share, half_width + share)

    target = block_owner[:, 0]
    index = jnp.arange(blocks, dtype=jnp.int32)
    same = target[:, None] == target[None, :]
    ahead = (block_user[None, :] < block_user[:, None]) | (
        (block_user[None, :] == block_user[:, None]) & (index[None, :] < index[:, None])
    )
    packed_start = jnp.sum(jnp.where(same & ahead, block_fill[None, :], 0), axis=1)
    inside = lax.broadcasted_iota(jnp.int32, (blocks, block_width), 1)
    packed = packed_start[:, None] + inside
    here = (inside < block_fill[:, None]) & (packed % cores == core)
    goes_to = jnp.where(here, target[:, None] * block_width + packed // cores, -1)
    goes_to = goes_to.reshape(1, blocks * block_width)

    def packed_half(base):
        slot = lax.broadcasted_iota(jnp.int32, (peers * unit_rows, 1), 0)
        slot = slot // unit_rows * block_width + slot % unit_rows + base
        sent = jnp.dot(
            (slot == goes_to).astype(jnp.bfloat16), flat_items, preferred_element_type=jnp.float32
        )
        return sent.astype(jnp.bfloat16).reshape(peers, unit_rows, model_width)

    def exchanged(x):
        return lax.all_to_all(x, "users", split_axis=0, concat_axis=0, tiled=True)

    bases = (0, unit_rows)
    arrived = [exchanged(packed_half(base)) for base in bases]

    goes = target[None, :] == lax.broadcasted_iota(jnp.int32, (peers, blocks), 0)
    weight = jnp.where(block_user == 0, CODE + 1, 1) * block_fill
    codes = jnp.sum(jnp.where(goes, weight[None, :], 0), axis=1)
    every = lax.all_gather(codes, "users", axis=0)
    me = lax.axis_index("users")
    mine = lax.broadcasted_iota(jnp.int32, (peers, peers), 1) == me
    codes = jnp.sum(jnp.where(mine, every, 0), axis=1)

    own = (jnp.swapaxes(prefix_keys, 1, 2), prefix_values, attn_gain[None, :])
    other = jax.tree.map(swapped, own)
    core_index = core.astype(jnp.int32).reshape(1)
    scores = [
        score_units(
            base, codes, core_index, x, own, other, w_all, mlp_gain[None, :], w_one, w_two[None, :]
        ).reshape(peers, unit_rows)
        for base, x in zip(bases, arrived)
    ]
    returned = exchanged(jnp.concatenate(scores, axis=1))
    returned = jnp.concatenate([returned, swapped(returned)], axis=1)
    row_scores = jnp.sum(
        jnp.where(goes[:, :, None], returned[:, None, :], 0.0), axis=0
    )
    lane = jnp.where(packed % cores == core, 0, block_width) + packed // cores
    wanted = lane[:, :, None] == lax.broadcasted_iota(
        jnp.int32, (blocks, block_width, cores * block_width), 2
    )
    block_scores = jnp.sum(jnp.where(wanted, row_scores[:, None, :], 0.0), axis=2)
    return jnp.where(inside < block_fill[:, None], block_scores, jnp.zeros_like(block_scores))


def solution(mesh):
    placed = (
        P(("groups", "users", "routers"), None, None),
        P(("groups", "users", "routers"), None),
        P(("groups", "users", "routers")),
        P(("groups", "users", "routers")),
        P(("groups", "users"), None, "heads"),
        P(("groups", "users"), None, "heads"),
        P(None, "routers", "heads"),
        P("heads"),
        P("heads", "routers"),
        P(),
        P(),
        P(),
    )
    return jax.shard_map(
        local,
        mesh=mesh,
        in_specs=placed,
        out_specs=P(("groups", "users", "routers"), None),
        check_vma=False,
    )
```

time: 228 us -> 253 us (1.11)
  blocking collectives: 0 us -> 78.9 us
  waiting for transfers between devices: 99.8 us -> 48.7 us
  starting transfers between devices: 78.8 us -> 60.1 us
  local copies, waits for them, and re-layouts: 7.01 us -> 19.6 us
    all_gather x2 -> x1, waiting for transfers between devices: 77.5 us -> 0.01 us  [local(): w_all = lax.all_gather(w_local, ('routers', 'heads'), axis=0)]
    unnamed x0 -> x1, blocking collectives: none -> 52.7 us
    all_to_all x0 -> x1, blocking collectives: none -> 26.2 us  [exchanged(): return lax.all_to_all(x, 'users', split_axis=0, concat_axis=0, tiled=True)]
    all_to_all x3 -> x2, waiting for transfers between devices: 21.5 us -> 47.5 us  [exchanged(): return lax.all_to_all(x, 'users', split_axis=0, concat_axis=0, tiled=True)]
    unnamed x19 -> x38, local copies, waits for them, and re-layouts: 1.28 us -> 19 us
    all_to_all x3 -> x2, starting transfers between devices: 68 us -> 51.8 us  [exchanged(): return lax.all_to_all(x, 'users', split_axis=0, concat_axis=0, tiled=True)]
    ppermute x5 -> x4, starting transfers between devices: 10.7 us -> 8.28 us  [swapped(): return lax.ppermute(x, 'heads', [(k, cores - 1 - k) for k in range(cores)])]
    pallas_call x1 -> x2, Pallas kernels: 18.6 us -> 16.4 us  [score_units(): pl.pallas_call(functools.partial(score_kernel, base), out_shape=jax.Shape...]
  transfers between devices with their start and end apart: 10 -> 7, of which waited for: 5 -> 2; matrix products, arithmetic and copies ran while one was open for 5% -> 4% of each run, Pallas kernels for 0% -> 5%
where the time goes in v2:
time: 253 us; the launch traced here: 249 us
  blocking collectives  78.9 us (31%)
  starting transfers between devices  60.1 us (24%)
  waiting for transfers between devices  48.7 us (19%)
  local copies, waits for them, and re-layouts  19.6 us (8%)
  Pallas kernels  16.4 us (6%)
  between operations  14.3 us (6%)
  other arithmetic  6.7 us (3%)
  matrix products  4.59 us (2%)
    unnamed x1, blocking collectives  52.7 us
    all_to_all x2, starting transfers between devices, exchanged(): return lax.all_to_all(x, 'users', split_axis=0, concat_axis=0, tiled=True)  51.8 us
    all_to_all x2, waiting for transfers between devices, exchanged(): return lax.all_to_all(x, 'users', split_axis=0, concat_axis=0, tiled=True)  47.5 us
    all_to_all x1, blocking collectives, exchanged(): return lax.all_to_all(x, 'users', split_axis=0, concat_axis=0, tiled=True)  26.2 us
    unnamed x38, local copies, waits for them, and re-layouts  19 us
    pallas_call x2, Pallas kernels, score_units(): pl.pallas_call(functools.partial(score_kernel, base), out_shape=jax.Shape...  16.4 us
    ppermute x4, starting transfers between devices, swapped(): return lax.ppermute(x, 'heads', [(k, cores - 1 - k) for k in range(cores)])  8.28 us
  transfers between devices with their start and end apart: 7, of which 2 were waited for; matrix products, arithmetic and copies ran while one was open for 4% of the time, Pallas kernels for 5%

profile of v2, /device:TPU:78, one launch (start us, length us, event | category | flops | bytes accessed | tf_op | source)
XLA Modules:
  0.0 249.2 jit_solution(17161125232612642934)
XLA Ops:
  6.6 2.2 pad_maximum_fusion
  8.7 0.1 all-gather.4.cloned.1.call-update
  8.8 0.7 fusion.39
  9.5 0.9 select_reduce_fusion.4
  10.4 0.1 fusion.15
  10.5 0.1 add.125
  10.5 0.7 multiply_bitcast_fusion
  11.2 0.1 add.128
  11.3 0.1 add.129
  11.3 0.7 iota_compare_fusion.3
  12.1 0.1 lt.75
  12.2 2.3 fusion.4
  14.5 43.7 %all-to-all-start = ((bf16[16,32,1024]{2,1,0:T(8,128)(2,1)}), bf16[16,32,1024]{2,1,0:T(8,128)(2,1)S(1)}, u32[]{:S(2)}, u32[]{:S(2)}) async-start(bf16[16,32,1024]{2,1,0:T(8,128)(2,1)} %bitcast.23), calls=%async_computation | async-start | bytes 2097152 | tf_op jit(solution)/shard_map/all_to_all | solution.py:260
  58.2 2.3 fusion.7
  60.5 47.5 %all-to-all-done.x_ref = bf16[16,32,1024]{2,1,0:T(8,128)(2,1)S(1)} async-done(((bf16[16,32,1024]{2,1,0:T(8,128)(2,1)}), bf16[16,32,1024]{2,1,0:T(8,128)(2,1)S(1)}, u32[]{:S(2)}, u32[]{:S(2)}) %all-to-all-start) | async-done | bytes 1048608 | tf_op jit(solution)/shard_map/all_to_all | solution.py:260
  108.0 1.1 copy-done.3
  109.0 8.1 %all-to-all-start.1 = ((bf16[16,32,1024]{2,1,0:T(8,128)(2,1)}), bf16[16,32,1024]{2,1,0:T(8,128)(2,1)}, u32[]{:S(2)}, u32[]{:S(2)}) async-start(bf16[16,32,1024]{2,1,0:T(8,128)(2,1)} %bitcast.22), calls=%async_computation.1 | async-start | bytes 2097152 | tf_op jit(solution)/shard_map/all_to_all | solution.py:260
  117.2 1.2 copy.15
  118.4 2.0 collective-permute-start
  120.4 2.4 collective-permute-start.1
  122.9 2.0 collective-permute-start.2
  124.8 1.3 dynamic-slice
  126.8 0.2 dynamic-update-slice
  127.0 52.7 %all-reduce = s32[256]{0:T(256)S(1)} all-reduce(s32[256]{0:T(256)S(1)} %dynamic-update-slice), channel_id=2, replica_groups=mesh['groups'=2,'users'=16,'routers'=8,'heads'=2] {'users'}, use_global_device_ids=true, to_apply=%add | all-reduce | flops 256 | bytes 2048
  179.7 0.1 reshape.229
  179.8 0.1 select_reduce_fusion.2.code_ref
  180.0 0.8 copy-done.9
  180.8 4.0 %copy-done.1 = bf16[64,128,640]{2,1,0:T(8,128)(2,1)S(1)} copy-done((bf16[64,128,640]{2,1,0:T(8,128)(2,1)S(1)}, bf16[64,128,640]{2,1,0:T(8,128)(2,1)}, u32[]{:S(2)}) %copy-start.1) | copy-done | bytes 10485784
  184.8 1.2 copy-done.4
  186.0 1.0 copy-done.5
  187.0 1.0 copy-done.7
  188.1 1.0 copy-done.10
  189.1 13.1 %score_units.2 = f32[4,128]{1,0:T(4,128)S(1)} custom-call(s32[16]{0:T(128)S(1)} %select_reduce_fusion.2.code_ref, s32[1]{0:T(128)} %bitcast.2.core_ref, bf16[16,32,1024]{2,1,0:T(8,128)(2,1)S(1)} %copy-done.4, bf16[2,512,256]{2,1,0:T(8,128)(2,1)S(1)} %bitcast.20, bf16[2,512,256]{2,1,0:T(8,128)(2,1)S(1)} %copy-done.10, bf16[2,256,512]{2,1,0:T(8,128)(2,1)S(1)} %copy-done.5, ...), custom_call_target="tpu_custom_call" | custom-call | tf_op jit(solution)/shard_map/score_units/pallas_call | solution.py:182
  202.3 0.1 reshape.226
  202.3 0.0 copy-start.2
  202.4 4.0 %copy-done.2 = bf16[64,128,640]{2,1,0:T(8,128)(2,1)S(1)} copy-done((bf16[64,128,640]{2,1,0:T(8,128)(2,1)S(1)}, bf16[64,128,640]{2,1,0:T(8,128)(2,1)}, u32[]{:S(2)}) %copy-start.2) | copy-done | bytes 10485784
  206.3 1.0 copy-done.8
  207.4 1.0 copy-done.11
  208.4 3.3 %score_units.3 = f32[4,128]{1,0:T(4,128)S(1)} custom-call(s32[16]{0:T(128)S(1)} %select_reduce_fusion.2.code_ref, s32[1]{0:T(128)} %bitcast.2.core_ref, bf16[16,32,1024]{2,1,0:T(8,128)(2,1)} %all-to-all-done.1.x_ref, bf16[2,512,256]{2,1,0:T(8,128)(2,1)S(1)} %bitcast.21, bf16[2,512,256]{2,1,0:T(8,128)(2,1)S(1)} %copy-done.11, ...), custom_call_target="tpu_custom_call" | custom-call | tf_op jit(solution)/shard_map/score_units/pallas_call | solution.py:182
  211.7 0.1 reshape.228
  211.8 0.1 pad_maximum_fusion.1
  211.9 26.2 %all_to_all.22 = f32[16,1,64]{2,1,0:T(1,128)S(1)} all-to-all(f32[16,1,64]{2,1,0:T(1,128)S(1)} %bitcast.27), channel_id=1, replica_groups=mesh['groups'=2,'users'=16,'routers'=8,'heads'=2] {'users'}, dimensions={0} | all-to-all | bytes 8192 | tf_op jit(solution)/shard_map/all_to_all | solution.py:260
  238.0 1.9 collective-permute-start.3
  240.0 1.1 collective-permute-done.3
  241.1 0.1 pad_maximum_fusion.2
  241.2 0.1 select_reduce_fusion.1
  241.3 0.4 select_reduce_fusion
  241.7 0.7 broadcast_select_fusion
  (38 shorter events, 0.1 us)
Async XLA Ops:
  6.5 5.6 %copy-start = (bf16[16,64,1024]{2,1,0:T(8,128)(2,1)S(1)}, bf16[16,64,1024]{2,1,0:T(8,128)(2,1)}, u32[]{:S(2)}) copy-start(bf16[16,64,1024]{2,1,0:T(8,128)(2,1)} %param.12) | copy-start | bytes 6291460
  6.6 174.2 %all-gather.4.cloned.1.call-start = ((), (), s32[]{:S(2)}) async-start(), calls=%async_computation.3 | async-start | bytes 11141120 | tf_op jit(solution)/shard_map/all_gather | solution.py:235
  14.5 93.5 %all-to-all-start = ((bf16[16,32,1024]{2,1,0:T(8,128)(2,1)}), bf16[16,32,1024]{2,1,0:T(8,128)(2,1)S(1)}, u32[]{:S(2)}, u32[]{:S(2)}) async-start(bf16[16,32,1024]{2,1,0:T(8,128)(2,1)} %bitcast.23), calls=%async_computation | async-start | bytes 2097152 | tf_op jit(solution)/shard_map/all_to_all | solution.py:260
  60.5 62.4 %copy-start.15 = (bf16[512]{0:T(512)(128)(2,1)S(1)}, bf16[512]{0:T(512)(128)(2,1)}, u32[]{:S(2)}) copy-start(bf16[512]{0:T(512)(128)(2,1)} %param.19) | copy-start | bytes 3076
  60.5 119.4 %copy-start.14 = (bf16[1024]{0:T(1024)(128)(2,1)S(1)}, bf16[1024]{0:T(1024)(128)(2,1)}, u32[]{:S(2)}) copy-start(bf16[1024]{0:T(1024)(128)(2,1)} %param.21) | copy-start | bytes 6148
  60.5 119.5 %copy-start.16 = (bf16[256]{0:T(256)(128)(2,1)S(1)}, bf16[256]{0:T(256)(128)(2,1)}, u32[]{:S(2)}) copy-start(bf16[256]{0:T(256)(128)(2,1)} %param.23) | copy-start | bytes 1540
  108.0 1.1 copy-start.3
  109.0 93.3 %all-to-all-start.1 = ((bf16[16,32,1024]{2,1,0:T(8,128)(2,1)}), bf16[16,32,1024]{2,1,0:T(8,128)(2,1)}, u32[]{:S(2)}, u32[]{:S(2)}) async-start(bf16[16,32,1024]{2,1,0:T(8,128)(2,1)} %bitcast.22), calls=%async_computation.1 | async-start | bytes 2097152 | tf_op jit(solution)/shard_map/all_to_all | solution.py:260
  118.4 61.5 %collective-permute-start = (bf16[2,512,256]{2,1,0:T(8,128)(2,1)S(1)}, bf16[2,512,256]{2,1,0:T(8,128)(2,1)S(1)}, u32[]{:S(2)}, u32[]{:S(2)}) collective-permute-start(bf16[2,512,256]{2,1,0:T(8,128)(2,1)S(1)} %bitcast.19), channel_id=1, source_target_pairs={{0,1},{1,0},{2,3},{3,2},{4,5},{5,4},{6,7},{7,6},{8,9},{9,8},{10,11... | collective-permute-start | bytes 1572872 | tf_op jit(solution)/shard_map/ppermute | solution.py:231
  120.4 60.4 %collective-permute-start.1 = (bf16[2,256,512]{2,1,0:T(8,128)(2,1)}, bf16[2,256,512]{2,1,0:T(8,128)(2,1)}, u32[]{:S(2)}, u32[]{:S(2)}) collective-permute-start(bf16[2,256,512]{2,1,0:T(8,128)(2,1)} %v_own.3), channel_id=1, source_target_pairs={{0,1},{1,0},{2,3},{3,2},{4,5},{5,4},{6,7},{7,6},{8,9},{9,8},{10,11... | collective-permute-start | bytes 1572872 | tf_op jit(solution)/shard_map/ppermute | solution.py:231
  122.9 57.1 %collective-permute-start.2 = (bf16[1,512]{1,0:T(2,128)(2,1)S(1)}, bf16[1,512]{1,0:T(2,128)(2,1)S(1)}, u32[]{:S(2)}, u32[]{:S(2)}) collective-permute-start(bf16[1,512]{1,0:T(2,128)(2,1)S(1)} %broadcast_in_dim.104.gain_own), channel_id=1, source_target_pairs={{0,1},{1,0},{2,3},{3,2},{4,5},{5,4},{6,7},{7,6},{8,9},{9,8},{10,11... | collective-permute-start | bytes 3080 | tf_op jit(solution)/shard_map/ppermute | solution.py:231
  180.0 0.8 copy-start.9
  180.8 4.0 %copy-start.1 = (bf16[64,128,640]{2,1,0:T(8,128)(2,1)S(1)}, bf16[64,128,640]{2,1,0:T(8,128)(2,1)}, u32[]{:S(2)}) copy-start(bf16[64,128,640]{2,1,0:T(8,128)(2,1)} %all-gather.4.cloned.1.call-done) | copy-start | bytes 31457284
  184.8 1.2 copy-start.4
  186.0 1.0 copy-start.5
  187.0 1.0 copy-start.7
  188.1 1.0 copy-start.10
  189.1 13.2 %copy-start.6 = (bf16[2,256,512]{2,1,0:T(8,128)(2,1)S(1)}, bf16[2,256,512]{2,1,0:T(8,128)(2,1)}, u32[]{:S(2)}) copy-start(bf16[2,256,512]{2,1,0:T(8,128)(2,1)} %v_own.3) | copy-start | bytes 1572868
  202.3 4.0 %copy-start.2 = (bf16[64,128,640]{2,1,0:T(8,128)(2,1)S(1)}, bf16[64,128,640]{2,1,0:T(8,128)(2,1)}, u32[]{:S(2)}) copy-start(bf16[64,128,640]{2,1,0:T(8,128)(2,1)} %all-gather.4.cloned.1.call-done) | copy-start | bytes 31457284
  206.3 1.0 copy-start.8
  207.4 1.0 copy-start.11
  208.4 31.5 %copy-start.12 = (s32[16,1]{0,1:T(1,128)S(1)}, s32[16,1]{0,1:T(1,128)}, u32[]{:S(2)}) copy-start(s32[16,1]{0,1:T(1,128)} %param.13) | copy-start | bytes 196
  208.4 33.2 %copy-start.13 = (s32[16]{0:T(128)S(1)}, s32[16]{0:T(128)}, u32[]{:S(2)}) copy-start(s32[16]{0:T(128)} %param.15) | copy-start | bytes 196
  238.0 3.1 %collective-permute-start.3 = (f32[16,64]{1,0:T(8,128)S(1)}, f32[16,64]{1,0:T(8,128)S(1)}, u32[]{:S(2)}, u32[]{:S(2)}) collective-permute-start(f32[16,64]{1,0:T(8,128)S(1)} %bitcast.25), channel_id=1, source_target_pairs={{0,1},{1,0},{2,3},{3,2},{4,5},{5,4},{6,7},{7,6},{8,9},{9,8},{10,11... | collective-permute-start | bytes 12296 | tf_op jit(solution)/shard_map/ppermute | solution.py:231
Sparse Core Ops, SparseCore 0:
  9.5 103.2 all-gather.3

commit v3 on v2

v3 whole, which is shorter than its diff:
```python
import jax
import jax.numpy as jnp
from jax import lax
from jax.experimental import pallas as pl
from jax.experimental.pallas import tpu as pltpu
from jax.sharding import PartitionSpec as P

HEAD_DIM = 128
EPSILON = 1e-05
TILE = 256
CHUNK = 256
ALIGN = 16
CODE = 256


def half_silu(half):
    return half * (1.0 + jnp.tanh(half))


def score_kernel(
    code_ref,
    core_ref,
    gain_own,
    gain_other,
    mlp_gain_ref,
    w_two_ref,
    x_hbm,
    kt_own,
    kt_other,
    v_own,
    v_other,
    w_hbm,
    w_one_hbm,
    out_ref,
    x_ref,
    kt_ref,
    values_ref,
    w_ref,
    wo_ref,
    w_one_ref,
    rows_ref,
    prefix_ref,
    own_ref,
    gate_ref,
    user_ref,
    score_ref,
    unit_ref,
    offset_ref,
    row_sem,
    chunk_sem,
    wo_sem,
    one_sem,
):
    units, unit_rows, width = x_hbm.shape
    routers, cores, matrices, share, _ = w_hbm.shape
    half_width = v_own.shape[2]
    per_side = half_width // CHUNK
    chunks = width // CHUNK
    scale = HEAD_DIM ** (-0.5)
    core = core_ref[0]
    lanes = score_ref.shape[1]
    unit_row = lax.broadcasted_iota(jnp.int32, (unit_rows, lanes), 0)
    sides = ((kt_own, v_own, core), (kt_other, v_other, cores - 1 - core))

    row_copy = pltpu.make_async_copy(x_hbm, x_ref, row_sem.at[0])
    row_copy.start()
    chunk_copies = []
    for chunk in range(chunks):
        kt, values, index = sides[chunk // per_side]
        low = chunk % per_side * CHUNK
        copies = (
            pltpu.make_async_copy(
                w_hbm.at[:, index, :, :, low : low + CHUNK], w_ref.at[chunk], chunk_sem.at[chunk, 0]
            ),
            pltpu.make_async_copy(
                kt.at[:, low : low + CHUNK, :], kt_ref.at[chunk], chunk_sem.at[chunk, 1]
            ),
            pltpu.make_async_copy(
                values.at[:, :, low : low + CHUNK], values_ref.at[chunk], chunk_sem.at[chunk, 2]
            ),
        )
        for copy in copies:
            copy.start()
        chunk_copies.append(copies)
    tail_copies = []
    for side, (_, _, index) in enumerate(sides):
        for router in range(routers):
            tail_copies.append(
                pltpu.make_async_copy(
                    w_hbm.at[router, index, :, :, half_width : half_width + share],
                    wo_ref.at[side, :, :, router * share : (router + 1) * share],
                    wo_sem.at[side, router],
                )
            )
    tail_copies.append(pltpu.make_async_copy(w_one_hbm, w_one_ref, one_sem.at[0]))
    for copy in tail_copies:
        copy.start()

    def rows_here(count):
        return (count + (cores - 1 - core)) // cores

    def place(unit, position):
        code = code_ref[unit]
        count = rows_here(code % CODE)
        first = rows_here(code // CODE)

        @pl.when(count > 0)
        def _():
            at = pl.multiple_of(position, ALIGN)
            rows_ref[pl.ds(at, unit_rows), :] = x_ref[unit]
            user_ref[pl.ds(at, unit_rows), :] = (unit_row >= first).astype(jnp.int32)

        offset_ref[unit] = position
        return position + (count + ALIGN - 1) // ALIGN * ALIGN

    row_copy.wait()
    total = lax.fori_loop(0, units, place, jnp.int32(0))

    def attend(user, queries, chunk, inner):
        raw = jnp.dot(
            queries,
            kt_ref[chunk, user, inner : inner + HEAD_DIM, :],
            preferred_element_type=jnp.float32,
        )
        weights = half_silu(raw * (0.5 * scale)).astype(jnp.bfloat16)
        return jnp.dot(
            weights,
            values_ref[chunk, user, :, inner : inner + HEAD_DIM],
            preferred_element_type=jnp.float32,
        )

    def tile_step(tile, wait):
        start = pl.multiple_of(tile * TILE, TILE)
        x = rows_ref[pl.ds(start, TILE), :]
        second = user_ref[pl.ds(start, TILE), :] > 0
        for chunk in range(chunks):
            at = chunk * CHUNK
            if wait:
                for copy in chunk_copies[chunk]:
                    copy.wait()

            def projected(which):
                weight = w_ref[chunk, :, which].reshape(width, CHUNK)
                return half_silu(jnp.dot(x, weight, preferred_element_type=jnp.float32) * 0.5)

            queries = projected(0).astype(jnp.bfloat16)
            keys = projected(1)
            values = projected(2)
            gate_ref[:, at : at + CHUNK] = projected(3)
            for inner in range(0, CHUNK, HEAD_DIM):
                part = slice(inner, inner + HEAD_DIM)
                place_at = slice(at + inner, at + inner + HEAD_DIM)
                raw = jnp.sum(
                    queries[:, part].astype(jnp.float32) * keys[:, part], axis=1, keepdims=True
                )
                own_ref[:, place_at] = half_silu(raw * (0.5 * scale)) * values[:, part]
                prefix_ref[:, place_at] = jnp.where(
                    second,
                    attend(1, queries[:, part], chunk, inner),
                    attend(0, queries[:, part], chunk, inner),
                ).astype(jnp.bfloat16)

        if wait:
            for copy in tail_copies:
                copy.wait()
        attended = prefix_ref[...].astype(jnp.float32) + own_ref[...]
        row_mean = jnp.sum(attended, axis=1, keepdims=True) / width
        row_var = jnp.sum(attended * attended, axis=1, keepdims=True) / width - row_mean * row_mean
        inverse = lax.rsqrt(row_var + EPSILON)
        residual = x.astype(jnp.float32)
        for side, gain_ref in enumerate((gain_own, gain_other)):
            part = slice(side * half_width, (side + 1) * half_width)
            gated = (
                (attended[:, part] - row_mean)
                * inverse
                * gain_ref[...].astype(jnp.float32)
                * gate_ref[:, part]
            ).astype(jnp.bfloat16)
            residual = residual + jnp.dot(
                gated,
                wo_ref[side].reshape(half_width, width),
                preferred_element_type=jnp.float32,
            )
        squares = jnp.sum(residual * residual, axis=1, keepdims=True)
        normed = (
            residual * lax.rsqrt(squares / width + EPSILON) * mlp_gain_ref[...].astype(jnp.float32)
        ).astype(jnp.bfloat16)
        inner_sum = jnp.dot(normed, w_one_ref[...], preferred_element_type=jnp.float32)
        hidden = half_silu(inner_sum * 0.5).astype(jnp.bfloat16).astype(jnp.float32)
        scores = jnp.sum(hidden * w_two_ref[...].astype(jnp.float32), axis=1, keepdims=True)
        score_ref[pl.ds(start, TILE), :] = jnp.broadcast_to(scores, (TILE, lanes))

    def later_tile(tile, carry):
        tile_step(tile, False)
        return carry

    tile_step(0, True)
    lax.fori_loop(1, (total + TILE - 1) // TILE, later_tile, 0)

    def unplace(unit, carry):
        count = rows_here(code_ref[unit] % CODE)
        to = pl.multiple_of(unit * unit_rows, unit_rows)

        @pl.when(count > 0)
        def _():
            at = pl.multiple_of(offset_ref[unit], ALIGN)
            found = score_ref[pl.ds(at, unit_rows), :]
            unit_ref[pl.ds(to, unit_rows), :] = jnp.where(unit_row < count, found, 0.0)

        @pl.when(count == 0)
        def _():
            unit_ref[pl.ds(to, unit_rows), :] = jnp.zeros((unit_rows, lanes), jnp.float32)

        return carry

    lax.fori_loop(0, units, unplace, 0)
    for block in range(units * unit_rows // lanes):
        out_ref[block : block + 1, :] = unit_ref[block * lanes : (block + 1) * lanes, :].T[0:1, :]


INTERPRET = False
VMEM_LIMIT = 40 * 1024 * 1024


def score_units(codes, core, x, own, other, w_all, mlp_gain, w_one, w_two):
    units, unit_rows, width = x.shape
    kt, values, gain = own
    kt2, values2, gain2 = other
    users, prefix, half_width = values.shape
    routers, cores, matrices, share, _ = w_all.shape
    chunks = width // CHUNK
    lanes = 128
    rows = units * unit_rows
    room = (rows + TILE - 1) // TILE * TILE + max(TILE, unit_rows)
    smem = pl.BlockSpec(memory_space=pltpu.SMEM)
    vmem = pl.BlockSpec(memory_space=pltpu.VMEM)
    hbm = pl.BlockSpec(memory_space=pltpu.HBM)
    return pl.pallas_call(
        score_kernel,
        out_shape=jax.ShapeDtypeStruct((rows // lanes, lanes), jnp.float32),
        in_specs=[smem] * 2 + [vmem] * 4 + [hbm] * 7,
        out_specs=vmem,
        scratch_shapes=[
            pltpu.VMEM(x.shape, jnp.bfloat16),
            pltpu.VMEM((chunks, users, CHUNK, prefix), jnp.bfloat16),
            pltpu.VMEM((chunks, users, prefix, CHUNK), jnp.bfloat16),
            pltpu.VMEM((chunks, routers, matrices, share, CHUNK), jnp.bfloat16),
            pltpu.VMEM((cores, matrices, share, width), jnp.bfloat16),
            pltpu.VMEM(w_one.shape, jnp.bfloat16),
            pltpu.VMEM((room, width), jnp.bfloat16),
            pltpu.VMEM((TILE, width), jnp.bfloat16),
            pltpu.VMEM((TILE, width), jnp.float32),
            pltpu.VMEM((TILE, width), jnp.float32),
            pltpu.VMEM((room, lanes), jnp.int32),
            pltpu.VMEM((room, lanes), jnp.float32),
            pltpu.VMEM((rows, lanes), jnp.float32),
            pltpu.SMEM((units,), jnp.int32),
            pltpu.SemaphoreType.DMA((1,)),
            pltpu.SemaphoreType.DMA((chunks, 3)),
            pltpu.SemaphoreType.DMA((cores, routers)),
            pltpu.SemaphoreType.DMA((1,)),
        ],
        compiler_params=pltpu.CompilerParams(vmem_limit_bytes=VMEM_LIMIT),
        name="score_units",
        interpret=INTERPRET,
    )(codes, core, gain, gain2, mlp_gain, w_two, x, kt, kt2, values, values2, w_all, w_one)


def local(
    items,
    block_owner,
    block_user,
    block_fill,
    prefix_keys,
    prefix_values,
    w_in,
    attn_gain,
    w_o,
    mlp_gain,
    w_one,
    w_two,
):
    blocks, block_width, model_width = items.shape
    peers = lax.axis_size("users")
    cores = lax.axis_size("heads")
    routers = lax.axis_size("routers")
    core = lax.axis_index("heads")
    flat_items = items.reshape(blocks * block_width, model_width)

    def swapped(x):
        return lax.ppermute(x, "heads", [(k, cores - 1 - k) for k in range(cores)])

    def exchanged(x):
        return lax.all_to_all(x, "users", split_axis=0, concat_axis=0, tiled=True)

    target = block_owner[:, 0]
    goes = target[None, :] == lax.broadcasted_iota(jnp.int32, (peers, blocks), 0)
    weight = jnp.where(block_user == 0, CODE + 1, 1) * block_fill
    codes = jnp.sum(jnp.where(goes, weight[None, :], 0), axis=1)
    codes = exchanged(codes.reshape(peers, 1)).reshape(peers)

    index = jnp.arange(blocks, dtype=jnp.int32)
    same = target[:, None] == target[None, :]
    ahead = (block_user[None, :] < block_user[:, None]) | (
        (block_user[None, :] == block_user[:, None]) & (index[None, :] < index[:, None])
    )
    packed_start = jnp.sum(jnp.where(same & ahead, block_fill[None, :], 0), axis=1)
    inside = lax.broadcasted_iota(jnp.int32, (blocks, block_width), 1)
    packed = packed_start[:, None] + inside
    here = (inside < block_fill[:, None]) & (packed % cores == core)
    goes_to = jnp.where(here, target[:, None] * block_width + packed // cores, -1)
    goes_to = goes_to.reshape(1, blocks * block_width)
    slot = lax.broadcasted_iota(jnp.int32, (peers * block_width, 1), 0)
    sent = jnp.dot(
        (slot == goes_to).astype(jnp.bfloat16), flat_items, preferred_element_type=jnp.float32
    ).astype(jnp.bfloat16)
    arrived = exchanged(sent.reshape(peers, block_width, model_width))

    matrices, share, half_width = w_in.shape
    w_local = jnp.concatenate([w_in, w_o.reshape(matrices, share, share)], axis=2)
    w_all = lax.all_gather(w_local, ("routers", "heads"), axis=0)
    w_all = w_all.reshape(routers, cores, matrices, share, half_width + share)
    own = (jnp.swapaxes(prefix_keys, 1, 2), prefix_values, attn_gain[None, :])
    other = jax.tree.map(swapped, own)
    core_index = core.astype(jnp.int32).reshape(1)
    scores = score_units(
        codes, core_index, arrived, own, other, w_all, mlp_gain[None, :], w_one, w_two[None, :]
    ).reshape(peers, block_width)
    returned = exchanged(scores)
    returned = jnp.concatenate([returned, swapped(returned)], axis=1)
    row_scores = jnp.sum(jnp.where(goes[:, :, None], returned[:, None, :], 0.0), axis=0)
    lane = jnp.where(packed % cores == core, 0, block_width) + packed // cores
    wanted = lane[:, :, None] == lax.broadcasted_iota(
        jnp.int32, (blocks, block_width, cores * block_width), 2
    )
    block_scores = jnp.sum(jnp.where(wanted, row_scores[:, None, :], 0.0), axis=2)
    return jnp.where(inside < block_fill[:, None], block_scores, jnp.zeros_like(block_scores))


def solution(mesh):
    placed = (
        P(("groups", "users", "routers"), None, None),
        P(("groups", "users", "routers"), None),
        P(("groups", "users", "routers")),
        P(("groups", "users", "routers")),
        P(("groups", "users"), None, "heads"),
        P(("groups", "users"), None, "heads"),
        P(None, "routers", "heads"),
        P("heads"),
        P("heads", "routers"),
        P(),
        P(),
        P(),
    )
    return jax.shard_map(
        local,
        mesh=mesh,
        in_specs=placed,
        out_specs=P(("groups", "users", "routers"), None),
        check_vma=False,
    )
```

time: 253 us -> 221 us (0.87)
  blocking collectives: 78.9 us -> 23.4 us
  waiting for transfers between devices: 48.7 us -> 95.3 us
  local copies, waits for them, and re-layouts: 19.6 us -> 3.39 us
  starting transfers between devices: 60.1 us -> 57.4 us
    unnamed x1 -> x0, blocking collectives: 52.7 us -> none
    all_to_all x2, waiting for transfers between devices: 47.5 us -> 93.4 us  [exchanged(): return lax.all_to_all(x, 'users', split_axis=0, concat_axis=0, tiled=True)]
    unnamed x38 -> x17, local copies, waits for them, and re-layouts: 19 us -> 2.31 us
    all_to_all x1, blocking collectives: 26.2 us -> 23.4 us  [exchanged(): return lax.all_to_all(x, 'users', split_axis=0, concat_axis=0, tiled=True)]
    all_to_all x2, starting transfers between devices: 51.8 us -> 49.2 us  [exchanged(): return lax.all_to_all(x, 'users', split_axis=0, concat_axis=0, tiled=True)]
    pallas_call x2 -> x1, Pallas kernels: 16.4 us -> 15.1 us  [score_units(): pl.pallas_call(score_kernel, out_shape=jax.ShapeDtypeStruct((rows // lane...]
  transfers between devices with their start and end apart: 7 -> 7, of which waited for: 2 -> 4; matrix products, arithmetic and copies ran while one was open for 4% -> 4% of each run, Pallas kernels for 5% -> 0%
where the time goes in v3:
time: 221 us; the launch traced here: 219 us
  waiting for transfers between devices  95.3 us (43%)
  starting transfers between devices  57.4 us (26%)
  blocking collectives  23.4 us (11%)
  Pallas kernels  15.1 us (7%)
  between operations  13.6 us (6%)
  other arithmetic  6.84 us (3%)
  matrix products  3.67 us (2%)
  local copies, waits for them, and re-layouts  3.39 us (2%)
    all_to_all x2, waiting for transfers between devices, exchanged(): return lax.all_to_all(x, 'users', split_axis=0, concat_axis=0, tiled=True)  93.4 us
    all_to_all x2, starting transfers between devices, exchanged(): return lax.all_to_all(x, 'users', split_axis=0, concat_axis=0, tiled=True)  49.2 us
    all_to_all x1, blocking collectives, exchanged(): return lax.all_to_all(x, 'users', split_axis=0, concat_axis=0, tiled=True)  23.4 us
    pallas_call x1, Pallas kernels, score_units(): pl.pallas_call(score_kernel, out_shape=jax.ShapeDtypeStruct((rows // lane...  15.1 us
    ppermute x4, starting transfers between devices, swapped(): return lax.ppermute(x, 'heads', [(k, cores - 1 - k) for k in range(cores)])  8.28 us
  transfers between devices with their start and end apart: 7, of which 4 were waited for; matrix products, arithmetic and copies ran while one was open for 4% of the time, Pallas kernels for 0%

profile of v3, /device:TPU:78, one launch (start us, length us, event | category | flops | bytes accessed | tf_op | source)
XLA Modules:
  0.0 218.8 jit_solution(10097856581829650919)
XLA Ops:
  6.5 0.0 copy-start
  6.6 0.0 all-gather.3.cloned.1.call-start
  6.6 2.1 pad_maximum_fusion
  8.7 0.1 all-gather.3.cloned.1.call-update
  8.8 0.7 fusion.19
  9.4 0.9 select_reduce_fusion.3
  10.4 0.7 copy.20
  11.0 43.7 %all-to-all-start = ((s32[16,1,1]{2,1,0:T(1,128)}), s32[16,1,1]{2,1,0:T(1,128)S(1)}, u32[]{:S(2)}, u32[]{:S(2)}) async-start(s32[16,1,1]{2,1,0:T(1,128)} %copy.20), calls=%async_computation | async-start | bytes 16384 | tf_op jit(solution)/shard_map/all_to_all | solution.py:294
  54.7 0.1 fusion.4
  54.8 0.1 add.73
  54.9 0.7 multiply_bitcast_fusion
  55.6 0.1 add.76
  55.6 0.1 add.77
  55.7 0.7 iota_compare_fusion.7
  56.4 0.1 lt.64
  56.5 0.0 copy-done
  56.5 3.7 %fusion.2 = bf16[1024,1024]{1,0:T(8,128)(2,1)} fusion(bf16[1024,1024]{1,0:T(8,128)(2,1)S(1)} %bitcast.13, s32[1024]{0:T(1024)S(1)} %fusion.15), kind=kOutput, calls=%fused_computation.3 | convolution fusion | flops 2149580800 | bytes 4198400 | tf_op jit(solution)/shard_map/dot_general | solution.py:314
  60.2 6.7 %all-to-all-done = s32[16,1,1]{2,1,0:T(1,128)S(1)} async-done(((s32[16,1,1]{2,1,0:T(1,128)}), s32[16,1,1]{2,1,0:T(1,128)S(1)}, u32[]{:S(2)}, u32[]{:S(2)}) %all-to-all-start) | async-done | bytes 96 | tf_op jit(solution)/shard_map/all_to_all | solution.py:294
  66.9 0.0 copy-start.1
  66.9 0.0 copy-start.6
  66.9 0.0 copy-start.5
  66.9 0.0 copy-start.7
  66.9 5.5 %all-to-all-start.1 = ((bf16[16,64,1024]{2,1,0:T(8,128)(2,1)}), bf16[16,64,1024]{2,1,0:T(8,128)(2,1)}, u32[]{:S(2)}, u32[]{:S(2)}) async-start(bf16[16,64,1024]{2,1,0:T(8,128)(2,1)} %bitcast.17), calls=%async_computation.1 | async-start | bytes 4194304 | tf_op jit(solution)/shard_map/all_to_all | solution.py:294
  72.4 1.2 copy.21
  73.7 2.0 collective-permute-start.1
  75.6 0.0 copy-done.1
  75.6 2.4 %collective-permute-start.2 = (bf16[2,256,512]{2,1,0:T(8,128)(2,1)S(1)}, bf16[2,256,512]{2,1,0:T(8,128)(2,1)}, u32[]{:S(2)}, u32[]{:S(2)}) collective-permute-start(bf16[2,256,512]{2,1,0:T(8,128)(2,1)S(1)} %copy-done.1), channel_id=1, source_target_pairs={{0,1},{1,0},{2,3},{3,2},{4,5},{5,4},{6,7},{7,6},{8,9},{9,8},{10,11... | collective-permute-start | bytes 1572872 | tf_op jit(solution)/shard_map/ppermute | solution.py:291
  78.1 0.0 copy-done.6
  78.1 2.0 collective-permute-start
  80.1 0.0 copy-done.5
  80.1 0.0 copy-done.7
  80.1 0.4 reduce.code_ref
  80.5 0.7 collective-permute-done.gain_other
  81.2 0.0 collective-permute-done.1.kt_other
  81.2 0.0 collective-permute-done.2.v_other
  81.2 86.7 %all-to-all-done.1.x_hbm = bf16[16,64,1024]{2,1,0:T(8,128)(2,1)} async-done(((bf16[16,64,1024]{2,1,0:T(8,128)(2,1)}), bf16[16,64,1024]{2,1,0:T(8,128)(2,1)}, u32[]{:S(2)}, u32[]{:S(2)}) %all-to-all-start.1) | async-done | bytes 2097184 | tf_op jit(solution)/shard_map/all_to_all | solution.py:294
  167.9 1.0 copy-done.2
  169.0 15.1 %score_units.1 = f32[8,128]{1,0:T(8,128)S(1)} custom-call(s32[16]{0:T(128)S(1)} %reduce.code_ref, s32[1]{0:T(128)} %bitcast.2.core_ref, bf16[1,512]{1,0:T(2,128)(2,1)S(1)} %broadcast_in_dim.100.gain_own, bf16[1,512]{1,0:T(2,128)(2,1)S(1)} %collective-permute-done.gain_other, bf16[1,1024]{1,0:T(2,128)(2,1)S(1)} %broadcast_in_dim.101.mlp_gain_ref, ...), custom_call_target="tpu_custom_call" | custom-call | tf_op jit(solution)/shard_map/score_units/pallas_call | solution.py:238
  184.1 0.1 all_to_all.20
  184.2 23.4 %all_to_all.26 = f32[16,1,64]{2,1,0:T(1,128)S(1)} all-to-all(f32[16,1,64]{2,1,0:T(1,128)S(1)} %bitcast.21), channel_id=1, replica_groups=mesh['groups'=2,'users'=16,'routers'=8,'heads'=2] {'users'}, dimensions={0} | all-to-all | bytes 8192 | tf_op jit(solution)/shard_map/all_to_all | solution.py:294
  207.6 1.9 collective-permute-start.3
  209.5 0.0 copy-done.3
  209.6 1.1 collective-permute-done.3
  210.7 0.1 pad_maximum_fusion.1
  210.7 0.1 select_reduce_fusion.1
  210.9 0.4 select_reduce_fusion
  211.2 0.0 copy-done.4
  211.3 0.7 broadcast_select_fusion
  (9 shorter events, 0.0 us)
Async XLA Ops:
  6.5 50.0 %copy-start = (bf16[16,64,1024]{2,1,0:T(8,128)(2,1)S(1)}, bf16[16,64,1024]{2,1,0:T(8,128)(2,1)}, u32[]{:S(2)}) copy-start(bf16[16,64,1024]{2,1,0:T(8,128)(2,1)} %param.12) | copy-start | bytes 6291460
  6.6 161.4 %all-gather.3.cloned.1.call-start = ((), (), s32[]{:S(2)}) async-start(), calls=%async_computation.3 | async-start | bytes 11141120 | tf_op jit(solution)/shard_map/all_gather | solution.py:321
  11.0 55.9 %all-to-all-start = ((s32[16,1,1]{2,1,0:T(1,128)}), s32[16,1,1]{2,1,0:T(1,128)S(1)}, u32[]{:S(2)}, u32[]{:S(2)}) async-start(s32[16,1,1]{2,1,0:T(1,128)} %copy.20), calls=%async_computation | async-start | bytes 16384 | tf_op jit(solution)/shard_map/all_to_all | solution.py:294
  66.9 8.7 %copy-start.1 = (bf16[2,256,512]{2,1,0:T(8,128)(2,1)S(1)}, bf16[2,256,512]{2,1,0:T(8,128)(2,1)}, u32[]{:S(2)}) copy-start(bf16[2,256,512]{2,1,0:T(8,128)(2,1)} %v_own.1) | copy-start | bytes 1572868
  66.9 11.2 %copy-start.6 = (bf16[512]{0:T(512)(128)(2,1)S(1)}, bf16[512]{0:T(512)(128)(2,1)}, u32[]{:S(2)}) copy-start(bf16[512]{0:T(512)(128)(2,1)} %param.19) | copy-start | bytes 3076
  66.9 13.1 %copy-start.5 = (bf16[1024]{0:T(1024)(128)(2,1)S(1)}, bf16[1024]{0:T(1024)(128)(2,1)}, u32[]{:S(2)}) copy-start(bf16[1024]{0:T(1024)(128)(2,1)} %param.21) | copy-start | bytes 6148
  66.9 13.2 %copy-start.7 = (bf16[256]{0:T(256)(128)(2,1)S(1)}, bf16[256]{0:T(256)(128)(2,1)}, u32[]{:S(2)}) copy-start(bf16[256]{0:T(256)(128)(2,1)} %param.23) | copy-start | bytes 1540
  66.9 101.0 %all-to-all-start.1 = ((bf16[16,64,1024]{2,1,0:T(8,128)(2,1)}), bf16[16,64,1024]{2,1,0:T(8,128)(2,1)}, u32[]{:S(2)}, u32[]{:S(2)}) async-start(bf16[16,64,1024]{2,1,0:T(8,128)(2,1)} %bitcast.17), calls=%async_computation.1 | async-start | bytes 4194304 | tf_op jit(solution)/shard_map/all_to_all | solution.py:294
  73.7 7.5 %collective-permute-start.1 = (bf16[2,512,256]{2,1,0:T(8,128)(2,1)S(1)}, bf16[2,512,256]{2,1,0:T(8,128)(2,1)}, u32[]{:S(2)}, u32[]{:S(2)}) collective-permute-start(bf16[2,512,256]{2,1,0:T(8,128)(2,1)S(1)} %bitcast.14), channel_id=1, source_target_pairs={{0,1},{1,0},{2,3},{3,2},{4,5},{5,4},{6,7},{7,6},{8,9},{9,8},{10,11... | collective-permute-start | bytes 1572872 | tf_op jit(solution)/shard_map/ppermute | solution.py:291
  75.6 5.6 %collective-permute-start.2 = (bf16[2,256,512]{2,1,0:T(8,128)(2,1)S(1)}, bf16[2,256,512]{2,1,0:T(8,128)(2,1)}, u32[]{:S(2)}, u32[]{:S(2)}) collective-permute-start(bf16[2,256,512]{2,1,0:T(8,128)(2,1)S(1)} %copy-done.1), channel_id=1, source_target_pairs={{0,1},{1,0},{2,3},{3,2},{4,5},{5,4},{6,7},{7,6},{8,9},{9,8},{10,11... | collective-permute-start | bytes 1572872 | tf_op jit(solution)/shard_map/ppermute | solution.py:291
  78.1 3.1 %collective-permute-start = (bf16[1,512]{1,0:T(2,128)(2,1)S(1)}, bf16[1,512]{1,0:T(2,128)(2,1)S(1)}, u32[]{:S(2)}, u32[]{:S(2)}) collective-permute-start(bf16[1,512]{1,0:T(2,128)(2,1)S(1)} %broadcast_in_dim.100.gain_own), channel_id=1, source_target_pairs={{0,1},{1,0},{2,3},{3,2},{4,5},{5,4},{6,7},{7,6},{8,9},{9,8},{10,11... | collective-permute-start | bytes 3080 | tf_op jit(solution)/shard_map/ppermute | solution.py:291
  167.9 1.0 copy-start.2
  168.9 40.6 %copy-start.3 = (s32[16,1]{0,1:T(1,128)S(1)}, s32[16,1]{0,1:T(1,128)}, u32[]{:S(2)}) copy-start(s32[16,1]{0,1:T(1,128)} %param.13) | copy-start | bytes 196
  169.0 42.3 %copy-start.4 = (s32[16]{0:T(128)S(1)}, s32[16]{0:T(128)}, u32[]{:S(2)}) copy-start(s32[16]{0:T(128)} %param.15) | copy-start | bytes 196
  207.6 3.1 %collective-permute-start.3 = (f32[16,64]{1,0:T(8,128)S(1)}, f32[16,64]{1,0:T(8,128)S(1)}, u32[]{:S(2)}, u32[]{:S(2)}) collective-permute-start(f32[16,64]{1,0:T(8,128)S(1)} %bitcast.19), channel_id=1, source_target_pairs={{0,1},{1,0},{2,3},{3,2},{4,5},{5,4},{6,7},{7,6},{8,9},{9,8},{10,11... | collective-permute-start | bytes 12296 | tf_op jit(solution)/shard_map/ppermute | solution.py:291
Sparse Core Ops, SparseCore 0:
  9.5 103.2 all-gather.2

commit v4 on v3

--- a/solution.py
+++ b/solution.py
@@ -4,6 +4,7 @@
 from jax.experimental import pallas as pl
 from jax.experimental.pallas import tpu as pltpu
 from jax.sharding import PartitionSpec as P
+
 
 HEAD_DIM = 128
 EPSILON = 1e-05
@@ -29,7 +30,8 @@
     kt_other,
     v_own,
     v_other,
-    w_hbm,
+    w_own,
+    w_other,
     w_one_hbm,
     out_ref,
     x_ref,
@@ -52,42 +54,55 @@
     one_sem,
 ):
     units, unit_rows, width = x_hbm.shape
-    routers, cores, matrices, share, _ = w_hbm.shape
+    routers, _, share, _ = w_own.shape
     half_width = v_own.shape[2]
+    cores = width // half_width
     per_side = half_width // CHUNK
     chunks = width // CHUNK
     scale = HEAD_DIM ** (-0.5)
     core = core_ref[0]
+    router_here = core_ref[1]
     lanes = score_ref.shape[1]
     unit_row = lax.broadcasted_iota(jnp.int32, (unit_rows, lanes), 0)
-    sides = ((kt_own, v_own, core), (kt_other, v_other, cores - 1 - core))
+    sides = ((kt_own, v_own, w_own), (kt_other, v_other, w_other))
+
+    def ring_index(router):
+        ahead = router - router_here
+        return jnp.where(ahead < 0, ahead + routers, ahead)
 
     row_copy = pltpu.make_async_copy(x_hbm, x_ref, row_sem.at[0])
     row_copy.start()
     chunk_copies = []
     for chunk in range(chunks):
-        kt, values, index = sides[chunk // per_side]
+        kt, values, weights = sides[chunk // per_side]
         low = chunk % per_side * CHUNK
-        copies = (
+        copies = [
             pltpu.make_async_copy(
-                w_hbm.at[:, index, :, :, low : low + CHUNK], w_ref.at[chunk], chunk_sem.at[chunk, 0]
+                weights.at[ring_index(router), :, :, low : low + CHUNK],
+                w_ref.at[chunk, router],
+                chunk_sem.at[chunk, router],
+            )
+            for router in range(routers)
+        ]
+        copies += [
+            pltpu.make_async_copy(
+                kt.at[:, low : low + CHUNK, :], kt_ref.at[chunk], chunk_sem.at[chunk, routers]
             ),
             pltpu.make_async_copy(
-                kt.at[:, low : low + CHUNK, :], kt_ref.at[chunk], chunk_sem.at[chunk, 1]
+                values.at[:, :, low : low + CHUNK],
+                values_ref.at[chunk],
+                chunk_sem.at[chunk, routers + 1],
             ),
-            pltpu.make_async_copy(
-                values.at[:, :, low : low + CHUNK], values_ref.at[chunk], chunk_sem.at[chunk, 2]
-            ),
-        )
+        ]
         for copy in copies:
             copy.start()
         chunk_copies.append(copies)
     tail_copies = []
-    for side, (_, _, index) in enumerate(sides):
+    for side, (_, _, weights) in enumerate(sides):
         for router in range(routers):
             tail_copies.append(
                 pltpu.make_async_copy(
-                    w_hbm.at[router, index, :, :, half_width : half_width + share],
+                    weights.at[ring_index(router), :, :, half_width : half_width + share],
                     wo_ref.at[side, :, :, router * share : (router + 1) * share],
                     wo_sem.at[side, router],
                 )
@@ -222,12 +237,13 @@
 VMEM_LIMIT = 40 * 1024 * 1024
 
 
-def score_units(codes, core, x, own, other, w_all, mlp_gain, w_one, w_two):
+def score_units(codes, core, x, own, other, mlp_gain, w_one, w_two):
     units, unit_rows, width = x.shape
-    kt, values, gain = own
-    kt2, values2, gain2 = other
+    kt, values, gain, w = own
+    kt2, values2, gain2, w2 = other
     users, prefix, half_width = values.shape
-    routers, cores, matrices, share, _ = w_all.shape
+    routers, matrices, share, _ = w.shape
+    cores = width // half_width
     chunks = width // CHUNK
     lanes = 128
     rows = units * unit_rows
@@ -238,7 +254,7 @@
     return pl.pallas_call(
         score_kernel,
         out_shape=jax.ShapeDtypeStruct((rows // lanes, lanes), jnp.float32),
-        in_specs=[smem] * 2 + [vmem] * 4 + [hbm] * 7,
+        in_specs=[smem] * 2 + [vmem] * 4 + [hbm] * 8,
         out_specs=vmem,
         scratch_shapes=[
             pltpu.VMEM(x.shape, jnp.bfloat16),
@@ -256,14 +272,14 @@
             pltpu.VMEM((rows, lanes), jnp.float32),
             pltpu.SMEM((units,), jnp.int32),
             pltpu.SemaphoreType.DMA((1,)),
-            pltpu.SemaphoreType.DMA((chunks, 3)),
+            pltpu.SemaphoreType.DMA((chunks, routers + 2)),
             pltpu.SemaphoreType.DMA((cores, routers)),
             pltpu.SemaphoreType.DMA((1,)),
         ],
         compiler_params=pltpu.CompilerParams(vmem_limit_bytes=VMEM_LIMIT),
         name="score_units",
         interpret=INTERPRET,
-    )(codes, core, gain, gain2, mlp_gain, w_two, x, kt, kt2, values, values2, w_all, w_one)
+    )(codes, core, gain, gain2, mlp_gain, w_two, x, kt, kt2, values, values2, w, w2, w_one)
 
 
 def local(
@@ -294,10 +310,7 @@
         return lax.all_to_all(x, "users", split_axis=0, concat_axis=0, tiled=True)
 
     target = block_owner[:, 0]
-    goes = target[None, :] == lax.broadcasted_iota(jnp.int32, (peers, blocks), 0)
-    weight = jnp.where(block_user == 0, CODE + 1, 1) * block_fill
-    codes = jnp.sum(jnp.where(goes, weight[None, :], 0), axis=1)
-    codes = exchanged(codes.reshape(peers, 1)).reshape(peers)
+    me = lax.axis_index("users")
 
     index = jnp.arange(blocks, dtype=jnp.int32)
     same = target[:, None] == target[None, :]
@@ -314,17 +327,47 @@
     sent = jnp.dot(
         (slot == goes_to).astype(jnp.bfloat16), flat_items, preferred_element_type=jnp.float32
     ).astype(jnp.bfloat16)
+    sent, block_user, w_in = lax.optimization_barrier((sent, block_user, w_in))
     arrived = exchanged(sent.reshape(peers, block_width, model_width))
 
-    matrices, share, half_width = w_in.shape
+    goes = target[None, :] == lax.broadcasted_iota(jnp.int32, (peers, blocks), 0)
+    weight = jnp.where(block_user == 0, CODE + 1, 1) * block_fill
+    every = jnp.sum(jnp.where(goes, weight[None, :], 0), axis=1)[None, :]
+    while every.shape[0] < peers:
+        step = every.shape[0]
+        pairs = [(k, (k + step) % peers) for k in range(peers)]
+        every = jnp.concatenate([every, lax.ppermute(every, "users", pairs)], axis=0)
+    source = (me + peers - lax.broadcasted_iota(jnp.int32, (peers, peers, peers), 1)) % peers
+    wanted = (source == lax.broadcasted_iota(jnp.int32, (peers, peers, peers), 0)) & (
+        lax.broadcasted_iota(jnp.int32, (peers, peers, peers), 2) == me
+    )
+    codes = jnp.sum(jnp.where(wanted, every[None], 0), axis=(1, 2))
+
+    matrices, share, _ = w_in.shape
     w_local = jnp.concatenate([w_in, w_o.reshape(matrices, share, share)], axis=2)
-    w_all = lax.all_gather(w_local, ("routers", "heads"), axis=0)
-    w_all = w_all.reshape(routers, cores, matrices, share, half_width + share)
-    own = (jnp.swapaxes(prefix_keys, 1, 2), prefix_values, attn_gain[None, :])
+    up = [(k, (k + 1) % routers) for k in range(routers)]
+    down = [(k, (k - 1) % routers) for k in range(routers)]
+    from_below, from_above = w_local, w_local
+    ring = {0: w_local}
+    for step in range(1, routers // 2):
+        from_below = lax.ppermute(from_below, "routers", up)
+        from_above = lax.ppermute(from_above, "routers", down)
+        ring[routers - step] = from_below
+        ring[step] = from_above
+    half = matrices // 2
+    ring[routers // 2] = jnp.concatenate(
+        [
+            lax.ppermute(from_below[:half], "routers", up),
+            lax.ppermute(from_above[half:], "routers", down),
+        ],
+        axis=0,
+    )
+    w_ring = jnp.stack([ring[k] for k in range(routers)])
+    own = (jnp.swapaxes(prefix_keys, 1, 2), prefix_values, attn_gain[None, :], w_ring)
     other = jax.tree.map(swapped, own)
-    core_index = core.astype(jnp.int32).reshape(1)
+    core_index = jnp.stack([core, lax.axis_index("routers")]).astype(jnp.int32)
     scores = score_units(
-        codes, core_index, arrived, own, other, w_all, mlp_gain[None, :], w_one, w_two[None, :]
+        codes, core_index, arrived, own, other, mlp_gain[None, :], w_one, w_two[None, :]
     ).reshape(peers, block_width)
     returned = exchanged(scores)
     returned = jnp.concatenate([returned, swapped(returned)], axis=1)

time: 221 us -> 249 us (1.13)
  the two profiles are of different devices: /device:TPU:78 before, /device:TPU:65 now
where the time goes in v4:
time: 249 us; the launch traced here: 248 us
  starting transfers between devices  117 us (47%)
  waiting for transfers between devices  71.5 us (29%)
  blocking collectives  21.9 us (9%)
  Pallas kernels  16 us (6%)
  local copies, waits for them, and re-layouts  11.6 us (5%)
  other arithmetic  6.48 us (3%)
  matrix products  3.66 us (1%)
    ppermute x4, waiting for transfers between devices, local(): lax.ppermute(every, 'users', pairs)  55.4 us
    all_to_all x1, starting transfers between devices, exchanged(): return lax.all_to_all(x, 'users', split_axis=0, concat_axis=0, tiled=True)  44.9 us
    all_to_all x1, blocking collectives, exchanged(): return lax.all_to_all(x, 'users', split_axis=0, concat_axis=0, tiled=True)  21.9 us
    ppermute x5, starting transfers between devices, swapped(): return lax.ppermute(x, 'heads', [(k, cores - 1 - k) for k in range(cores)])  20.7 us
    ppermute x4, starting transfers between devices, local(): lax.ppermute(every, 'users', pairs)  18.3 us
    pallas_call x1, Pallas kernels, score_units(): pl.pallas_call(score_kernel, out_shape=jax.ShapeDtypeStruct((rows // lane...  16 us
    ppermute x3, waiting for transfers between devices, local(): from_below = lax.ppermute(from_below, 'routers', up)  14.2 us
    ppermute x3, starting transfers between devices, local(): from_above = lax.ppermute(from_above, 'routers', down)  13.8 us
  transfers between devices with their start and end apart: 18, of which 9 were waited for; matrix products, arithmetic and copies ran while one was open for 5% of the time, Pallas kernels for 0%

profile of v4, /device:TPU:65, one launch (start us, length us, event | category | flops | bytes accessed | tf_op | source)
XLA Modules:
  0.0 248.5 jit_solution(13372076110311632291)
XLA Ops:
  0.0 0.8 multiply_bitcast_fusion
  0.8 0.7 iota_compare_fusion.8
  1.5 0.9 select_reduce_fusion.4
  2.9 3.7 %fusion.2 = bf16[1024,1024]{1,0:T(8,128)(2,1)} fusion(bf16[1024,1024]{1,0:T(8,128)(2,1)S(1)} %bitcast.31, s32[1024]{0:T(1024)S(1)} %fusion.17), kind=kOutput, calls=%fused_computation.3 | convolution fusion | flops 2149580800 | bytes 4198400 | tf_op jit(solution)/shard_map/dot_general | solution.py:327
  6.6 4.1 %collective-permute-start.10 = (bf16[4,128,640]{2,1,0:T(8,128)(2,1)S(1)}, bf16[4,128,640]{2,1,0:T(8,128)(2,1)S(1)}, u32[]{:S(2)}, u32[]{:S(2)}) collective-permute-start(bf16[4,128,640]{2,1,0:T(8,128)(2,1)S(1)} %pad_maximum_fusion), channel_id=1, source_target_pairs={{0,2},{2,4},{4,6},{6,8},{8,10},{10,12},{12,14},{14,0},{1,3},{3,5},... | collective-permute-start | bytes 1966088 | tf_op jit(solution)/shard_map/ppermute | solution.py:353
  10.7 4.1 %collective-permute-start.7 = (bf16[4,128,640]{2,1,0:T(8,128)(2,1)S(1)}, bf16[4,128,640]{2,1,0:T(8,128)(2,1)}, u32[]{:S(2)}, u32[]{:S(2)}) collective-permute-start(bf16[4,128,640]{2,1,0:T(8,128)(2,1)S(1)} %pad_maximum_fusion), channel_id=1, source_target_pairs={{0,14},{2,0},{4,2},{6,4},{8,6},{10,8},{12,10},{14,12},{1,15},{3,1}... | collective-permute-start | bytes 1966088 | tf_op jit(solution)/shard_map/ppermute | solution.py:354
  14.9 6.0 %collective-permute-done.10 = bf16[4,128,640]{2,1,0:T(8,128)(2,1)S(1)} collective-permute-done((bf16[4,128,640]{2,1,0:T(8,128)(2,1)S(1)}, bf16[4,128,640]{2,1,0:T(8,128)(2,1)S(1)}, u32[]{:S(2)}, u32[]{:S(2)}) %collective-permute-start.10) | collective-permute-done | bytes 655392 | tf_op jit(solution)/shard_map/ppermute | solution.py:353
  20.9 6.6 %collective-permute-start.11 = (bf16[4,128,640]{2,1,0:T(8,128)(2,1)S(1)}, bf16[4,128,640]{2,1,0:T(8,128)(2,1)}, u32[]{:S(2)}, u32[]{:S(2)}) collective-permute-start(bf16[4,128,640]{2,1,0:T(8,128)(2,1)S(1)} %collective-permute-done.10), channel_id=1, source_target_pairs={{0,2},{2,4},{4,6},{6,8},{8,10},{10,12},{12,14},{14,0},{1,3},{3,5},... | collective-permute-start | bytes 1966088 | tf_op jit(solution)/shard_map/ppermute | solution.py:353
  27.5 5.0 %collective-permute-start.8 = (bf16[4,128,640]{2,1,0:T(8,128)(2,1)}, bf16[4,128,640]{2,1,0:T(8,128)(2,1)}, u32[]{:S(2)}, u32[]{:S(2)}) collective-permute-start(bf16[4,128,640]{2,1,0:T(8,128)(2,1)} %collective-permute-done.7), channel_id=1, source_target_pairs={{0,14},{2,0},{4,2},{6,4},{8,6},{10,8},{12,10},{14,12},{1,15},{3,1}... | collective-permute-start | bytes 1966088 | tf_op jit(solution)/shard_map/ppermute | solution.py:354
  32.5 44.9 %all-to-all-start = ((bf16[16,64,1024]{2,1,0:T(8,128)(2,1)}), bf16[16,64,1024]{2,1,0:T(8,128)(2,1)}, u32[]{:S(2)}, u32[]{:S(2)}) async-start(bf16[16,64,1024]{2,1,0:T(8,128)(2,1)} %bitcast.34), calls=%async_computation | async-start | bytes 4194304 | tf_op jit(solution)/shard_map/all_to_all | solution.py:310
  77.4 2.0 collective-permute-start.12
  79.4 4.6 %collective-permute-start.9 = (bf16[4,128,640]{2,1,0:T(8,128)(2,1)}, bf16[4,128,640]{2,1,0:T(8,128)(2,1)S(1)}, u32[]{:S(2)}, u32[]{:S(2)}) collective-permute-start(bf16[4,128,640]{2,1,0:T(8,128)(2,1)} %collective-permute-done.8), channel_id=1, source_target_pairs={{0,14},{2,0},{4,2},{6,4},{8,6},{10,8},{12,10},{14,12},{1,15},{3,1}... | collective-permute-start | bytes 1966088 | tf_op jit(solution)/shard_map/ppermute | solution.py:354
  84.0 0.9 bitcast_dynamic-update-slice_fusion.6
  84.9 2.0 bitcast_dynamic-update-slice_fusion.5
  87.0 8.2 %collective-permute-done.12 = bf16[4,128,640]{2,1,0:T(8,128)(2,1)S(1)} collective-permute-done((bf16[4,128,640]{2,1,0:T(8,128)(2,1)}, bf16[4,128,640]{2,1,0:T(8,128)(2,1)S(1)}, u32[]{:S(2)}, u32[]{:S(2)}) %collective-permute-start.12) | collective-permute-done | bytes 655392 | tf_op jit(solution)/shard_map/ppermute | solution.py:353
  95.2 2.0 collective-permute-start.13
  97.2 4.6 %collective-permute-start.14 = (bf16[2,128,640]{2,1,0:T(8,128)(2,1)S(1)}, bf16[2,128,640]{2,1,0:T(8,128)(2,1)S(1)}, u32[]{:S(2)}, u32[]{:S(2)}) collective-permute-start(bf16[2,128,640]{2,1,0:T(8,128)(2,1)S(1)} %slice.9), channel_id=1, source_target_pairs={{0,14},{2,0},{4,2},{6,4},{8,6},{10,8},{12,10},{14,12},{1,15},{3,1}... | collective-permute-start | bytes 983048 | tf_op jit(solution)/shard_map/ppermute | solution.py:361
  101.8 2.0 bitcast_dynamic-update-slice_fusion.4
  103.8 0.9 bitcast_dynamic-update-slice_fusion.3
  104.7 0.2 collective-permute-done.13
  104.9 0.9 collective-permute-done.14
  105.8 1.0 fusion.3
  106.8 1.0 bitcast_dynamic-update-slice_fusion.2
  107.8 2.0 bitcast_dynamic-update-slice_fusion.1
  109.8 0.9 bitcast_dynamic-update-slice_fusion.w_own
  110.7 5.8 %collective-permute-start.15 = (bf16[8,4,128,640]{3,2,1,0:T(8,128)(2,1)}, bf16[8,4,128,640]{3,2,1,0:T(8,128)(2,1)}, u32[]{:S(2)}, u32[]{:S(2)}) collective-permute-start(bf16[8,4,128,640]{3,2,1,0:T(8,128)(2,1)} %bitcast_dynamic-update-slice_fusion.w_own), channel_id=1, source_target_pairs={{0,1},{1,0},{2,3},{3,2},{4,5},{5,4},{6,7},{7,6},{8,9},{9,8},{10,11... | collective-permute-start | bytes 15728648 | tf_op jit(solution)/shard_map/ppermute | solution.py:307
  116.5 0.1 select_reduce_fusion.3
  116.7 3.1 %collective-permute-start = (s32[1,16]{1,0:T(1,128)S(1)}, s32[1,16]{1,0:T(1,128)S(1)}, u32[]{:S(2)}, u32[]{:S(2)}) collective-permute-start(s32[1,16]{1,0:T(1,128)S(1)} %bitcast.40), channel_id=1, source_target_pairs={{0,16},{16,32},{32,48},{48,64},{64,80},{80,96},{96,112},{112,128},... | collective-permute-start | bytes 200 | tf_op jit(solution)/shard_map/ppermute | solution.py:339
  119.8 1.2 copy.16
  121.0 2.2 collective-permute-start.5
  123.3 2.2 collective-permute-start.4
  125.4 2.2 collective-permute-start.6
  127.7 43.0 %collective-permute-done = s32[1,16]{1,0:T(1,128)S(1)} collective-permute-done((s32[1,16]{1,0:T(1,128)S(1)}, s32[1,16]{1,0:T(1,128)S(1)}, u32[]{:S(2)}, u32[]{:S(2)}) %collective-permute-start) | collective-permute-done | bytes 96 | tf_op jit(solution)/shard_map/ppermute | solution.py:339
  170.7 1.9 collective-permute-start.1
  172.7 4.5 %collective-permute-done.1 = s32[2,16]{1,0:T(2,128)S(1)} collective-permute-done((s32[2,16]{1,0:T(2,128)S(1)}, s32[2,16]{1,0:T(2,128)S(1)}, u32[]{:S(2)}, u32[]{:S(2)}) %collective-permute-start.1) | collective-permute-done | bytes 160 | tf_op jit(solution)/shard_map/ppermute | solution.py:339
  177.2 4.3 %collective-permute-start.2 = (s32[4,16]{1,0:T(4,128)S(1)}, s32[4,16]{1,0:T(4,128)S(1)}, u32[]{:S(2)}, u32[]{:S(2)}) collective-permute-start(s32[4,16]{1,0:T(4,128)S(1)} %pad_add_fusion.1), channel_id=1, source_target_pairs={{0,64},{16,80},{32,96},{48,112},{64,128},{80,144},{96,160},{112,17... | collective-permute-start | bytes 776 | tf_op jit(solution)/shard_map/ppermute | solution.py:339
  181.5 4.0 %collective-permute-done.2 = s32[4,16]{1,0:T(4,128)S(1)} collective-permute-done((s32[4,16]{1,0:T(4,128)S(1)}, s32[4,16]{1,0:T(4,128)S(1)}, u32[]{:S(2)}, u32[]{:S(2)}) %collective-permute-start.2) | collective-permute-done | bytes 288 | tf_op jit(solution)/shard_map/ppermute | solution.py:339
  185.4 9.0 %collective-permute-start.3 = (s32[8,16]{1,0:T(8,128)S(1)}, s32[8,16]{1,0:T(8,128)S(1)}, u32[]{:S(2)}, u32[]{:S(2)}) collective-permute-start(s32[8,16]{1,0:T(8,128)S(1)} %pad_add_fusion), channel_id=1, source_target_pairs={{0,128},{16,144},{32,160},{48,176},{64,192},{80,208},{96,224},{112... | collective-permute-start | bytes 1544 | tf_op jit(solution)/shard_map/ppermute | solution.py:339
  194.6 4.0 %collective-permute-done.3 = s32[8,16]{1,0:T(8,128)S(1)} collective-permute-done((s32[8,16]{1,0:T(8,128)S(1)}, s32[8,16]{1,0:T(8,128)S(1)}, u32[]{:S(2)}, u32[]{:S(2)}) %collective-permute-start.3) | collective-permute-done | bytes 544 | tf_op jit(solution)/shard_map/ppermute | solution.py:339
  198.6 0.5 select_reduce_fusion.2.code_ref
  199.1 1.0 copy-done.2
  200.1 16.0 %score_units.1 = f32[8,128]{1,0:T(8,128)S(1)} custom-call(s32[16]{0:T(128)S(1)} %select_reduce_fusion.2.code_ref, s32[2]{0:T(128)S(1)} %pad_add_fusion.3.core_ref, bf16[1,512]{1,0:T(2,128)(2,1)S(1)} %broadcast_in_dim.116.gain_own, bf16[1,512]{1,0:T(2,128)(2,1)S(1)} %collective-permute-done.4.gain_other, bf16[1,1024]{1,0:T(2,128)(2,1)S(1)} %broadcast_in_dim.117.mlp_gain_ref, ...), custom_call_target="tpu_custom_call" | custom-call | tf_op jit(solution)/shard_map/score_units/pallas_call | solution.py:254
  216.2 21.9 %all_to_all.17 = f32[16,1,64]{2,1,0:T(1,128)S(1)} all-to-all(f32[16,1,64]{2,1,0:T(1,128)S(1)} %bitcast.39), channel_id=1, replica_groups=mesh['groups'=2,'users'=16,'routers'=8,'heads'=2] {'users'}, dimensions={0} | all-to-all | bytes 8192 | tf_op jit(solution)/shard_map/all_to_all | solution.py:310
  238.1 8.3 %collective-permute-start.16 = (f32[16,64]{1,0:T(8,128)S(1)}, f32[16,64]{1,0:T(8,128)S(1)}, u32[]{:S(2)}, u32[]{:S(2)}) collective-permute-start(f32[16,64]{1,0:T(8,128)S(1)} %bitcast.37), channel_id=1, source_target_pairs={{0,1},{1,0},{2,3},{3,2},{4,5},{5,4},{6,7},{7,6},{8,9},{9,8},{10,11... | collective-permute-start | bytes 12296 | tf_op jit(solution)/shard_map/ppermute | solution.py:307
  246.4 0.8 collective-permute-done.16
  247.3 0.1 select_reduce_fusion.1
  247.4 0.4 select_reduce_fusion
  247.8 0.7 broadcast_select_fusion
  (53 shorter events, 0.9 us)
Async XLA Ops:
  0.0 2.9 %copy-start = (bf16[16,64,1024]{2,1,0:T(8,128)(2,1)S(1)}, bf16[16,64,1024]{2,1,0:T(8,128)(2,1)}, u32[]{:S(2)}) copy-start(bf16[16,64,1024]{2,1,0:T(8,128)(2,1)} %param.12) | copy-start | bytes 6291460
  2.9 3.7 %copy-start.3 = (bf16[4,128,512]{2,1,0:T(8,128)(2,1)S(1)}, bf16[4,128,512]{2,1,0:T(8,128)(2,1)}, u32[]{:S(2)}) copy-start(bf16[4,128,512]{2,1,0:T(8,128)(2,1)} %param.18) | copy-start | bytes 1572868
  2.9 3.7 %copy-start.4 = (bf16[512,128]{1,0:T(8,128)(2,1)S(1)}, bf16[512,128]{1,0:T(8,128)(2,1)}, u32[]{:S(2)}) copy-start(bf16[512,128]{1,0:T(8,128)(2,1)} %param.20) | copy-start | bytes 393220
  6.6 14.3 %collective-permute-start.10 = (bf16[4,128,640]{2,1,0:T(8,128)(2,1)S(1)}, bf16[4,128,640]{2,1,0:T(8,128)(2,1)S(1)}, u32[]{:S(2)}, u32[]{:S(2)}) collective-permute-start(bf16[4,128,640]{2,1,0:T(8,128)(2,1)S(1)} %pad_maximum_fusion), channel_id=1, source_target_pairs={{0,2},{2,4},{4,6},{6,8},{8,10},{10,12},{12,14},{14,0},{1,3},{3,5},... | collective-permute-start | bytes 1966088 | tf_op jit(solution)/shard_map/ppermute | solution.py:353
  10.7 16.7 %collective-permute-start.7 = (bf16[4,128,640]{2,1,0:T(8,128)(2,1)S(1)}, bf16[4,128,640]{2,1,0:T(8,128)(2,1)}, u32[]{:S(2)}, u32[]{:S(2)}) collective-permute-start(bf16[4,128,640]{2,1,0:T(8,128)(2,1)S(1)} %pad_maximum_fusion), channel_id=1, source_target_pairs={{0,14},{2,0},{4,2},{6,4},{8,6},{10,8},{12,10},{14,12},{1,15},{3,1}... | collective-permute-start | bytes 1966088 | tf_op jit(solution)/shard_map/ppermute | solution.py:354
  20.9 56.5 %collective-permute-start.11 = (bf16[4,128,640]{2,1,0:T(8,128)(2,1)S(1)}, bf16[4,128,640]{2,1,0:T(8,128)(2,1)}, u32[]{:S(2)}, u32[]{:S(2)}) collective-permute-start(bf16[4,128,640]{2,1,0:T(8,128)(2,1)S(1)} %collective-permute-done.10), channel_id=1, source_target_pairs={{0,2},{2,4},{4,6},{6,8},{8,10},{10,12},{12,14},{14,0},{1,3},{3,5},... | collective-permute-start | bytes 1966088 | tf_op jit(solution)/shard_map/ppermute | solution.py:353
  27.5 51.9 %collective-permute-start.8 = (bf16[4,128,640]{2,1,0:T(8,128)(2,1)}, bf16[4,128,640]{2,1,0:T(8,128)(2,1)}, u32[]{:S(2)}, u32[]{:S(2)}) collective-permute-start(bf16[4,128,640]{2,1,0:T(8,128)(2,1)} %collective-permute-done.7), channel_id=1, source_target_pairs={{0,14},{2,0},{4,2},{6,4},{8,6},{10,8},{12,10},{14,12},{1,15},{3,1}... | collective-permute-start | bytes 1966088 | tf_op jit(solution)/shard_map/ppermute | solution.py:354
  32.5 166.6 %all-to-all-start = ((bf16[16,64,1024]{2,1,0:T(8,128)(2,1)}), bf16[16,64,1024]{2,1,0:T(8,128)(2,1)}, u32[]{:S(2)}, u32[]{:S(2)}) async-start(bf16[16,64,1024]{2,1,0:T(8,128)(2,1)} %bitcast.34), calls=%async_computation | async-start | bytes 4194304 | tf_op jit(solution)/shard_map/all_to_all | solution.py:310
  77.4 17.7 %collective-permute-start.12 = (bf16[4,128,640]{2,1,0:T(8,128)(2,1)}, bf16[4,128,640]{2,1,0:T(8,128)(2,1)S(1)}, u32[]{:S(2)}, u32[]{:S(2)}) collective-permute-start(bf16[4,128,640]{2,1,0:T(8,128)(2,1)} %collective-permute-done.11), channel_id=1, source_target_pairs={{0,2},{2,4},{4,6},{6,8},{8,10},{10,12},{12,14},{14,0},{1,3},{3,5},... | collective-permute-start | bytes 1966088 | tf_op jit(solution)/shard_map/ppermute | solution.py:353
  79.4 17.7 %collective-permute-start.9 = (bf16[4,128,640]{2,1,0:T(8,128)(2,1)}, bf16[4,128,640]{2,1,0:T(8,128)(2,1)S(1)}, u32[]{:S(2)}, u32[]{:S(2)}) collective-permute-start(bf16[4,128,640]{2,1,0:T(8,128)(2,1)} %collective-permute-done.8), channel_id=1, source_target_pairs={{0,14},{2,0},{4,2},{6,4},{8,6},{10,8},{12,10},{14,12},{1,15},{3,1}... | collective-permute-start | bytes 1966088 | tf_op jit(solution)/shard_map/ppermute | solution.py:354
  84.9 31.6 %copy-start.6 = (s32[16]{0:T(128)S(1)}, s32[16]{0:T(128)}, u32[]{:S(2)}) copy-start(s32[16]{0:T(128)} %param.15) | copy-start | bytes 196
  84.9 31.6 %copy-start.8 = (s32[16]{0:T(128)S(1)}, s32[16]{0:T(128)}, u32[]{:S(2)}) copy-start(s32[16]{0:T(128)} %param.14) | copy-start | bytes 196
  84.9 31.6 %copy-start.5 = (s32[16,1]{0,1:T(1,128)S(1)}, s32[16,1]{0,1:T(1,128)}, u32[]{:S(2)}) copy-start(s32[16,1]{0,1:T(1,128)} %param.13) | copy-start | bytes 196
  87.0 36.3 %copy-start.9 = (bf16[512]{0:T(512)(128)(2,1)S(1)}, bf16[512]{0:T(512)(128)(2,1)}, u32[]{:S(2)}) copy-start(bf16[512]{0:T(512)(128)(2,1)} %param.19) | copy-start | bytes 3076
  87.0 38.5 %copy-start.1 = (bf16[2,256,512]{2,1,0:T(8,128)(2,1)S(1)}, bf16[2,256,512]{2,1,0:T(8,128)(2,1)}, u32[]{:S(2)}) copy-start(bf16[2,256,512]{2,1,0:T(8,128)(2,1)} %v_own.1) | copy-start | bytes 1572868
  87.0 107.6 %copy-start.7 = (bf16[1024]{0:T(1024)(128)(2,1)S(1)}, bf16[1024]{0:T(1024)(128)(2,1)}, u32[]{:S(2)}) copy-start(bf16[1024]{0:T(1024)(128)(2,1)} %param.21) | copy-start | bytes 6148
  87.0 107.6 %copy-start.10 = (bf16[256]{0:T(256)(128)(2,1)S(1)}, bf16[256]{0:T(256)(128)(2,1)}, u32[]{:S(2)}) copy-start(bf16[256]{0:T(256)(128)(2,1)} %param.23) | copy-start | bytes 1540
  95.2 9.7 %collective-permute-start.13 = (bf16[2,128,640]{2,1,0:T(8,128)(2,1)S(1)}, bf16[2,128,640]{2,1,0:T(8,128)(2,1)S(1)}, u32[]{:S(2)}, u32[]{:S(2)}) collective-permute-start(bf16[2,128,640]{2,1,0:T(8,128)(2,1)S(1)} %slice.8), channel_id=1, source_target_pairs={{0,2},{2,4},{4,6},{6,8},{8,10},{10,12},{12,14},{14,0},{1,3},{3,5},... | collective-permute-start | bytes 983048 | tf_op jit(solution)/shard_map/ppermute | solution.py:360
  97.2 8.6 %collective-permute-start.14 = (bf16[2,128,640]{2,1,0:T(8,128)(2,1)S(1)}, bf16[2,128,640]{2,1,0:T(8,128)(2,1)S(1)}, u32[]{:S(2)}, u32[]{:S(2)}) collective-permute-start(bf16[2,128,640]{2,1,0:T(8,128)(2,1)S(1)} %slice.9), channel_id=1, source_target_pairs={{0,14},{2,0},{4,2},{6,4},{8,6},{10,8},{12,10},{14,12},{1,15},{3,1}... | collective-permute-start | bytes 983048 | tf_op jit(solution)/shard_map/ppermute | solution.py:361
  110.7 88.4 %collective-permute-start.15 = (bf16[8,4,128,640]{3,2,1,0:T(8,128)(2,1)}, bf16[8,4,128,640]{3,2,1,0:T(8,128)(2,1)}, u32[]{:S(2)}, u32[]{:S(2)}) collective-permute-start(bf16[8,4,128,640]{3,2,1,0:T(8,128)(2,1)} %bitcast_dynamic-update-slice_fusion.w_own), channel_id=1, source_target_pairs={{0,1},{1,0},{2,3},{3,2},{4,5},{5,4},{6,7},{7,6},{8,9},{9,8},{10,11... | collective-permute-start | bytes 15728648 | tf_op jit(solution)/shard_map/ppermute | solution.py:307
  116.7 54.0 %collective-permute-start = (s32[1,16]{1,0:T(1,128)S(1)}, s32[1,16]{1,0:T(1,128)S(1)}, u32[]{:S(2)}, u32[]{:S(2)}) collective-permute-start(s32[1,16]{1,0:T(1,128)S(1)} %bitcast.40), channel_id=1, source_target_pairs={{0,16},{16,32},{32,48},{48,64},{64,80},{80,96},{96,112},{112,128},... | collective-permute-start | bytes 200 | tf_op jit(solution)/shard_map/ppermute | solution.py:339
  121.0 78.0 %collective-permute-start.5 = (bf16[2,512,256]{2,1,0:T(8,128)(2,1)S(1)}, bf16[2,512,256]{2,1,0:T(8,128)(2,1)}, u32[]{:S(2)}, u32[]{:S(2)}) collective-permute-start(bf16[2,512,256]{2,1,0:T(8,128)(2,1)S(1)} %bitcast.32), channel_id=1, source_target_pairs={{0,1},{1,0},{2,3},{3,2},{4,5},{5,4},{6,7},{7,6},{8,9},{9,8},{10,11... | collective-permute-start | bytes 1572872 | tf_op jit(solution)/shard_map/ppermute | solution.py:307
  123.3 75.8 %collective-permute-start.4 = (bf16[1,512]{1,0:T(2,128)(2,1)S(1)}, bf16[1,512]{1,0:T(2,128)(2,1)S(1)}, u32[]{:S(2)}, u32[]{:S(2)}) collective-permute-start(bf16[1,512]{1,0:T(2,128)(2,1)S(1)} %broadcast_in_dim.116.gain_own), channel_id=1, source_target_pairs={{0,1},{1,0},{2,3},{3,2},{4,5},{5,4},{6,7},{7,6},{8,9},{9,8},{10,11... | collective-permute-start | bytes 3080 | tf_op jit(solution)/shard_map/ppermute | solution.py:307
  125.4 73.6 %collective-permute-start.6 = (bf16[2,256,512]{2,1,0:T(8,128)(2,1)S(1)}, bf16[2,256,512]{2,1,0:T(8,128)(2,1)}, u32[]{:S(2)}, u32[]{:S(2)}) collective-permute-start(bf16[2,256,512]{2,1,0:T(8,128)(2,1)S(1)} %copy-done.1), channel_id=1, source_target_pairs={{0,1},{1,0},{2,3},{3,2},{4,5},{5,4},{6,7},{7,6},{8,9},{9,8},{10,11... | collective-permute-start | bytes 1572872 | tf_op jit(solution)/shard_map/ppermute | solution.py:307
  170.7 6.5 %collective-permute-start.1 = (s32[2,16]{1,0:T(2,128)S(1)}, s32[2,16]{1,0:T(2,128)S(1)}, u32[]{:S(2)}, u32[]{:S(2)}) collective-permute-start(s32[2,16]{1,0:T(2,128)S(1)} %pad_add_fusion.2), channel_id=1, source_target_pairs={{0,32},{16,48},{32,64},{48,80},{64,96},{80,112},{96,128},{112,144}... | collective-permute-start | bytes 392 | tf_op jit(solution)/shard_map/ppermute | solution.py:339
  177.2 8.3 %collective-permute-start.2 = (s32[4,16]{1,0:T(4,128)S(1)}, s32[4,16]{1,0:T(4,128)S(1)}, u32[]{:S(2)}, u32[]{:S(2)}) collective-permute-start(s32[4,16]{1,0:T(4,128)S(1)} %pad_add_fusion.1), channel_id=1, source_target_pairs={{0,64},{16,80},{32,96},{48,112},{64,128},{80,144},{96,160},{112,17... | collective-permute-start | bytes 776 | tf_op jit(solution)/shard_map/ppermute | solution.py:339
  185.4 13.1 %collective-permute-start.3 = (s32[8,16]{1,0:T(8,128)S(1)}, s32[8,16]{1,0:T(8,128)S(1)}, u32[]{:S(2)}, u32[]{:S(2)}) collective-permute-start(s32[8,16]{1,0:T(8,128)S(1)} %pad_add_fusion), channel_id=1, source_target_pairs={{0,128},{16,144},{32,160},{48,176},{64,192},{80,208},{96,224},{112... | collective-permute-start | bytes 1544 | tf_op jit(solution)/shard_map/ppermute | solution.py:339
  199.1 1.0 copy-start.2
  238.1 9.1 %collective-permute-start.16 = (f32[16,64]{1,0:T(8,128)S(1)}, f32[16,64]{1,0:T(8,128)S(1)}, u32[]{:S(2)}, u32[]{:S(2)}) collective-permute-start(f32[16,64]{1,0:T(8,128)S(1)} %bitcast.37), channel_id=1, source_target_pairs={{0,1},{1,0},{2,3},{3,2},{4,5},{5,4},{6,7},{7,6},{8,9},{9,8},{10,11... | collective-permute-start | bytes 12296 | tf_op jit(solution)/shard_map/ppermute | solution.py:307

commit v5 on v4

--- a/solution.py
+++ b/solution.py
@@ -333,15 +333,13 @@
     goes = target[None, :] == lax.broadcasted_iota(jnp.int32, (peers, blocks), 0)
     weight = jnp.where(block_user == 0, CODE + 1, 1) * block_fill
     every = jnp.sum(jnp.where(goes, weight[None, :], 0), axis=1)[None, :]
-    while every.shape[0] < peers:
-        step = every.shape[0]
+
+    def doubled(rows):
+        step = rows.shape[0]
+        if step >= peers:
+            return rows
         pairs = [(k, (k + step) % peers) for k in range(peers)]
-        every = jnp.concatenate([every, lax.ppermute(every, "users", pairs)], axis=0)
-    source = (me + peers - lax.broadcasted_iota(jnp.int32, (peers, peers, peers), 1)) % peers
-    wanted = (source == lax.broadcasted_iota(jnp.int32, (peers, peers, peers), 0)) & (
-        lax.broadcasted_iota(jnp.int32, (peers, peers, peers), 2) == me
-    )
-    codes = jnp.sum(jnp.where(wanted, every[None], 0), axis=(1, 2))
+        return jnp.concatenate([rows, lax.ppermute(rows, "users", pairs)], axis=0)
 
     matrices, share, _ = w_in.shape
     w_local = jnp.concatenate([w_in, w_o.reshape(matrices, share, share)], axis=2)
@@ -352,16 +350,22 @@
     for step in range(1, routers // 2):
         from_below = lax.ppermute(from_below, "routers", up)
         from_above = lax.ppermute(from_above, "routers", down)
+        every = doubled(every)
+        from_below, from_above, every = lax.optimization_barrier((from_below, from_above, every))
         ring[routers - step] = from_below
         ring[step] = from_above
     half = matrices // 2
-    ring[routers // 2] = jnp.concatenate(
-        [
-            lax.ppermute(from_below[:half], "routers", up),
-            lax.ppermute(from_above[half:], "routers", down),
-        ],
-        axis=0,
+    lower = lax.ppermute(from_below[:half], "routers", up)
+    upper = lax.ppermute(from_above[half:], "routers", down)
+    ring[routers // 2] = jnp.concatenate([lower, upper], axis=0)
+    every = doubled(every)
+    while every.shape[0] < peers:
+        every = doubled(every)
+    source = (me + peers - lax.broadcasted_iota(jnp.int32, (peers, peers, peers), 1)) % peers
+    wanted = (source == lax.broadcasted_iota(jnp.int32, (peers, peers, peers), 0)) & (
+        lax.broadcasted_iota(jnp.int32, (peers, peers, peers), 2) == me
     )
+    codes = jnp.sum(jnp.where(wanted, every[None], 0), axis=(1, 2))
     w_ring = jnp.stack([ring[k] for k in range(routers)])
     own = (jnp.swapaxes(prefix_keys, 1, 2), prefix_values, attn_gain[None, :], w_ring)
     other = jax.tree.map(swapped, own)

time: 249 us -> 285 us (1.14)
  the two profiles are of different devices: /device:TPU:65 before, /device:TPU:78 now
where the time goes in v5:
time: 285 us; the launch traced here: 282 us
  starting transfers between devices  111 us (39%)
  waiting for transfers between devices  105 us (37%)
  blocking collectives  33.5 us (12%)
  local copies, waits for them, and re-layouts  11.5 us (4%)
  Pallas kernels  10.9 us (4%)
  other arithmetic  6.48 us (2%)
  matrix products  3.66 us (1%)
    ppermute x4, waiting for transfers between devices, doubled(): return jnp.concatenate([rows, lax.ppermute(rows, 'users', pairs)], axis=0)  94.5 us
    ppermute x3, starting transfers between devices, local(): from_below = lax.ppermute(from_below, 'routers', up)  46.8 us
    all_to_all x1, blocking collectives, exchanged(): return lax.all_to_all(x, 'users', split_axis=0, concat_axis=0, tiled=True)  33.5 us
    ppermute x4, starting transfers between devices, doubled(): return jnp.concatenate([rows, lax.ppermute(rows, 'users', pairs)], axis=0)  28.2 us
    pallas_call x1, Pallas kernels, score_units(): pl.pallas_call(score_kernel, out_shape=jax.ShapeDtypeStruct((rows // lane...  10.9 us
    ppermute x5, starting transfers between devices, swapped(): return lax.ppermute(x, 'heads', [(k, cores - 1 - k) for k in range(cores)])  10.7 us
    all_to_all x1, starting transfers between devices, exchanged(): return lax.all_to_all(x, 'users', split_axis=0, concat_axis=0, tiled=True)  10.2 us
    unnamed x28, local copies, waits for them, and re-layouts  10.2 us
  transfers between devices with their start and end apart: 18, of which 8 were waited for; matrix products, arithmetic and copies ran while one was open for 5% of the time, Pallas kernels for 0%

profile of v5, /device:TPU:78, one launch (start us, length us, event | category | flops | bytes accessed | tf_op | source)
XLA Modules:
  0.0 282.0 jit_solution(7795588707699670494)
XLA Ops:
  0.0 0.8 multiply_bitcast_fusion
  0.8 0.7 iota_compare_fusion.8
  1.5 0.9 select_reduce_fusion.4
  2.5 0.1 fusion.6
  2.9 3.7 %fusion.2 = bf16[1024,1024]{1,0:T(8,128)(2,1)} fusion(bf16[1024,1024]{1,0:T(8,128)(2,1)S(1)} %bitcast.31, s32[1024]{0:T(1024)S(1)} %fusion.17), kind=kOutput, calls=%fused_computation.3 | convolution fusion | flops 2149580800 | bytes 4198400 | tf_op jit(solution)/shard_map/dot_general | solution.py:327
  6.7 41.4 %collective-permute-start = (bf16[4,128,640]{2,1,0:T(8,128)(2,1)S(1)}, bf16[4,128,640]{2,1,0:T(8,128)(2,1)S(1)}, u32[]{:S(2)}, u32[]{:S(2)}) collective-permute-start(bf16[4,128,640]{2,1,0:T(8,128)(2,1)S(1)} %pad_maximum_fusion), channel_id=1, source_target_pairs={{0,2},{2,4},{4,6},{6,8},{8,10},{10,12},{12,14},{14,0},{1,3},{3,5},... | collective-permute-start | bytes 1966088 | tf_op jit(solution)/shard_map/ppermute | solution.py:351
  48.0 2.0 collective-permute-start.1
  50.0 0.1 select_reduce_fusion.3
  50.1 1.9 collective-permute-start.2
  52.1 6.2 %collective-permute-done.2 = s32[1,16]{1,0:T(1,128)S(1)} collective-permute-done((s32[1,16]{1,0:T(1,128)S(1)}, s32[1,16]{1,0:T(1,128)S(1)}, u32[]{:S(2)}, u32[]{:S(2)}) %collective-permute-start.2) | collective-permute-done | bytes 96 | tf_op jit(solution)/shard_map/ppermute | solution.py:342
  58.3 3.5 %collective-permute-done.1 = bf16[4,128,640]{2,1,0:T(8,128)(2,1)} collective-permute-done((bf16[4,128,640]{2,1,0:T(8,128)(2,1)S(1)}, bf16[4,128,640]{2,1,0:T(8,128)(2,1)}, u32[]{:S(2)}, u32[]{:S(2)}) %collective-permute-start.1) | collective-permute-done | bytes 655392 | tf_op jit(solution)/shard_map/ppermute | solution.py:352
  61.9 1.9 collective-permute-start.3
  63.8 4.0 %collective-permute-start.4 = (bf16[4,128,640]{2,1,0:T(8,128)(2,1)}, bf16[4,128,640]{2,1,0:T(8,128)(2,1)}, u32[]{:S(2)}, u32[]{:S(2)}) collective-permute-start(bf16[4,128,640]{2,1,0:T(8,128)(2,1)} %collective-permute-done.1), channel_id=1, source_target_pairs={{0,14},{2,0},{4,2},{6,4},{8,6},{10,8},{12,10},{14,12},{1,15},{3,1}... | collective-permute-start | bytes 1966088 | tf_op jit(solution)/shard_map/ppermute | solution.py:352
  67.8 10.2 %all-to-all-start = ((bf16[16,64,1024]{2,1,0:T(8,128)(2,1)}), bf16[16,64,1024]{2,1,0:T(8,128)(2,1)}, u32[]{:S(2)}, u32[]{:S(2)}) async-start(bf16[16,64,1024]{2,1,0:T(8,128)(2,1)} %bitcast.34), calls=%async_computation | async-start | bytes 4194304 | tf_op jit(solution)/shard_map/all_to_all | solution.py:310
  78.0 4.5 %collective-permute-start.5 = (s32[2,16]{1,0:T(2,128)S(1)}, s32[2,16]{1,0:T(2,128)S(1)}, u32[]{:S(2)}, u32[]{:S(2)}) collective-permute-start(s32[2,16]{1,0:T(2,128)S(1)} %pad_add_fusion.3), channel_id=1, source_target_pairs={{0,32},{16,48},{32,64},{48,80},{64,96},{80,112},{96,128},{112,144}... | collective-permute-start | bytes 392 | tf_op jit(solution)/shard_map/ppermute | solution.py:342
  82.6 83.6 %collective-permute-done.5 = s32[2,16]{1,0:T(2,128)S(1)} collective-permute-done((s32[2,16]{1,0:T(2,128)S(1)}, s32[2,16]{1,0:T(2,128)S(1)}, u32[]{:S(2)}, u32[]{:S(2)}) %collective-permute-start.5) | collective-permute-done | bytes 160 | tf_op jit(solution)/shard_map/ppermute | solution.py:342
  166.2 3.5 %collective-permute-start.6 = (bf16[4,128,640]{2,1,0:T(8,128)(2,1)}, bf16[4,128,640]{2,1,0:T(8,128)(2,1)S(1)}, u32[]{:S(2)}, u32[]{:S(2)}) collective-permute-start(bf16[4,128,640]{2,1,0:T(8,128)(2,1)} %collective-permute-done.3), channel_id=1, source_target_pairs={{0,2},{2,4},{4,6},{6,8},{8,10},{10,12},{12,14},{14,0},{1,3},{3,5},... | collective-permute-start | bytes 1966088 | tf_op jit(solution)/shard_map/ppermute | solution.py:351
  169.6 2.4 collective-permute-start.7
  172.1 0.9 bitcast_dynamic-update-slice_fusion.6
  173.0 8.4 %collective-permute-start.8 = (s32[4,16]{1,0:T(4,128)S(1)}, s32[4,16]{1,0:T(4,128)S(1)}, u32[]{:S(2)}, u32[]{:S(2)}) collective-permute-start(s32[4,16]{1,0:T(4,128)S(1)} %pad_add_fusion.2), channel_id=1, source_target_pairs={{0,64},{16,80},{32,96},{48,112},{64,128},{80,144},{96,160},{112,17... | collective-permute-start | bytes 776 | tf_op jit(solution)/shard_map/ppermute | solution.py:342
  181.4 2.0 bitcast_dynamic-update-slice_fusion.5
  183.4 3.3 %collective-permute-done.8 = s32[4,16]{1,0:T(4,128)S(1)} collective-permute-done((s32[4,16]{1,0:T(4,128)S(1)}, s32[4,16]{1,0:T(4,128)S(1)}, u32[]{:S(2)}, u32[]{:S(2)}) %collective-permute-start.8) | collective-permute-done | bytes 288 | tf_op jit(solution)/shard_map/ppermute | solution.py:342
  186.7 0.2 collective-permute-done.7
  186.9 4.5 %collective-permute-start.13 = (bf16[2,128,640]{2,1,0:T(8,128)(2,1)S(1)}, bf16[2,128,640]{2,1,0:T(8,128)(2,1)S(1)}, u32[]{:S(2)}, u32[]{:S(2)}) collective-permute-start(bf16[2,128,640]{2,1,0:T(8,128)(2,1)S(1)} %slice.6), channel_id=1, source_target_pairs={{0,2},{2,4},{4,6},{6,8},{8,10},{10,12},{12,14},{14,0},{1,3},{3,5},... | collective-permute-start | bytes 983048 | tf_op jit(solution)/shard_map/ppermute | solution.py:358
  191.4 2.0 collective-permute-start.14
  193.4 2.0 bitcast_dynamic-update-slice_fusion.4
  195.4 0.9 bitcast_dynamic-update-slice_fusion.3
  196.3 5.4 %collective-permute-done.14 = bf16[2,128,640]{2,1,0:T(8,128)(2,1)S(1)} collective-permute-done((bf16[2,128,640]{2,1,0:T(8,128)(2,1)S(1)}, bf16[2,128,640]{2,1,0:T(8,128)(2,1)S(1)}, u32[]{:S(2)}, u32[]{:S(2)}) %collective-permute-start.14) | collective-permute-done | bytes 327712 | tf_op jit(solution)/shard_map/ppermute | solution.py:359
  201.6 1.0 fusion.3
  202.6 1.0 bitcast_dynamic-update-slice_fusion.2
  203.6 2.0 bitcast_dynamic-update-slice_fusion.1
  205.6 0.9 bitcast_dynamic-update-slice_fusion.w_own
  206.5 1.9 collective-permute-start.15
  208.5 1.2 copy.16
  209.7 2.4 collective-permute-start.11
  212.2 2.0 collective-permute-start.10
  214.1 2.4 collective-permute-start.12
  216.6 13.4 %collective-permute-start.9 = (s32[8,16]{1,0:T(8,128)S(1)}, s32[8,16]{1,0:T(8,128)S(1)}, u32[]{:S(2)}, u32[]{:S(2)}) collective-permute-start(s32[8,16]{1,0:T(8,128)S(1)} %pad_add_fusion.1), channel_id=1, source_target_pairs={{0,128},{16,144},{32,160},{48,176},{64,192},{80,208},{96,224},{112... | collective-permute-start | bytes 1544 | tf_op jit(solution)/shard_map/ppermute | solution.py:342
  230.1 1.5 collective-permute-done.9
  231.6 0.5 select_reduce_fusion.2.code_ref
  232.1 1.0 copy-done.2
  233.1 10.9 %score_units.1 = f32[8,128]{1,0:T(8,128)S(1)} custom-call(s32[16]{0:T(128)S(1)} %select_reduce_fusion.2.code_ref, s32[2]{0:T(128)S(1)} %pad_add_fusion.4.core_ref, bf16[1,512]{1,0:T(2,128)(2,1)S(1)} %broadcast_in_dim.116.gain_own, bf16[1,512]{1,0:T(2,128)(2,1)S(1)} %collective-permute-done.10.gain_other, bf16[1,1024]{1,0:T(2,128)(2,1)S(1)} %broadcast_in_dim.117.mlp_gain_ref, ...), custom_call_target="tpu_custom_call" | custom-call | tf_op jit(solution)/shard_map/score_units/pallas_call | solution.py:254
  244.1 33.5 %all_to_all.17 = f32[16,1,64]{2,1,0:T(1,128)S(1)} all-to-all(f32[16,1,64]{2,1,0:T(1,128)S(1)} %bitcast.39), channel_id=1, replica_groups=mesh['groups'=2,'users'=16,'routers'=8,'heads'=2] {'users'}, dimensions={0} | all-to-all | bytes 8192 | tf_op jit(solution)/shard_map/all_to_all | solution.py:310
  277.6 1.9 collective-permute-start.16
  279.6 1.1 collective-permute-done.16
  280.8 0.1 select_reduce_fusion.1
  280.9 0.4 select_reduce_fusion
  281.3 0.7 broadcast_select_fusion
  (53 shorter events, 0.8 us)
Async XLA Ops:
  0.0 2.9 %copy-start = (bf16[16,64,1024]{2,1,0:T(8,128)(2,1)S(1)}, bf16[16,64,1024]{2,1,0:T(8,128)(2,1)}, u32[]{:S(2)}) copy-start(bf16[16,64,1024]{2,1,0:T(8,128)(2,1)} %param.12) | copy-start | bytes 6291460
  2.9 3.7 %copy-start.3 = (bf16[4,128,512]{2,1,0:T(8,128)(2,1)S(1)}, bf16[4,128,512]{2,1,0:T(8,128)(2,1)}, u32[]{:S(2)}) copy-start(bf16[4,128,512]{2,1,0:T(8,128)(2,1)} %param.18) | copy-start | bytes 1572868
  2.9 3.7 %copy-start.4 = (bf16[512,128]{1,0:T(8,128)(2,1)S(1)}, bf16[512,128]{1,0:T(8,128)(2,1)}, u32[]{:S(2)}) copy-start(bf16[512,128]{1,0:T(8,128)(2,1)} %param.20) | copy-start | bytes 393220
  2.9 47.1 %copy-start.6 = (s32[16]{0:T(128)S(1)}, s32[16]{0:T(128)}, u32[]{:S(2)}) copy-start(s32[16]{0:T(128)} %param.15) | copy-start | bytes 196
  2.9 47.1 %copy-start.8 = (s32[16]{0:T(128)S(1)}, s32[16]{0:T(128)}, u32[]{:S(2)}) copy-start(s32[16]{0:T(128)} %param.14) | copy-start | bytes 196
  2.9 47.1 %copy-start.5 = (s32[16,1]{0,1:T(1,128)S(1)}, s32[16,1]{0,1:T(1,128)}, u32[]{:S(2)}) copy-start(s32[16,1]{0,1:T(1,128)} %param.13) | copy-start | bytes 196
  6.7 51.6 %collective-permute-start = (bf16[4,128,640]{2,1,0:T(8,128)(2,1)S(1)}, bf16[4,128,640]{2,1,0:T(8,128)(2,1)S(1)}, u32[]{:S(2)}, u32[]{:S(2)}) collective-permute-start(bf16[4,128,640]{2,1,0:T(8,128)(2,1)S(1)} %pad_maximum_fusion), channel_id=1, source_target_pairs={{0,2},{2,4},{4,6},{6,8},{8,10},{10,12},{12,14},{14,0},{1,3},{3,5},... | collective-permute-start | bytes 1966088 | tf_op jit(solution)/shard_map/ppermute | solution.py:351
  48.0 13.8 %collective-permute-start.1 = (bf16[4,128,640]{2,1,0:T(8,128)(2,1)S(1)}, bf16[4,128,640]{2,1,0:T(8,128)(2,1)}, u32[]{:S(2)}, u32[]{:S(2)}) collective-permute-start(bf16[4,128,640]{2,1,0:T(8,128)(2,1)S(1)} %pad_maximum_fusion), channel_id=1, source_target_pairs={{0,14},{2,0},{4,2},{6,4},{8,6},{10,8},{12,10},{14,12},{1,15},{3,1}... | collective-permute-start | bytes 1966088 | tf_op jit(solution)/shard_map/ppermute | solution.py:352
  50.1 8.1 %collective-permute-start.2 = (s32[1,16]{1,0:T(1,128)S(1)}, s32[1,16]{1,0:T(1,128)S(1)}, u32[]{:S(2)}, u32[]{:S(2)}) collective-permute-start(s32[1,16]{1,0:T(1,128)S(1)} %bitcast.43), channel_id=1, source_target_pairs={{0,16},{16,32},{32,48},{48,64},{64,80},{80,96},{96,112},{112,128},... | collective-permute-start | bytes 200 | tf_op jit(solution)/shard_map/ppermute | solution.py:342
  61.9 104.3 %collective-permute-start.3 = (bf16[4,128,640]{2,1,0:T(8,128)(2,1)S(1)}, bf16[4,128,640]{2,1,0:T(8,128)(2,1)}, u32[]{:S(2)}, u32[]{:S(2)}) collective-permute-start(bf16[4,128,640]{2,1,0:T(8,128)(2,1)S(1)} %collective-permute-done), channel_id=1, source_target_pairs={{0,2},{2,4},{4,6},{6,8},{8,10},{10,12},{12,14},{14,0},{1,3},{3,5},... | collective-permute-start | bytes 1966088 | tf_op jit(solution)/shard_map/ppermute | solution.py:351
  63.8 102.3 %collective-permute-start.4 = (bf16[4,128,640]{2,1,0:T(8,128)(2,1)}, bf16[4,128,640]{2,1,0:T(8,128)(2,1)}, u32[]{:S(2)}, u32[]{:S(2)}) collective-permute-start(bf16[4,128,640]{2,1,0:T(8,128)(2,1)} %collective-permute-done.1), channel_id=1, source_target_pairs={{0,14},{2,0},{4,2},{6,4},{8,6},{10,8},{12,10},{14,12},{1,15},{3,1}... | collective-permute-start | bytes 1966088 | tf_op jit(solution)/shard_map/ppermute | solution.py:352
  67.8 164.3 %all-to-all-start = ((bf16[16,64,1024]{2,1,0:T(8,128)(2,1)}), bf16[16,64,1024]{2,1,0:T(8,128)(2,1)}, u32[]{:S(2)}, u32[]{:S(2)}) async-start(bf16[16,64,1024]{2,1,0:T(8,128)(2,1)} %bitcast.34), calls=%async_computation | async-start | bytes 4194304 | tf_op jit(solution)/shard_map/all_to_all | solution.py:310
  78.0 88.1 %collective-permute-start.5 = (s32[2,16]{1,0:T(2,128)S(1)}, s32[2,16]{1,0:T(2,128)S(1)}, u32[]{:S(2)}, u32[]{:S(2)}) collective-permute-start(s32[2,16]{1,0:T(2,128)S(1)} %pad_add_fusion.3), channel_id=1, source_target_pairs={{0,32},{16,48},{32,64},{48,80},{64,96},{80,112},{96,128},{112,144}... | collective-permute-start | bytes 392 | tf_op jit(solution)/shard_map/ppermute | solution.py:342
  166.2 20.5 %collective-permute-start.6 = (bf16[4,128,640]{2,1,0:T(8,128)(2,1)}, bf16[4,128,640]{2,1,0:T(8,128)(2,1)S(1)}, u32[]{:S(2)}, u32[]{:S(2)}) collective-permute-start(bf16[4,128,640]{2,1,0:T(8,128)(2,1)} %collective-permute-done.3), channel_id=1, source_target_pairs={{0,2},{2,4},{4,6},{6,8},{8,10},{10,12},{12,14},{14,0},{1,3},{3,5},... | collective-permute-start | bytes 1966088 | tf_op jit(solution)/shard_map/ppermute | solution.py:351
  169.6 17.3 %collective-permute-start.7 = (bf16[4,128,640]{2,1,0:T(8,128)(2,1)}, bf16[4,128,640]{2,1,0:T(8,128)(2,1)S(1)}, u32[]{:S(2)}, u32[]{:S(2)}) collective-permute-start(bf16[4,128,640]{2,1,0:T(8,128)(2,1)} %collective-permute-done.4), channel_id=1, source_target_pairs={{0,14},{2,0},{4,2},{6,4},{8,6},{10,8},{12,10},{14,12},{1,15},{3,1}... | collective-permute-start | bytes 1966088 | tf_op jit(solution)/shard_map/ppermute | solution.py:352
  173.0 13.7 %collective-permute-start.8 = (s32[4,16]{1,0:T(4,128)S(1)}, s32[4,16]{1,0:T(4,128)S(1)}, u32[]{:S(2)}, u32[]{:S(2)}) collective-permute-start(s32[4,16]{1,0:T(4,128)S(1)} %pad_add_fusion.2), channel_id=1, source_target_pairs={{0,64},{16,80},{32,96},{48,112},{64,128},{80,144},{96,160},{112,17... | collective-permute-start | bytes 776 | tf_op jit(solution)/shard_map/ppermute | solution.py:342
  183.4 28.8 %copy-start.9 = (bf16[512]{0:T(512)(128)(2,1)S(1)}, bf16[512]{0:T(512)(128)(2,1)}, u32[]{:S(2)}) copy-start(bf16[512]{0:T(512)(128)(2,1)} %param.19) | copy-start | bytes 3076
  183.4 30.7 %copy-start.1 = (bf16[2,256,512]{2,1,0:T(8,128)(2,1)S(1)}, bf16[2,256,512]{2,1,0:T(8,128)(2,1)}, u32[]{:S(2)}) copy-start(bf16[2,256,512]{2,1,0:T(8,128)(2,1)} %v_own.1) | copy-start | bytes 1572868
  183.4 46.7 %copy-start.7 = (bf16[1024]{0:T(1024)(128)(2,1)S(1)}, bf16[1024]{0:T(1024)(128)(2,1)}, u32[]{:S(2)}) copy-start(bf16[1024]{0:T(1024)(128)(2,1)} %param.21) | copy-start | bytes 6148
  183.4 46.7 %copy-start.10 = (bf16[256]{0:T(256)(128)(2,1)S(1)}, bf16[256]{0:T(256)(128)(2,1)}, u32[]{:S(2)}) copy-start(bf16[256]{0:T(256)(128)(2,1)} %param.23) | copy-start | bytes 1540
  186.9 9.4 %collective-permute-start.13 = (bf16[2,128,640]{2,1,0:T(8,128)(2,1)S(1)}, bf16[2,128,640]{2,1,0:T(8,128)(2,1)S(1)}, u32[]{:S(2)}, u32[]{:S(2)}) collective-permute-start(bf16[2,128,640]{2,1,0:T(8,128)(2,1)S(1)} %slice.6), channel_id=1, source_target_pairs={{0,2},{2,4},{4,6},{6,8},{8,10},{10,12},{12,14},{14,0},{1,3},{3,5},... | collective-permute-start | bytes 983048 | tf_op jit(solution)/shard_map/ppermute | solution.py:358
  191.4 10.2 %collective-permute-start.14 = (bf16[2,128,640]{2,1,0:T(8,128)(2,1)S(1)}, bf16[2,128,640]{2,1,0:T(8,128)(2,1)S(1)}, u32[]{:S(2)}, u32[]{:S(2)}) collective-permute-start(bf16[2,128,640]{2,1,0:T(8,128)(2,1)S(1)} %slice.7), channel_id=1, source_target_pairs={{0,14},{2,0},{4,2},{6,4},{8,6},{10,8},{12,10},{14,12},{1,15},{3,1}... | collective-permute-start | bytes 983048 | tf_op jit(solution)/shard_map/ppermute | solution.py:359
  206.5 25.6 %collective-permute-start.15 = (bf16[8,4,128,640]{3,2,1,0:T(8,128)(2,1)}, bf16[8,4,128,640]{3,2,1,0:T(8,128)(2,1)}, u32[]{:S(2)}, u32[]{:S(2)}) collective-permute-start(bf16[8,4,128,640]{3,2,1,0:T(8,128)(2,1)} %bitcast_dynamic-update-slice_fusion.w_own), channel_id=1, source_target_pairs={{0,1},{1,0},{2,3},{3,2},{4,5},{5,4},{6,7},{7,6},{8,9},{9,8},{10,11... | collective-permute-start | bytes 15728648 | tf_op jit(solution)/shard_map/ppermute | solution.py:307
  209.7 22.4 %collective-permute-start.11 = (bf16[2,512,256]{2,1,0:T(8,128)(2,1)S(1)}, bf16[2,512,256]{2,1,0:T(8,128)(2,1)}, u32[]{:S(2)}, u32[]{:S(2)}) collective-permute-start(bf16[2,512,256]{2,1,0:T(8,128)(2,1)S(1)} %bitcast.32), channel_id=1, source_target_pairs={{0,1},{1,0},{2,3},{3,2},{4,5},{5,4},{6,7},{7,6},{8,9},{9,8},{10,11... | collective-permute-start | bytes 1572872 | tf_op jit(solution)/shard_map/ppermute | solution.py:307
  212.2 19.9 %collective-permute-start.10 = (bf16[1,512]{1,0:T(2,128)(2,1)S(1)}, bf16[1,512]{1,0:T(2,128)(2,1)S(1)}, u32[]{:S(2)}, u32[]{:S(2)}) collective-permute-start(bf16[1,512]{1,0:T(2,128)(2,1)S(1)} %broadcast_in_dim.116.gain_own), channel_id=1, source_target_pairs={{0,1},{1,0},{2,3},{3,2},{4,5},{5,4},{6,7},{7,6},{8,9},{9,8},{10,11... | collective-permute-start | bytes 3080 | tf_op jit(solution)/shard_map/ppermute | solution.py:307
  214.1 17.9 %collective-permute-start.12 = (bf16[2,256,512]{2,1,0:T(8,128)(2,1)S(1)}, bf16[2,256,512]{2,1,0:T(8,128)(2,1)}, u32[]{:S(2)}, u32[]{:S(2)}) collective-permute-start(bf16[2,256,512]{2,1,0:T(8,128)(2,1)S(1)} %copy-done.1), channel_id=1, source_target_pairs={{0,1},{1,0},{2,3},{3,2},{4,5},{5,4},{6,7},{7,6},{8,9},{9,8},{10,11... | collective-permute-start | bytes 1572872 | tf_op jit(solution)/shard_map/ppermute | solution.py:307
  216.6 14.9 %collective-permute-start.9 = (s32[8,16]{1,0:T(8,128)S(1)}, s32[8,16]{1,0:T(8,128)S(1)}, u32[]{:S(2)}, u32[]{:S(2)}) collective-permute-start(s32[8,16]{1,0:T(8,128)S(1)} %pad_add_fusion.1), channel_id=1, source_target_pairs={{0,128},{16,144},{32,160},{48,176},{64,192},{80,208},{96,224},{112... | collective-permute-start | bytes 1544 | tf_op jit(solution)/shard_map/ppermute | solution.py:342
  232.1 1.0 copy-start.2
  277.6 3.1 %collective-permute-start.16 = (f32[16,64]{1,0:T(8,128)S(1)}, f32[16,64]{1,0:T(8,128)S(1)}, u32[]{:S(2)}, u32[]{:S(2)}) collective-permute-start(f32[16,64]{1,0:T(8,128)S(1)} %bitcast.37), channel_id=1, source_target_pairs={{0,1},{1,0},{2,3},{3,2},{4,5},{5,4},{6,7},{7,6},{8,9},{9,8},{10,11... | collective-permute-start | bytes 12296 | tf_op jit(solution)/shard_map/ppermute | solution.py:307

commit v6 on v5

--- a/solution.py
+++ b/solution.py
@@ -310,7 +310,10 @@
         return lax.all_to_all(x, "users", split_axis=0, concat_axis=0, tiled=True)
 
     target = block_owner[:, 0]
-    me = lax.axis_index("users")
+    goes = target[None, :] == lax.broadcasted_iota(jnp.int32, (peers, blocks), 0)
+    weight = jnp.where(block_user == 0, CODE + 1, 1) * block_fill
+    codes = jnp.sum(jnp.where(goes, weight[None, :], 0), axis=1)
+    codes = exchanged(codes.reshape(peers, 1)).reshape(peers)
 
     index = jnp.arange(blocks, dtype=jnp.int32)
     same = target[:, None] == target[None, :]
@@ -327,19 +330,8 @@
     sent = jnp.dot(
         (slot == goes_to).astype(jnp.bfloat16), flat_items, preferred_element_type=jnp.float32
     ).astype(jnp.bfloat16)
-    sent, block_user, w_in = lax.optimization_barrier((sent, block_user, w_in))
+    sent, w_in = lax.optimization_barrier((sent, w_in))
     arrived = exchanged(sent.reshape(peers, block_width, model_width))
-
-    goes = target[None, :] == lax.broadcasted_iota(jnp.int32, (peers, blocks), 0)
-    weight = jnp.where(block_user == 0, CODE + 1, 1) * block_fill
-    every = jnp.sum(jnp.where(goes, weight[None, :], 0), axis=1)[None, :]
-
-    def doubled(rows):
-        step = rows.shape[0]
-        if step >= peers:
-            return rows
-        pairs = [(k, (k + step) % peers) for k in range(peers)]
-        return jnp.concatenate([rows, lax.ppermute(rows, "users", pairs)], axis=0)
 
     matrices, share, _ = w_in.shape
     w_local = jnp.concatenate([w_in, w_o.reshape(matrices, share, share)], axis=2)
@@ -350,22 +342,12 @@
     for step in range(1, routers // 2):
         from_below = lax.ppermute(from_below, "routers", up)
         from_above = lax.ppermute(from_above, "routers", down)
-        every = doubled(every)
-        from_below, from_above, every = lax.optimization_barrier((from_below, from_above, every))
         ring[routers - step] = from_below
         ring[step] = from_above
     half = matrices // 2
     lower = lax.ppermute(from_below[:half], "routers", up)
     upper = lax.ppermute(from_above[half:], "routers", down)
     ring[routers // 2] = jnp.concatenate([lower, upper], axis=0)
-    every = doubled(every)
-    while every.shape[0] < peers:
-        every = doubled(every)
-    source = (me + peers - lax.broadcasted_iota(jnp.int32, (peers, peers, peers), 1)) % peers
-    wanted = (source == lax.broadcasted_iota(jnp.int32, (peers, peers, peers), 0)) & (
-        lax.broadcasted_iota(jnp.int32, (peers, peers, peers), 2) == me
-    )
-    codes = jnp.sum(jnp.where(wanted, every[None], 0), axis=(1, 2))
     w_ring = jnp.stack([ring[k] for k in range(routers)])
     own = (jnp.swapaxes(prefix_keys, 1, 2), prefix_values, attn_gain[None, :], w_ring)
     other = jax.tree.map(swapped, own)
@@ -373,10 +355,16 @@
     scores = score_units(
         codes, core_index, arrived, own, other, mlp_gain[None, :], w_one, w_two[None, :]
     ).reshape(peers, block_width)
-    returned = exchanged(scores)
-    returned = jnp.concatenate([returned, swapped(returned)], axis=1)
+    back = jnp.broadcast_to(scores[:, None, :], (peers, cores, block_width))
+    returned = lax.all_to_all(
+        back.reshape(peers * cores, block_width),
+        ("users", "heads"),
+        split_axis=0,
+        concat_axis=0,
+        tiled=True,
+    ).reshape(peers, cores * block_width)
     row_scores = jnp.sum(jnp.where(goes[:, :, None], returned[:, None, :], 0.0), axis=0)
-    lane = jnp.where(packed % cores == core, 0, block_width) + packed // cores
+    lane = packed % cores * block_width + packed // cores
     wanted = lane[:, :, None] == lax.broadcasted_iota(
         jnp.int32, (blocks, block_width, cores * block_width), 2
     )

time: 285 us -> 235 us (0.82)
  waiting for transfers between devices: 105 us -> 72.3 us
  starting transfers between devices: 111 us -> 100 us
  blocking collectives: 33.5 us -> 25.5 us
    ppermute x4 -> x0, waiting for transfers between devices: 94.5 us -> none  [doubled(): return jnp.concatenate([rows, lax.ppermute(rows, 'users', pairs)], axis=0)]
    all_to_all x1, waiting for transfers between devices: 0.01 us -> 43.3 us  [exchanged(): return lax.all_to_all(x, 'users', split_axis=0, concat_axis=0, tiled=True)]
    ppermute x4 -> x0, starting transfers between devices: 28.2 us -> none  [doubled(): return jnp.concatenate([rows, lax.ppermute(rows, 'users', pairs)], axis=0)]
    all_to_all x0 -> x1, starting transfers between devices: none -> 21.9 us  [local(): lax.all_to_all(back.reshape(peers * cores, block_width), ('users', 'heads...]
    all_to_all x0 -> x1, waiting for transfers between devices: none -> 11.8 us  [local(): lax.all_to_all(back.reshape(peers * cores, block_width), ('users', 'heads...]
    ppermute x3, waiting for transfers between devices: 3.75 us -> 13.7 us  [local(): from_above = lax.ppermute(from_above, 'routers', down)]
    all_to_all x1, blocking collectives: 33.5 us -> 25.5 us  [exchanged(): return lax.all_to_all(x, 'users', split_axis=0, concat_axis=0, tiled=True)]
    all_to_all x1, starting transfers between devices: 10.2 us -> 4.83 us  [exchanged(): return lax.all_to_all(x, 'users', split_axis=0, concat_axis=0, tiled=True)]
  transfers between devices with their start and end apart: 18 -> 14, of which waited for: 8 -> 7; matrix products, arithmetic and copies ran while one was open for 5% -> 5% of each run, Pallas kernels for 0% -> 0%
where the time goes in v6:
time: 235 us; the launch traced here: 233 us
  starting transfers between devices  100 us (43%)
  waiting for transfers between devices  72.3 us (31%)
  blocking collectives  25.5 us (11%)
  local copies, waits for them, and re-layouts  12.8 us (5%)
  Pallas kernels  10.9 us (5%)
  other arithmetic  7.49 us (3%)
  matrix products  3.67 us (2%)
    ppermute x3, starting transfers between devices, local(): from_below = lax.ppermute(from_below, 'routers', up)  50.4 us
    all_to_all x1, waiting for transfers between devices, exchanged(): return lax.all_to_all(x, 'users', split_axis=0, concat_axis=0, tiled=True)  43.3 us
    all_to_all x1, blocking collectives, exchanged(): return lax.all_to_all(x, 'users', split_axis=0, concat_axis=0, tiled=True)  25.5 us
    all_to_all x1, starting transfers between devices, local(): lax.all_to_all(back.reshape(peers * cores, block_width), ('users', 'heads...  21.9 us
    ppermute x3, waiting for transfers between devices, local(): from_above = lax.ppermute(from_above, 'routers', down)  13.7 us
    all_to_all x1, waiting for transfers between devices, local(): lax.all_to_all(back.reshape(peers * cores, block_width), ('users', 'heads...  11.8 us
    pallas_call x1, Pallas kernels, score_units(): pl.pallas_call(score_kernel, out_shape=jax.ShapeDtypeStruct((rows // lane...  10.9 us
    unnamed x26, local copies, waits for them, and re-layouts  10.2 us
  transfers between devices with their start and end apart: 14, of which 7 were waited for; matrix products, arithmetic and copies ran while one was open for 5% of the time, Pallas kernels for 0%

profile of v6, /device:TPU:78, one launch (start us, length us, event | category | flops | bytes accessed | tf_op | source)
XLA Modules:
  0.0 233.1 jit_solution(9236475164874140520)
XLA Ops:
  0.0 0.9 iota_compare_fusion.7
  0.9 0.7 fusion.20
  1.6 0.7 multiply_bitcast_fusion
  2.2 0.9 select_reduce_fusion.3
  3.1 0.1 fusion.5
  3.4 0.1 lt.64
  3.6 3.7 %fusion.2 = bf16[1024,1024]{1,0:T(8,128)(2,1)} fusion(bf16[1024,1024]{1,0:T(8,128)(2,1)S(1)} %bitcast.30, s32[1024]{0:T(1024)S(1)} %fusion.16), kind=kOutput, calls=%fused_computation.3 | convolution fusion | flops 2149580800 | bytes 4198400 | tf_op jit(solution)/shard_map/dot_general | solution.py:330
  7.3 3.2 %collective-permute-start.3 = (bf16[4,128,640]{2,1,0:T(8,128)(2,1)S(1)}, bf16[4,128,640]{2,1,0:T(8,128)(2,1)}, u32[]{:S(2)}, u32[]{:S(2)}) collective-permute-start(bf16[4,128,640]{2,1,0:T(8,128)(2,1)S(1)} %pad_maximum_fusion), channel_id=1, source_target_pairs={{0,14},{2,0},{4,2},{6,4},{8,6},{10,8},{12,10},{14,12},{1,15},{3,1}... | collective-permute-start | bytes 1966088 | tf_op jit(solution)/shard_map/ppermute | solution.py:344
  10.6 40.1 %collective-permute-start.6 = (bf16[4,128,640]{2,1,0:T(8,128)(2,1)S(1)}, bf16[4,128,640]{2,1,0:T(8,128)(2,1)S(1)}, u32[]{:S(2)}, u32[]{:S(2)}) collective-permute-start(bf16[4,128,640]{2,1,0:T(8,128)(2,1)S(1)} %pad_maximum_fusion), channel_id=1, source_target_pairs={{0,2},{2,4},{4,6},{6,8},{8,10},{10,12},{12,14},{14,0},{1,3},{3,5},... | collective-permute-start | bytes 1966088 | tf_op jit(solution)/shard_map/ppermute | solution.py:343
  50.6 6.7 %collective-permute-done.3 = bf16[4,128,640]{2,1,0:T(8,128)(2,1)} collective-permute-done((bf16[4,128,640]{2,1,0:T(8,128)(2,1)S(1)}, bf16[4,128,640]{2,1,0:T(8,128)(2,1)}, u32[]{:S(2)}, u32[]{:S(2)}) %collective-permute-start.3) | collective-permute-done | bytes 655392 | tf_op jit(solution)/shard_map/ppermute | solution.py:344
  57.3 1.9 collective-permute-start.4
  59.3 5.2 %collective-permute-start.7 = (bf16[4,128,640]{2,1,0:T(8,128)(2,1)S(1)}, bf16[4,128,640]{2,1,0:T(8,128)(2,1)}, u32[]{:S(2)}, u32[]{:S(2)}) collective-permute-start(bf16[4,128,640]{2,1,0:T(8,128)(2,1)S(1)} %collective-permute-done.6), channel_id=1, source_target_pairs={{0,2},{2,4},{4,6},{6,8},{8,10},{10,12},{12,14},{14,0},{1,3},{3,5},... | collective-permute-start | bytes 1966088 | tf_op jit(solution)/shard_map/ppermute | solution.py:343
  64.5 0.1 copy.18
  64.5 25.5 %all_to_all.23 = s32[16,1,1]{2,1,0:T(1,128)S(1)} all-to-all(s32[16,1,1]{2,1,0:T(1,128)S(1)} %copy.18), channel_id=1, replica_groups=mesh['groups'=2,'users'=16,'routers'=8,'heads'=2] {'users'}, dimensions={0} | all-to-all | bytes 128 | tf_op jit(solution)/shard_map/all_to_all | solution.py:310
  90.1 4.8 %all-to-all-start.1 = ((bf16[16,64,1024]{2,1,0:T(8,128)(2,1)}), bf16[16,64,1024]{2,1,0:T(8,128)(2,1)}, u32[]{:S(2)}, u32[]{:S(2)}) async-start(bf16[16,64,1024]{2,1,0:T(8,128)(2,1)} %bitcast.33), calls=%async_computation.1 | async-start | bytes 4194304 | tf_op jit(solution)/shard_map/all_to_all | solution.py:310
  94.9 2.0 collective-permute-start.5
  96.9 5.2 %collective-permute-start.8 = (bf16[4,128,640]{2,1,0:T(8,128)(2,1)}, bf16[4,128,640]{2,1,0:T(8,128)(2,1)S(1)}, u32[]{:S(2)}, u32[]{:S(2)}) collective-permute-start(bf16[4,128,640]{2,1,0:T(8,128)(2,1)} %collective-permute-done.7), channel_id=1, source_target_pairs={{0,2},{2,4},{4,6},{6,8},{8,10},{10,12},{12,14},{14,0},{1,3},{3,5},... | collective-permute-start | bytes 1966088 | tf_op jit(solution)/shard_map/ppermute | solution.py:343
  102.0 0.9 bitcast_dynamic-update-slice_fusion.6
  103.0 2.0 bitcast_dynamic-update-slice_fusion.5
  105.0 7.0 %collective-permute-done.5 = bf16[4,128,640]{2,1,0:T(8,128)(2,1)S(1)} collective-permute-done((bf16[4,128,640]{2,1,0:T(8,128)(2,1)}, bf16[4,128,640]{2,1,0:T(8,128)(2,1)S(1)}, u32[]{:S(2)}, u32[]{:S(2)}) %collective-permute-start.5) | collective-permute-done | bytes 655392 | tf_op jit(solution)/shard_map/ppermute | solution.py:344
  112.0 2.0 collective-permute-start.10
  114.0 5.2 %collective-permute-start.9 = (bf16[2,128,640]{2,1,0:T(8,128)(2,1)S(1)}, bf16[2,128,640]{2,1,0:T(8,128)(2,1)S(1)}, u32[]{:S(2)}, u32[]{:S(2)}) collective-permute-start(bf16[2,128,640]{2,1,0:T(8,128)(2,1)S(1)} %slice.8), channel_id=1, source_target_pairs={{0,2},{2,4},{4,6},{6,8},{8,10},{10,12},{12,14},{14,0},{1,3},{3,5},... | collective-permute-start | bytes 983048 | tf_op jit(solution)/shard_map/ppermute | solution.py:348
  119.2 2.0 bitcast_dynamic-update-slice_fusion.4
  121.2 0.9 bitcast_dynamic-update-slice_fusion.3
  122.1 0.1 collective-permute-done.10
  122.2 1.5 collective-permute-done.9
  123.7 1.0 fusion.3
  124.7 1.0 bitcast_dynamic-update-slice_fusion.2
  125.7 2.0 bitcast_dynamic-update-slice_fusion.1
  127.6 0.9 bitcast_dynamic-update-slice_fusion.w_own
  128.5 1.9 collective-permute-start.11
  130.5 1.2 copy.19
  131.7 2.4 %collective-permute-start.1 = (bf16[2,512,256]{2,1,0:T(8,128)(2,1)S(1)}, bf16[2,512,256]{2,1,0:T(8,128)(2,1)}, u32[]{:S(2)}, u32[]{:S(2)}) collective-permute-start(bf16[2,512,256]{2,1,0:T(8,128)(2,1)S(1)} %bitcast.31), channel_id=1, source_target_pairs={{0,1},{1,0},{2,3},{3,2},{4,5},{5,4},{6,7},{7,6},{8,9},{9,8},{10,11... | collective-permute-start | bytes 1572872 | tf_op jit(solution)/shard_map/ppermute | solution.py:307
  134.2 2.0 collective-permute-start.2
  136.2 2.4 %collective-permute-start = (bf16[1,512]{1,0:T(2,128)(2,1)S(1)}, bf16[1,512]{1,0:T(2,128)(2,1)S(1)}, u32[]{:S(2)}, u32[]{:S(2)}) collective-permute-start(bf16[1,512]{1,0:T(2,128)(2,1)S(1)} %broadcast_in_dim.101.gain_own), channel_id=1, source_target_pairs={{0,1},{1,0},{2,3},{3,2},{4,5},{5,4},{6,7},{7,6},{8,9},{9,8},{10,11... | collective-permute-start | bytes 3080 | tf_op jit(solution)/shard_map/ppermute | solution.py:307
  138.7 0.4 reduce.code_ref
  139.1 1.8 collective-permute-done.gain_other
  141.0 43.3 %all-to-all-done.1.x_hbm = bf16[16,64,1024]{2,1,0:T(8,128)(2,1)} async-done(((bf16[16,64,1024]{2,1,0:T(8,128)(2,1)}), bf16[16,64,1024]{2,1,0:T(8,128)(2,1)}, u32[]{:S(2)}, u32[]{:S(2)}) %all-to-all-start.1) | async-done | bytes 2097184 | tf_op jit(solution)/shard_map/all_to_all | solution.py:310
  184.3 1.0 copy-done.2
  185.3 10.9 %score_units.1 = f32[8,128]{1,0:T(8,128)S(1)} custom-call(s32[16]{0:T(128)S(1)} %reduce.code_ref, s32[2]{0:T(128)S(1)} %pad_add_fusion.core_ref, bf16[1,512]{1,0:T(2,128)(2,1)S(1)} %broadcast_in_dim.101.gain_own, bf16[1,512]{1,0:T(2,128)(2,1)S(1)} %collective-permute-done.gain_other, bf16[1,1024]{1,0:T(2,128)(2,1)S(1)} %broadcast_in_dim.102.mlp_gain_ref, ...), custom_call_target="tpu_custom_call" | custom-call | tf_op jit(solution)/shard_map/score_units/pallas_call | solution.py:254
  196.3 0.6 broadcast_in_dim.105
  196.9 21.9 %all-to-all-start.2 = ((f32[32,1,64]{2,1,0:T(1,128)}), f32[32,1,64]{2,1,0:T(1,128)S(1)}, u32[]{:S(2)}, u32[]{:S(2)}) async-start(f32[32,1,64]{2,1,0:T(1,128)} %bitcast.17), calls=%async_computation.2 | async-start | bytes 32768 | tf_op jit(solution)/shard_map/all_to_all | solution.py:359
  218.8 11.8 %all-to-all-done.2 = f32[32,1,64]{2,1,0:T(1,128)S(1)} async-done(((f32[32,1,64]{2,1,0:T(1,128)}), f32[32,1,64]{2,1,0:T(1,128)S(1)}, u32[]{:S(2)}, u32[]{:S(2)}) %all-to-all-start.2) | async-done | bytes 8224 | tf_op jit(solution)/shard_map/all_to_all | solution.py:359
  230.6 0.5 broadcast.179
  231.1 0.7 reduce.4
  231.9 0.1 select_reduce_fusion.1
  232.0 0.4 select_reduce_fusion
  232.4 0.7 broadcast_select_fusion
  (40 shorter events, 0.6 us)
Async XLA Ops:
  0.0 3.5 %copy-start = (bf16[16,64,1024]{2,1,0:T(8,128)(2,1)S(1)}, bf16[16,64,1024]{2,1,0:T(8,128)(2,1)}, u32[]{:S(2)}) copy-start(bf16[16,64,1024]{2,1,0:T(8,128)(2,1)} %param.12) | copy-start | bytes 6291460
  3.5 3.7 %copy-start.3 = (bf16[4,128,512]{2,1,0:T(8,128)(2,1)S(1)}, bf16[4,128,512]{2,1,0:T(8,128)(2,1)}, u32[]{:S(2)}) copy-start(bf16[4,128,512]{2,1,0:T(8,128)(2,1)} %param.18) | copy-start | bytes 1572868
  3.6 3.7 %copy-start.4 = (bf16[512,128]{1,0:T(8,128)(2,1)S(1)}, bf16[512,128]{1,0:T(8,128)(2,1)}, u32[]{:S(2)}) copy-start(bf16[512,128]{1,0:T(8,128)(2,1)} %param.20) | copy-start | bytes 393220
  7.3 50.0 %collective-permute-start.3 = (bf16[4,128,640]{2,1,0:T(8,128)(2,1)S(1)}, bf16[4,128,640]{2,1,0:T(8,128)(2,1)}, u32[]{:S(2)}, u32[]{:S(2)}) collective-permute-start(bf16[4,128,640]{2,1,0:T(8,128)(2,1)S(1)} %pad_maximum_fusion), channel_id=1, source_target_pairs={{0,14},{2,0},{4,2},{6,4},{8,6},{10,8},{12,10},{14,12},{1,15},{3,1}... | collective-permute-start | bytes 1966088 | tf_op jit(solution)/shard_map/ppermute | solution.py:344
  10.6 48.7 %collective-permute-start.6 = (bf16[4,128,640]{2,1,0:T(8,128)(2,1)S(1)}, bf16[4,128,640]{2,1,0:T(8,128)(2,1)S(1)}, u32[]{:S(2)}, u32[]{:S(2)}) collective-permute-start(bf16[4,128,640]{2,1,0:T(8,128)(2,1)S(1)} %pad_maximum_fusion), channel_id=1, source_target_pairs={{0,2},{2,4},{4,6},{6,8},{8,10},{10,12},{12,14},{14,0},{1,3},{3,5},... | collective-permute-start | bytes 1966088 | tf_op jit(solution)/shard_map/ppermute | solution.py:343
  57.3 37.6 %collective-permute-start.4 = (bf16[4,128,640]{2,1,0:T(8,128)(2,1)}, bf16[4,128,640]{2,1,0:T(8,128)(2,1)}, u32[]{:S(2)}, u32[]{:S(2)}) collective-permute-start(bf16[4,128,640]{2,1,0:T(8,128)(2,1)} %collective-permute-done.3), channel_id=1, source_target_pairs={{0,14},{2,0},{4,2},{6,4},{8,6},{10,8},{12,10},{14,12},{1,15},{3,1}... | collective-permute-start | bytes 1966088 | tf_op jit(solution)/shard_map/ppermute | solution.py:344
  59.3 37.6 %collective-permute-start.7 = (bf16[4,128,640]{2,1,0:T(8,128)(2,1)S(1)}, bf16[4,128,640]{2,1,0:T(8,128)(2,1)}, u32[]{:S(2)}, u32[]{:S(2)}) collective-permute-start(bf16[4,128,640]{2,1,0:T(8,128)(2,1)S(1)} %collective-permute-done.6), channel_id=1, source_target_pairs={{0,2},{2,4},{4,6},{6,8},{8,10},{10,12},{12,14},{14,0},{1,3},{3,5},... | collective-permute-start | bytes 1966088 | tf_op jit(solution)/shard_map/ppermute | solution.py:343
  90.1 94.2 %all-to-all-start.1 = ((bf16[16,64,1024]{2,1,0:T(8,128)(2,1)}), bf16[16,64,1024]{2,1,0:T(8,128)(2,1)}, u32[]{:S(2)}, u32[]{:S(2)}) async-start(bf16[16,64,1024]{2,1,0:T(8,128)(2,1)} %bitcast.33), calls=%async_computation.1 | async-start | bytes 4194304 | tf_op jit(solution)/shard_map/all_to_all | solution.py:310
  94.9 17.0 %collective-permute-start.5 = (bf16[4,128,640]{2,1,0:T(8,128)(2,1)}, bf16[4,128,640]{2,1,0:T(8,128)(2,1)S(1)}, u32[]{:S(2)}, u32[]{:S(2)}) collective-permute-start(bf16[4,128,640]{2,1,0:T(8,128)(2,1)} %collective-permute-done.4), channel_id=1, source_target_pairs={{0,14},{2,0},{4,2},{6,4},{8,6},{10,8},{12,10},{14,12},{1,15},{3,1}... | collective-permute-start | bytes 1966088 | tf_op jit(solution)/shard_map/ppermute | solution.py:344
  96.9 17.1 %collective-permute-start.8 = (bf16[4,128,640]{2,1,0:T(8,128)(2,1)}, bf16[4,128,640]{2,1,0:T(8,128)(2,1)S(1)}, u32[]{:S(2)}, u32[]{:S(2)}) collective-permute-start(bf16[4,128,640]{2,1,0:T(8,128)(2,1)} %collective-permute-done.7), channel_id=1, source_target_pairs={{0,2},{2,4},{4,6},{6,8},{8,10},{10,12},{12,14},{14,0},{1,3},{3,5},... | collective-permute-start | bytes 1966088 | tf_op jit(solution)/shard_map/ppermute | solution.py:343
  105.0 29.2 %copy-start.1 = (bf16[2,256,512]{2,1,0:T(8,128)(2,1)S(1)}, bf16[2,256,512]{2,1,0:T(8,128)(2,1)}, u32[]{:S(2)}) copy-start(bf16[2,256,512]{2,1,0:T(8,128)(2,1)} %v_own.1) | copy-start | bytes 1572868
  105.0 31.2 %copy-start.8 = (bf16[512]{0:T(512)(128)(2,1)S(1)}, bf16[512]{0:T(512)(128)(2,1)}, u32[]{:S(2)}) copy-start(bf16[512]{0:T(512)(128)(2,1)} %param.19) | copy-start | bytes 3076
  105.0 33.7 %copy-start.7 = (bf16[1024]{0:T(1024)(128)(2,1)S(1)}, bf16[1024]{0:T(1024)(128)(2,1)}, u32[]{:S(2)}) copy-start(bf16[1024]{0:T(1024)(128)(2,1)} %param.21) | copy-start | bytes 6148
  105.0 33.7 %copy-start.9 = (bf16[256]{0:T(256)(128)(2,1)S(1)}, bf16[256]{0:T(256)(128)(2,1)}, u32[]{:S(2)}) copy-start(bf16[256]{0:T(256)(128)(2,1)} %param.23) | copy-start | bytes 1540
  112.0 10.2 %collective-permute-start.10 = (bf16[2,128,640]{2,1,0:T(8,128)(2,1)S(1)}, bf16[2,128,640]{2,1,0:T(8,128)(2,1)S(1)}, u32[]{:S(2)}, u32[]{:S(2)}) collective-permute-start(bf16[2,128,640]{2,1,0:T(8,128)(2,1)S(1)} %slice.9), channel_id=1, source_target_pairs={{0,14},{2,0},{4,2},{6,4},{8,6},{10,8},{12,10},{14,12},{1,15},{3,1}... | collective-permute-start | bytes 983048 | tf_op jit(solution)/shard_map/ppermute | solution.py:349
  114.0 9.7 %collective-permute-start.9 = (bf16[2,128,640]{2,1,0:T(8,128)(2,1)S(1)}, bf16[2,128,640]{2,1,0:T(8,128)(2,1)S(1)}, u32[]{:S(2)}, u32[]{:S(2)}) collective-permute-start(bf16[2,128,640]{2,1,0:T(8,128)(2,1)S(1)} %slice.8), channel_id=1, source_target_pairs={{0,2},{2,4},{4,6},{6,8},{8,10},{10,12},{12,14},{14,0},{1,3},{3,5},... | collective-permute-start | bytes 983048 | tf_op jit(solution)/shard_map/ppermute | solution.py:348
  128.5 12.4 %collective-permute-start.11 = (bf16[8,4,128,640]{3,2,1,0:T(8,128)(2,1)}, bf16[8,4,128,640]{3,2,1,0:T(8,128)(2,1)}, u32[]{:S(2)}, u32[]{:S(2)}) collective-permute-start(bf16[8,4,128,640]{3,2,1,0:T(8,128)(2,1)} %bitcast_dynamic-update-slice_fusion.w_own), channel_id=1, source_target_pairs={{0,1},{1,0},{2,3},{3,2},{4,5},{5,4},{6,7},{7,6},{8,9},{9,8},{10,11... | collective-permute-start | bytes 15728648 | tf_op jit(solution)/shard_map/ppermute | solution.py:307
  131.7 9.2 %collective-permute-start.1 = (bf16[2,512,256]{2,1,0:T(8,128)(2,1)S(1)}, bf16[2,512,256]{2,1,0:T(8,128)(2,1)}, u32[]{:S(2)}, u32[]{:S(2)}) collective-permute-start(bf16[2,512,256]{2,1,0:T(8,128)(2,1)S(1)} %bitcast.31), channel_id=1, source_target_pairs={{0,1},{1,0},{2,3},{3,2},{4,5},{5,4},{6,7},{7,6},{8,9},{9,8},{10,11... | collective-permute-start | bytes 1572872 | tf_op jit(solution)/shard_map/ppermute | solution.py:307
  134.2 6.8 %collective-permute-start.2 = (bf16[2,256,512]{2,1,0:T(8,128)(2,1)S(1)}, bf16[2,256,512]{2,1,0:T(8,128)(2,1)}, u32[]{:S(2)}, u32[]{:S(2)}) collective-permute-start(bf16[2,256,512]{2,1,0:T(8,128)(2,1)S(1)} %copy-done.1), channel_id=1, source_target_pairs={{0,1},{1,0},{2,3},{3,2},{4,5},{5,4},{6,7},{7,6},{8,9},{9,8},{10,11... | collective-permute-start | bytes 1572872 | tf_op jit(solution)/shard_map/ppermute | solution.py:307
  136.2 4.8 %collective-permute-start = (bf16[1,512]{1,0:T(2,128)(2,1)S(1)}, bf16[1,512]{1,0:T(2,128)(2,1)S(1)}, u32[]{:S(2)}, u32[]{:S(2)}) collective-permute-start(bf16[1,512]{1,0:T(2,128)(2,1)S(1)} %broadcast_in_dim.101.gain_own), channel_id=1, source_target_pairs={{0,1},{1,0},{2,3},{3,2},{4,5},{5,4},{6,7},{7,6},{8,9},{9,8},{10,11... | collective-permute-start | bytes 3080 | tf_op jit(solution)/shard_map/ppermute | solution.py:307
  138.7 80.1 %copy-start.5 = (s32[16,1]{0,1:T(1,128)S(1)}, s32[16,1]{0,1:T(1,128)}, u32[]{:S(2)}) copy-start(s32[16,1]{0,1:T(1,128)} %param.13) | copy-start | bytes 196
  138.7 93.7 %copy-start.6 = (s32[16]{0:T(128)S(1)}, s32[16]{0:T(128)}, u32[]{:S(2)}) copy-start(s32[16]{0:T(128)} %param.15) | copy-start | bytes 196
  184.3 1.0 copy-start.2
  196.9 33.7 %all-to-all-start.2 = ((f32[32,1,64]{2,1,0:T(1,128)}), f32[32,1,64]{2,1,0:T(1,128)S(1)}, u32[]{:S(2)}, u32[]{:S(2)}) async-start(f32[32,1,64]{2,1,0:T(1,128)} %bitcast.17), calls=%async_computation.2 | async-start | bytes 32768 | tf_op jit(solution)/shard_map/all_to_all | solution.py:359

commit v7 on v6

--- a/solution.py
+++ b/solution.py
@@ -11,15 +11,54 @@
 TILE = 256
 CHUNK = 256
 ALIGN = 16
-CODE = 256
+CODE = 128
+UNUSED = 200.0
+HEADER = 64.0
+LOW = 32.0
+HIGH = 4096.0
+TINY = 2.0**-110
+TINY_MARK = 2.0**14
+LIFT = 2.0**125
 
 
 def half_silu(half):
     return half * (1.0 + jnp.tanh(half))
 
 
+def marked(rows, count, first):
+    slots = rows.shape[1]
+    slot = lax.broadcasted_iota(jnp.int32, rows.shape, 1)
+    lane = lax.broadcasted_iota(jnp.int32, rows.shape, 2)
+    count = count[:, None, None]
+    first = first[:, None, None]
+    last = slot == slots - 1
+    unused = jnp.where(last, HEADER + first.astype(jnp.float32), UNUSED)
+    lifted = jnp.where(jnp.abs(rows) < TINY, TINY_MARK, rows * LIFT)
+    full = last & (count == slots)
+    lift = full & (((lane == 0) & (first > 0)) | ((lane == 1) & (first == slots)))
+    return jnp.where((slot >= count) & (lane == 0), unused, jnp.where(lift, lifted, rows))
+
+
+def code_of(head):
+    slots = head.shape[0]
+    slot = lax.broadcasted_iota(jnp.int32, head.shape, 0)
+    lane = lax.broadcasted_iota(jnp.int32, head.shape, 1)
+    size = jnp.abs(head)
+    valid = (size < LOW) | (size > HIGH)
+    last = slot == slots - 1
+    counts = jnp.where((lane == 0) & valid, 1.0, 0.0)
+    header = jnp.where(last & (lane == 0) & ~valid, head - HEADER, 0.0)
+    lifted = jnp.where(last & (lane <= 1) & (size > HIGH), slots / 2.0, 0.0)
+    return jnp.sum(counts + CODE * (header + lifted))
+
+
+def unmarked(rows):
+    size = jnp.abs(rows)
+    lowered = jnp.where(size < 2.0 * TINY_MARK, 0.0, rows * (1.0 / LIFT))
+    return jnp.where(size > HIGH, lowered, rows)
+
+
 def score_kernel(
-    code_ref,
     core_ref,
     gain_own,
     gain_other,
@@ -48,6 +87,7 @@
     score_ref,
     unit_ref,
     offset_ref,
+    code_ref,
     row_sem,
     chunk_sem,
     wo_sem,
@@ -56,12 +96,10 @@
     units, unit_rows, width = x_hbm.shape
     routers, _, share, _ = w_own.shape
     half_width = v_own.shape[2]
-    cores = width // half_width
     per_side = half_width // CHUNK
     chunks = width // CHUNK
     scale = HEAD_DIM ** (-0.5)
-    core = core_ref[0]
-    router_here = core_ref[1]
+    router_here = core_ref[0]
     lanes = score_ref.shape[1]
     unit_row = lax.broadcasted_iota(jnp.int32, (unit_rows, lanes), 0)
     sides = ((kt_own, v_own, w_own), (kt_other, v_other, w_other))
@@ -111,13 +149,10 @@
     for copy in tail_copies:
         copy.start()
 
-    def rows_here(count):
-        return (count + (cores - 1 - core)) // cores
-
     def place(unit, position):
         code = code_ref[unit]
-        count = rows_here(code % CODE)
-        first = rows_here(code // CODE)
+        count = code % CODE
+        first = code // CODE
 
         @pl.when(count > 0)
         def _():
@@ -129,6 +164,10 @@
         return position + (count + ALIGN - 1) // ALIGN * ALIGN
 
     row_copy.wait()
+    for unit in range(units):
+        head = x_ref[unit, :, 0:lanes].astype(jnp.float32)
+        code_ref[unit] = code_of(head).astype(jnp.int32)
+        x_ref[unit, :, 0:lanes] = unmarked(head).astype(jnp.bfloat16)
     total = lax.fori_loop(0, units, place, jnp.int32(0))
 
     def attend(user, queries, chunk, inner):
@@ -213,7 +252,7 @@
     lax.fori_loop(1, (total + TILE - 1) // TILE, later_tile, 0)
 
     def unplace(unit, carry):
-        count = rows_here(code_ref[unit] % CODE)
+        count = code_ref[unit] % CODE
         to = pl.multiple_of(unit * unit_rows, unit_rows)
 
         @pl.when(count > 0)
@@ -237,7 +276,7 @@
 VMEM_LIMIT = 40 * 1024 * 1024
 
 
-def score_units(codes, core, x, own, other, mlp_gain, w_one, w_two):
+def score_units(place_here, x, own, other, mlp_gain, w_one, w_two):
     units, unit_rows, width = x.shape
     kt, values, gain, w = own
     kt2, values2, gain2, w2 = other
@@ -254,7 +293,7 @@
     return pl.pallas_call(
         score_kernel,
         out_shape=jax.ShapeDtypeStruct((rows // lanes, lanes), jnp.float32),
-        in_specs=[smem] * 2 + [vmem] * 4 + [hbm] * 8,
+        in_specs=[smem] + [vmem] * 4 + [hbm] * 8,
         out_specs=vmem,
         scratch_shapes=[
             pltpu.VMEM(x.shape, jnp.bfloat16),
@@ -271,6 +310,7 @@
             pltpu.VMEM((room, lanes), jnp.float32),
             pltpu.VMEM((rows, lanes), jnp.float32),
             pltpu.SMEM((units,), jnp.int32),
+            pltpu.SMEM((units,), jnp.int32),
             pltpu.SemaphoreType.DMA((1,)),
             pltpu.SemaphoreType.DMA((chunks, routers + 2)),
             pltpu.SemaphoreType.DMA((cores, routers)),
@@ -279,7 +319,7 @@
         compiler_params=pltpu.CompilerParams(vmem_limit_bytes=VMEM_LIMIT),
         name="score_units",
         interpret=INTERPRET,
-    )(codes, core, gain, gain2, mlp_gain, w_two, x, kt, kt2, values, values2, w, w2, w_one)
+    )(place_here, gain, gain2, mlp_gain, w_two, x, kt, kt2, values, values2, w, w2, w_one)
 
 
 def local(
@@ -311,9 +351,10 @@
 
     target = block_owner[:, 0]
     goes = target[None, :] == lax.broadcasted_iota(jnp.int32, (peers, blocks), 0)
-    weight = jnp.where(block_user == 0, CODE + 1, 1) * block_fill
-    codes = jnp.sum(jnp.where(goes, weight[None, :], 0), axis=1)
-    codes = exchanged(codes.reshape(peers, 1)).reshape(peers)
+
+    def rows_here(chosen):
+        rows = jnp.sum(jnp.where(goes & chosen[None, :], block_fill[None, :], 0), axis=1)
+        return (rows + (cores - 1 - core)) // cores
 
     index = jnp.arange(blocks, dtype=jnp.int32)
     same = target[:, None] == target[None, :]
@@ -329,9 +370,10 @@
     slot = lax.broadcasted_iota(jnp.int32, (peers * block_width, 1), 0)
     sent = jnp.dot(
         (slot == goes_to).astype(jnp.bfloat16), flat_items, preferred_element_type=jnp.float32
-    ).astype(jnp.bfloat16)
+    ).reshape(peers, block_width, model_width)
+    sent = marked(sent, rows_here(block_user >= 0), rows_here(block_user == 0)).astype(jnp.bfloat16)
     sent, w_in = lax.optimization_barrier((sent, w_in))
-    arrived = exchanged(sent.reshape(peers, block_width, model_width))
+    arrived = exchanged(sent)
 
     matrices, share, _ = w_in.shape
     w_local = jnp.concatenate([w_in, w_o.reshape(matrices, share, share)], axis=2)
@@ -351,9 +393,9 @@
     w_ring = jnp.stack([ring[k] for k in range(routers)])
     own = (jnp.swapaxes(prefix_keys, 1, 2), prefix_values, attn_gain[None, :], w_ring)
     other = jax.tree.map(swapped, own)
-    core_index = jnp.stack([core, lax.axis_index("routers")]).astype(jnp.int32)
+    place_here = lax.axis_index("routers").astype(jnp.int32).reshape(1)
     scores = score_units(
-        codes, core_index, arrived, own, other, mlp_gain[None, :], w_one, w_two[None, :]
+        place_here, arrived, own, other, mlp_gain[None, :], w_one, w_two[None, :]
     ).reshape(peers, block_width)
     back = jnp.broadcast_to(scores[:, None, :], (peers, cores, block_width))
     returned = lax.all_to_all(

time: 235 us -> 220 us (0.936)
  blocking collectives: 25.5 us -> 0 us
  waiting for transfers between devices: 72.3 us -> 77.5 us
  starting transfers between devices: 100 us -> 105 us
    all_to_all x1 -> x0, blocking collectives: 25.5 us -> none  [exchanged(): return lax.all_to_all(x, 'users', split_axis=0, concat_axis=0, tiled=True)]
    all_to_all x1, starting transfers between devices: 4.83 us -> 13.5 us  [exchanged(): return lax.all_to_all(x, 'users', split_axis=0, concat_axis=0, tiled=True)]
    all_to_all x1, waiting for transfers between devices: 43.3 us -> 46.9 us  [exchanged(): return lax.all_to_all(x, 'users', split_axis=0, concat_axis=0, tiled=True)]
    all_to_all x1, starting transfers between devices: 21.9 us -> 18.3 us  [local(): lax.all_to_all(back.reshape(peers * cores, block_width), ('users', 'heads...]
  transfers between devices with their start and end apart: 14 -> 14, of which waited for: 7 -> 6; matrix products, arithmetic and copies ran while one was open for 5% -> 5% of each run, Pallas kernels for 0% -> 0%
where the time goes in v7:
time: 220 us; the launch traced here: 218 us
  starting transfers between devices  105 us (48%)
  waiting for transfers between devices  77.5 us (35%)
  local copies, waits for them, and re-layouts  12.7 us (6%)
  Pallas kernels  10.5 us (5%)
  other arithmetic  7.11 us (3%)
  matrix products  4.68 us (2%)
    ppermute x3, starting transfers between devices, local(): from_below = lax.ppermute(from_below, 'routers', up)  50.4 us
    all_to_all x1, waiting for transfers between devices, exchanged(): return lax.all_to_all(x, 'users', split_axis=0, concat_axis=0, tiled=True)  46.9 us
    all_to_all x1, starting transfers between devices, local(): lax.all_to_all(back.reshape(peers * cores, block_width), ('users', 'heads...  18.3 us
    ppermute x3, waiting for transfers between devices, local(): from_above = lax.ppermute(from_above, 'routers', down)  14.8 us
    all_to_all x1, starting transfers between devices, exchanged(): return lax.all_to_all(x, 'users', split_axis=0, concat_axis=0, tiled=True)  13.5 us
    all_to_all x1, waiting for transfers between devices, local(): lax.all_to_all(back.reshape(peers * cores, block_width), ('users', 'heads...  11.8 us
    pallas_call x1, Pallas kernels, score_units(): pl.pallas_call(score_kernel, out_shape=jax.ShapeDtypeStruct((rows // lane...  10.5 us
    unnamed x26, local copies, waits for them, and re-layouts  10.2 us
  transfers between devices with their start and end apart: 14, of which 6 were waited for; matrix products, arithmetic and copies ran while one was open for 5% of the time, Pallas kernels for 0%

profile of v7, /device:TPU:78, one launch (start us, length us, event | category | flops | bytes accessed | tf_op | source)
XLA Modules:
  0.0 218.2 jit_solution(7454822996659522593)
XLA Ops:
  0.0 0.8 broadcast_compare_fusion.3
  0.8 0.9 select_reduce_fusion.4
  1.8 0.7 multiply_bitcast_fusion
  2.5 0.7 iota_compare_fusion.4
  3.2 0.1 fusion.9
  3.3 0.1 add.135
  3.5 0.1 add.139
  3.5 0.1 lt.70
  3.7 4.7 %select_convert_fusion = bf16[16,64,1024]{2,1,0:T(8,128)(2,1)} fusion(bf16[16]{0:T(256)(128)(2,1)S(1)} %convert_add_fusion, s32[16]{0:T(128)S(1)} %get-tuple-element.13, pred[1024]{0:T(1024)(128)(4,1)S(1)} %get-tuple-element.22, pred[1024]{0:T(1024)(128)(4,1)S(1)} %get-tuple-element.23, pred[16]{0:T(512)(128)(4,1)S(1)} %broadcast_compare_fusion, ...), kind=kOutput, calls=%fused_computation | convolution fusion | flops 2163212288 | bytes 4204752 | tf_op jit(solution)/shard_map/dot_general | solution.py:371
  8.4 3.2 %collective-permute-start.3 = (bf16[4,128,640]{2,1,0:T(8,128)(2,1)S(1)}, bf16[4,128,640]{2,1,0:T(8,128)(2,1)}, u32[]{:S(2)}, u32[]{:S(2)}) collective-permute-start(bf16[4,128,640]{2,1,0:T(8,128)(2,1)S(1)} %pad_maximum_fusion), channel_id=1, source_target_pairs={{0,14},{2,0},{4,2},{6,4},{8,6},{10,8},{12,10},{14,12},{1,15},{3,1}... | collective-permute-start | bytes 1966088 | tf_op jit(solution)/shard_map/ppermute | solution.py:386
  11.7 40.1 %collective-permute-start.6 = (bf16[4,128,640]{2,1,0:T(8,128)(2,1)S(1)}, bf16[4,128,640]{2,1,0:T(8,128)(2,1)S(1)}, u32[]{:S(2)}, u32[]{:S(2)}) collective-permute-start(bf16[4,128,640]{2,1,0:T(8,128)(2,1)S(1)} %pad_maximum_fusion), channel_id=1, source_target_pairs={{0,2},{2,4},{4,6},{6,8},{8,10},{10,12},{12,14},{14,0},{1,3},{3,5},... | collective-permute-start | bytes 1966088 | tf_op jit(solution)/shard_map/ppermute | solution.py:385
  51.7 6.7 %collective-permute-done.3 = bf16[4,128,640]{2,1,0:T(8,128)(2,1)} collective-permute-done((bf16[4,128,640]{2,1,0:T(8,128)(2,1)S(1)}, bf16[4,128,640]{2,1,0:T(8,128)(2,1)}, u32[]{:S(2)}, u32[]{:S(2)}) %collective-permute-start.3) | collective-permute-done | bytes 655392 | tf_op jit(solution)/shard_map/ppermute | solution.py:386
  58.4 1.9 collective-permute-start.4
  60.4 5.2 %collective-permute-start.7 = (bf16[4,128,640]{2,1,0:T(8,128)(2,1)S(1)}, bf16[4,128,640]{2,1,0:T(8,128)(2,1)}, u32[]{:S(2)}, u32[]{:S(2)}) collective-permute-start(bf16[4,128,640]{2,1,0:T(8,128)(2,1)S(1)} %collective-permute-done.6), channel_id=1, source_target_pairs={{0,2},{2,4},{4,6},{6,8},{8,10},{10,12},{12,14},{14,0},{1,3},{3,5},... | collective-permute-start | bytes 1966088 | tf_op jit(solution)/shard_map/ppermute | solution.py:385
  65.6 13.5 %all-to-all-start = ((bf16[16,64,1024]{2,1,0:T(8,128)(2,1)}), bf16[16,64,1024]{2,1,0:T(8,128)(2,1)}, u32[]{:S(2)}, u32[]{:S(2)}) async-start(bf16[16,64,1024]{2,1,0:T(8,128)(2,1)} %select_convert_fusion), calls=%async_computation | async-start | bytes 4194304 | tf_op jit(solution)/shard_map/all_to_all | solution.py:350
  79.0 2.0 collective-permute-start.5
  81.0 5.2 %collective-permute-start.8 = (bf16[4,128,640]{2,1,0:T(8,128)(2,1)}, bf16[4,128,640]{2,1,0:T(8,128)(2,1)S(1)}, u32[]{:S(2)}, u32[]{:S(2)}) collective-permute-start(bf16[4,128,640]{2,1,0:T(8,128)(2,1)} %collective-permute-done.7), channel_id=1, source_target_pairs={{0,2},{2,4},{4,6},{6,8},{8,10},{10,12},{12,14},{14,0},{1,3},{3,5},... | collective-permute-start | bytes 1966088 | tf_op jit(solution)/shard_map/ppermute | solution.py:385
  86.2 0.9 bitcast_dynamic-update-slice_fusion.6
  87.1 2.0 bitcast_dynamic-update-slice_fusion.5
  89.1 8.1 %collective-permute-done.5 = bf16[4,128,640]{2,1,0:T(8,128)(2,1)S(1)} collective-permute-done((bf16[4,128,640]{2,1,0:T(8,128)(2,1)}, bf16[4,128,640]{2,1,0:T(8,128)(2,1)S(1)}, u32[]{:S(2)}, u32[]{:S(2)}) %collective-permute-start.5) | collective-permute-done | bytes 655392 | tf_op jit(solution)/shard_map/ppermute | solution.py:386
  97.3 2.0 collective-permute-start.10
  99.3 5.3 %collective-permute-start.9 = (bf16[2,128,640]{2,1,0:T(8,128)(2,1)S(1)}, bf16[2,128,640]{2,1,0:T(8,128)(2,1)S(1)}, u32[]{:S(2)}, u32[]{:S(2)}) collective-permute-start(bf16[2,128,640]{2,1,0:T(8,128)(2,1)S(1)} %slice.8), channel_id=1, source_target_pairs={{0,2},{2,4},{4,6},{6,8},{8,10},{10,12},{12,14},{14,0},{1,3},{3,5},... | collective-permute-start | bytes 983048 | tf_op jit(solution)/shard_map/ppermute | solution.py:390
  104.6 2.0 bitcast_dynamic-update-slice_fusion.4
  106.6 0.9 bitcast_dynamic-update-slice_fusion.3
  107.5 1.7 collective-permute-done.9
  109.2 1.0 fusion.7
  110.2 1.0 bitcast_dynamic-update-slice_fusion.2
  111.1 2.0 bitcast_dynamic-update-slice_fusion.1
  113.1 0.9 bitcast_dynamic-update-slice_fusion.w_own
  114.0 1.9 collective-permute-start.11
  116.0 1.2 copy.15
  117.2 2.4 %collective-permute-start.1 = (bf16[2,512,256]{2,1,0:T(8,128)(2,1)S(1)}, bf16[2,512,256]{2,1,0:T(8,128)(2,1)}, u32[]{:S(2)}, u32[]{:S(2)}) collective-permute-start(bf16[2,512,256]{2,1,0:T(8,128)(2,1)S(1)} %bitcast.30), channel_id=1, source_target_pairs={{0,1},{1,0},{2,3},{3,2},{4,5},{5,4},{6,7},{7,6},{8,9},{9,8},{10,11... | collective-permute-start | bytes 1572872 | tf_op jit(solution)/shard_map/ppermute | solution.py:347
  119.7 2.0 collective-permute-start.2
  121.6 2.4 %collective-permute-start = (bf16[1,512]{1,0:T(2,128)(2,1)S(1)}, bf16[1,512]{1,0:T(2,128)(2,1)S(1)}, u32[]{:S(2)}, u32[]{:S(2)}) collective-permute-start(bf16[1,512]{1,0:T(2,128)(2,1)S(1)} %broadcast_in_dim.113.gain_own), channel_id=1, source_target_pairs={{0,1},{1,0},{2,3},{3,2},{4,5},{5,4},{6,7},{7,6},{8,9},{9,8},{10,11... | collective-permute-start | bytes 3080 | tf_op jit(solution)/shard_map/ppermute | solution.py:347
  124.1 2.3 %collective-permute-done.gain_other = bf16[1,512]{1,0:T(2,128)(2,1)S(1)} collective-permute-done((bf16[1,512]{1,0:T(2,128)(2,1)S(1)}, bf16[1,512]{1,0:T(2,128)(2,1)S(1)}, u32[]{:S(2)}, u32[]{:S(2)}) %collective-permute-start) | collective-permute-done | bytes 1056 | tf_op jit(solution)/shard_map/ppermute | solution.py:347
  126.4 46.9 %all-to-all-done.x_hbm = bf16[16,64,1024]{2,1,0:T(8,128)(2,1)} async-done(((bf16[16,64,1024]{2,1,0:T(8,128)(2,1)}), bf16[16,64,1024]{2,1,0:T(8,128)(2,1)}, u32[]{:S(2)}, u32[]{:S(2)}) %all-to-all-start) | async-done | bytes 2097184 | tf_op jit(solution)/shard_map/all_to_all | solution.py:350
  173.3 1.0 copy-done.2
  174.4 10.5 %score_units.1 = f32[8,128]{1,0:T(8,128)S(1)} custom-call(s32[1]{0:T(128)} %bitcast.1.core_ref, bf16[1,512]{1,0:T(2,128)(2,1)S(1)} %broadcast_in_dim.113.gain_own, bf16[1,512]{1,0:T(2,128)(2,1)S(1)} %collective-permute-done.gain_other, bf16[1,1024]{1,0:T(2,128)(2,1)S(1)} %broadcast_in_dim.114.mlp_gain_ref, bf16[1,256]{1,0:T(2,128)(2,1)S(1)} %broadcast_in_dim.115.w_two_ref, ...), custom_call_target="tpu_custom_call" | custom-call | tf_op jit(solution)/shard_map/score_units/pallas_call | solution.py:293
  184.9 0.1 broadcast_in_dim.119
  185.0 0.6 broadcast_in_dim.120
  185.6 18.3 %all-to-all-start.1 = ((f32[32,1,64]{2,1,0:T(1,128)}), f32[32,1,64]{2,1,0:T(1,128)S(1)}, u32[]{:S(2)}, u32[]{:S(2)}) async-start(f32[32,1,64]{2,1,0:T(1,128)} %bitcast.15), calls=%async_computation.1 | async-start | bytes 32768 | tf_op jit(solution)/shard_map/all_to_all | solution.py:401
  203.9 11.8 %all-to-all-done.1 = f32[32,1,64]{2,1,0:T(1,128)S(1)} async-done(((f32[32,1,64]{2,1,0:T(1,128)}), f32[32,1,64]{2,1,0:T(1,128)S(1)}, u32[]{:S(2)}, u32[]{:S(2)}) %all-to-all-start.1) | async-done | bytes 8224 | tf_op jit(solution)/shard_map/all_to_all | solution.py:401
  215.7 0.5 broadcast.386
  216.2 0.7 reduce.3
  216.9 0.1 broadcast_in_dim.121
  217.0 0.1 select_reduce_fusion.1
  217.1 0.4 select_reduce_fusion
  217.5 0.7 broadcast_select_fusion
  (42 shorter events, 0.3 us)
Async XLA Ops:
  0.0 3.6 %copy-start = (bf16[16,64,1024]{2,1,0:T(8,128)(2,1)S(1)}, bf16[16,64,1024]{2,1,0:T(8,128)(2,1)}, u32[]{:S(2)}) copy-start(bf16[16,64,1024]{2,1,0:T(8,128)(2,1)} %param.12) | copy-start | bytes 6291460
  3.6 4.7 %copy-start.3 = (bf16[4,128,512]{2,1,0:T(8,128)(2,1)S(1)}, bf16[4,128,512]{2,1,0:T(8,128)(2,1)}, u32[]{:S(2)}) copy-start(bf16[4,128,512]{2,1,0:T(8,128)(2,1)} %param.18) | copy-start | bytes 1572868
  3.7 4.7 %copy-start.4 = (bf16[512,128]{1,0:T(8,128)(2,1)S(1)}, bf16[512,128]{1,0:T(8,128)(2,1)}, u32[]{:S(2)}) copy-start(bf16[512,128]{1,0:T(8,128)(2,1)} %param.20) | copy-start | bytes 393220
  8.4 50.0 %collective-permute-start.3 = (bf16[4,128,640]{2,1,0:T(8,128)(2,1)S(1)}, bf16[4,128,640]{2,1,0:T(8,128)(2,1)}, u32[]{:S(2)}, u32[]{:S(2)}) collective-permute-start(bf16[4,128,640]{2,1,0:T(8,128)(2,1)S(1)} %pad_maximum_fusion), channel_id=1, source_target_pairs={{0,14},{2,0},{4,2},{6,4},{8,6},{10,8},{12,10},{14,12},{1,15},{3,1}... | collective-permute-start | bytes 1966088 | tf_op jit(solution)/shard_map/ppermute | solution.py:386
  11.7 48.7 %collective-permute-start.6 = (bf16[4,128,640]{2,1,0:T(8,128)(2,1)S(1)}, bf16[4,128,640]{2,1,0:T(8,128)(2,1)S(1)}, u32[]{:S(2)}, u32[]{:S(2)}) collective-permute-start(bf16[4,128,640]{2,1,0:T(8,128)(2,1)S(1)} %pad_maximum_fusion), channel_id=1, source_target_pairs={{0,2},{2,4},{4,6},{6,8},{8,10},{10,12},{12,14},{14,0},{1,3},{3,5},... | collective-permute-start | bytes 1966088 | tf_op jit(solution)/shard_map/ppermute | solution.py:385
  58.4 20.6 %collective-permute-start.4 = (bf16[4,128,640]{2,1,0:T(8,128)(2,1)}, bf16[4,128,640]{2,1,0:T(8,128)(2,1)}, u32[]{:S(2)}, u32[]{:S(2)}) collective-permute-start(bf16[4,128,640]{2,1,0:T(8,128)(2,1)} %collective-permute-done.3), channel_id=1, source_target_pairs={{0,14},{2,0},{4,2},{6,4},{8,6},{10,8},{12,10},{14,12},{1,15},{3,1}... | collective-permute-start | bytes 1966088 | tf_op jit(solution)/shard_map/ppermute | solution.py:386
  60.4 20.6 %collective-permute-start.7 = (bf16[4,128,640]{2,1,0:T(8,128)(2,1)S(1)}, bf16[4,128,640]{2,1,0:T(8,128)(2,1)}, u32[]{:S(2)}, u32[]{:S(2)}) collective-permute-start(bf16[4,128,640]{2,1,0:T(8,128)(2,1)S(1)} %collective-permute-done.6), channel_id=1, source_target_pairs={{0,2},{2,4},{4,6},{6,8},{8,10},{10,12},{12,14},{14,0},{1,3},{3,5},... | collective-permute-start | bytes 1966088 | tf_op jit(solution)/shard_map/ppermute | solution.py:385
  65.6 107.8 %all-to-all-start = ((bf16[16,64,1024]{2,1,0:T(8,128)(2,1)}), bf16[16,64,1024]{2,1,0:T(8,128)(2,1)}, u32[]{:S(2)}, u32[]{:S(2)}) async-start(bf16[16,64,1024]{2,1,0:T(8,128)(2,1)} %select_convert_fusion), calls=%async_computation | async-start | bytes 4194304 | tf_op jit(solution)/shard_map/all_to_all | solution.py:350
  79.0 18.2 %collective-permute-start.5 = (bf16[4,128,640]{2,1,0:T(8,128)(2,1)}, bf16[4,128,640]{2,1,0:T(8,128)(2,1)S(1)}, u32[]{:S(2)}, u32[]{:S(2)}) collective-permute-start(bf16[4,128,640]{2,1,0:T(8,128)(2,1)} %collective-permute-done.4), channel_id=1, source_target_pairs={{0,14},{2,0},{4,2},{6,4},{8,6},{10,8},{12,10},{14,12},{1,15},{3,1}... | collective-permute-start | bytes 1966088 | tf_op jit(solution)/shard_map/ppermute | solution.py:386
  81.0 18.2 %collective-permute-start.8 = (bf16[4,128,640]{2,1,0:T(8,128)(2,1)}, bf16[4,128,640]{2,1,0:T(8,128)(2,1)S(1)}, u32[]{:S(2)}, u32[]{:S(2)}) collective-permute-start(bf16[4,128,640]{2,1,0:T(8,128)(2,1)} %collective-permute-done.7), channel_id=1, source_target_pairs={{0,2},{2,4},{4,6},{6,8},{8,10},{10,12},{12,14},{14,0},{1,3},{3,5},... | collective-permute-start | bytes 1966088 | tf_op jit(solution)/shard_map/ppermute | solution.py:385
  97.3 10.2 %collective-permute-start.10 = (bf16[2,128,640]{2,1,0:T(8,128)(2,1)S(1)}, bf16[2,128,640]{2,1,0:T(8,128)(2,1)S(1)}, u32[]{:S(2)}, u32[]{:S(2)}) collective-permute-start(bf16[2,128,640]{2,1,0:T(8,128)(2,1)S(1)} %slice.9), channel_id=1, source_target_pairs={{0,14},{2,0},{4,2},{6,4},{8,6},{10,8},{12,10},{14,12},{1,15},{3,1}... | collective-permute-start | bytes 983048 | tf_op jit(solution)/shard_map/ppermute | solution.py:391
  99.3 20.4 %copy-start.1 = (bf16[2,256,512]{2,1,0:T(8,128)(2,1)S(1)}, bf16[2,256,512]{2,1,0:T(8,128)(2,1)}, u32[]{:S(2)}) copy-start(bf16[2,256,512]{2,1,0:T(8,128)(2,1)} %v_own.1) | copy-start | bytes 1572868
  99.3 22.3 %copy-start.8 = (bf16[512]{0:T(512)(128)(2,1)S(1)}, bf16[512]{0:T(512)(128)(2,1)}, u32[]{:S(2)}) copy-start(bf16[512]{0:T(512)(128)(2,1)} %param.19) | copy-start | bytes 3076
  99.3 24.8 %copy-start.7 = (bf16[1024]{0:T(1024)(128)(2,1)S(1)}, bf16[1024]{0:T(1024)(128)(2,1)}, u32[]{:S(2)}) copy-start(bf16[1024]{0:T(1024)(128)(2,1)} %param.21) | copy-start | bytes 6148
  99.3 24.8 %copy-start.9 = (bf16[256]{0:T(256)(128)(2,1)S(1)}, bf16[256]{0:T(256)(128)(2,1)}, u32[]{:S(2)}) copy-start(bf16[256]{0:T(256)(128)(2,1)} %param.23) | copy-start | bytes 1540
  99.3 9.9 %collective-permute-start.9 = (bf16[2,128,640]{2,1,0:T(8,128)(2,1)S(1)}, bf16[2,128,640]{2,1,0:T(8,128)(2,1)S(1)}, u32[]{:S(2)}, u32[]{:S(2)}) collective-permute-start(bf16[2,128,640]{2,1,0:T(8,128)(2,1)S(1)} %slice.8), channel_id=1, source_target_pairs={{0,2},{2,4},{4,6},{6,8},{8,10},{10,12},{12,14},{14,0},{1,3},{3,5},... | collective-permute-start | bytes 983048 | tf_op jit(solution)/shard_map/ppermute | solution.py:390
  114.0 12.4 %collective-permute-start.11 = (bf16[8,4,128,640]{3,2,1,0:T(8,128)(2,1)}, bf16[8,4,128,640]{3,2,1,0:T(8,128)(2,1)}, u32[]{:S(2)}, u32[]{:S(2)}) collective-permute-start(bf16[8,4,128,640]{3,2,1,0:T(8,128)(2,1)} %bitcast_dynamic-update-slice_fusion.w_own), channel_id=1, source_target_pairs={{0,1},{1,0},{2,3},{3,2},{4,5},{5,4},{6,7},{7,6},{8,9},{9,8},{10,11... | collective-permute-start | bytes 15728648 | tf_op jit(solution)/shard_map/ppermute | solution.py:347
  117.2 9.2 %collective-permute-start.1 = (bf16[2,512,256]{2,1,0:T(8,128)(2,1)S(1)}, bf16[2,512,256]{2,1,0:T(8,128)(2,1)}, u32[]{:S(2)}, u32[]{:S(2)}) collective-permute-start(bf16[2,512,256]{2,1,0:T(8,128)(2,1)S(1)} %bitcast.30), channel_id=1, source_target_pairs={{0,1},{1,0},{2,3},{3,2},{4,5},{5,4},{6,7},{7,6},{8,9},{9,8},{10,11... | collective-permute-start | bytes 1572872 | tf_op jit(solution)/shard_map/ppermute | solution.py:347
  119.7 6.8 %collective-permute-start.2 = (bf16[2,256,512]{2,1,0:T(8,128)(2,1)S(1)}, bf16[2,256,512]{2,1,0:T(8,128)(2,1)}, u32[]{:S(2)}, u32[]{:S(2)}) collective-permute-start(bf16[2,256,512]{2,1,0:T(8,128)(2,1)S(1)} %copy-done.1), channel_id=1, source_target_pairs={{0,1},{1,0},{2,3},{3,2},{4,5},{5,4},{6,7},{7,6},{8,9},{9,8},{10,11... | collective-permute-start | bytes 1572872 | tf_op jit(solution)/shard_map/ppermute | solution.py:347
  121.6 4.8 %collective-permute-start = (bf16[1,512]{1,0:T(2,128)(2,1)S(1)}, bf16[1,512]{1,0:T(2,128)(2,1)S(1)}, u32[]{:S(2)}, u32[]{:S(2)}) collective-permute-start(bf16[1,512]{1,0:T(2,128)(2,1)S(1)} %broadcast_in_dim.113.gain_own), channel_id=1, source_target_pairs={{0,1},{1,0},{2,3},{3,2},{4,5},{5,4},{6,7},{7,6},{8,9},{9,8},{10,11... | collective-permute-start | bytes 3080 | tf_op jit(solution)/shard_map/ppermute | solution.py:347
  173.3 1.0 copy-start.2
  174.4 29.5 %copy-start.5 = (s32[16,1]{0,1:T(1,128)S(1)}, s32[16,1]{0,1:T(1,128)}, u32[]{:S(2)}) copy-start(s32[16,1]{0,1:T(1,128)} %param.13) | copy-start | bytes 196
  174.4 43.1 %copy-start.6 = (s32[16]{0:T(128)S(1)}, s32[16]{0:T(128)}, u32[]{:S(2)}) copy-start(s32[16]{0:T(128)} %param.15) | copy-start | bytes 196
  185.6 30.1 %all-to-all-start.1 = ((f32[32,1,64]{2,1,0:T(1,128)}), f32[32,1,64]{2,1,0:T(1,128)S(1)}, u32[]{:S(2)}, u32[]{:S(2)}) async-start(f32[32,1,64]{2,1,0:T(1,128)} %bitcast.15), calls=%async_computation.1 | async-start | bytes 32768 | tf_op jit(solution)/shard_map/all_to_all | solution.py:401

commit v8 on v7

--- a/solution.py
+++ b/solution.py
@@ -268,8 +268,15 @@
         return carry
 
     lax.fori_loop(0, units, unplace, 0)
+    square = (lanes, lanes)
+    diagonal = lax.broadcasted_iota(jnp.int32, square, 0) == lax.broadcasted_iota(
+        jnp.int32, square, 1
+    )
     for block in range(units * unit_rows // lanes):
-        out_ref[block : block + 1, :] = unit_ref[block * lanes : (block + 1) * lanes, :].T[0:1, :]
+        rows = unit_ref[block * lanes : (block + 1) * lanes, :]
+        out_ref[block : block + 1, :] = jnp.sum(
+            jnp.where(diagonal, rows, 0.0), axis=0, keepdims=True
+        )
 
 
 INTERPRET = False
@@ -406,12 +413,13 @@
         tiled=True,
     ).reshape(peers, cores * block_width)
     row_scores = jnp.sum(jnp.where(goes[:, :, None], returned[:, None, :], 0.0), axis=0)
-    lane = packed % cores * block_width + packed // cores
+    lane = jnp.where(
+        inside < block_fill[:, None], packed % cores * block_width + packed // cores, -1
+    )
     wanted = lane[:, :, None] == lax.broadcasted_iota(
         jnp.int32, (blocks, block_width, cores * block_width), 2
     )
-    block_scores = jnp.sum(jnp.where(wanted, row_scores[:, None, :], 0.0), axis=2)
-    return jnp.where(inside < block_fill[:, None], block_scores, jnp.zeros_like(block_scores))
+    return jnp.sum(jnp.where(wanted, row_scores[:, None, :], 0.0), axis=2)
 
 
 def solution(mesh):

time: 220 us -> 221 us (level)
    unnamed x26 -> x24, local copies, waits for them, and re-layouts: 10.2 us -> 10.2 us
where the time goes in v8:
time: 221 us; the launch traced here: 219 us
  starting transfers between devices  105 us (48%)
  waiting for transfers between devices  77.5 us (35%)
  local copies, waits for them, and re-layouts  12.7 us (6%)
  Pallas kernels  10.4 us (5%)
  other arithmetic  7.68 us (3%)
  matrix products  4.66 us (2%)
    ppermute x3, starting transfers between devices, local(): from_below = lax.ppermute(from_below, 'routers', up)  50.4 us
    all_to_all x1, waiting for transfers between devices, exchanged(): return lax.all_to_all(x, 'users', split_axis=0, concat_axis=0, tiled=True)  47 us
    all_to_all x1, starting transfers between devices, local(): lax.all_to_all(back.reshape(peers * cores, block_width), ('users', 'heads...  18.3 us
    ppermute x3, waiting for transfers between devices, local(): from_above = lax.ppermute(from_above, 'routers', down)  14.8 us
    all_to_all x1, starting transfers between devices, exchanged(): return lax.all_to_all(x, 'users', split_axis=0, concat_axis=0, tiled=True)  13.5 us
    all_to_all x1, waiting for transfers between devices, local(): lax.all_to_all(back.reshape(peers * cores, block_width), ('users', 'heads...  11.8 us
    pallas_call x1, Pallas kernels, score_units(): pl.pallas_call(score_kernel, out_shape=jax.ShapeDtypeStruct((rows // lane...  10.4 us
    unnamed x24, local copies, waits for them, and re-layouts  10.2 us
  transfers between devices with their start and end apart: 14, of which 6 were waited for; matrix products, arithmetic and copies ran while one was open for 5% of the time, Pallas kernels for 0%

profile of v8, /device:TPU:78, one launch (start us, length us, event | category | flops | bytes accessed | tf_op | source)
XLA Modules:
  0.0 218.6 jit_solution(13188102873851019831)
XLA Ops:
  0.0 0.8 broadcast_compare_fusion.3
  0.8 0.9 select_reduce_fusion.4
  1.8 0.7 multiply_bitcast_fusion
  2.5 0.7 iota_compare_fusion.4
  3.2 0.7 fusion.10
  4.0 0.1 add.135
  4.0 0.1 add.138
  4.1 0.1 add.139
  4.2 0.1 lt.74
  4.3 4.7 %select_convert_fusion = bf16[16,64,1024]{2,1,0:T(8,128)(2,1)} fusion(bf16[16]{0:T(256)(128)(2,1)S(1)} %convert_add_fusion, s32[16]{0:T(128)S(1)} %get-tuple-element.13, pred[1024]{0:T(1024)(128)(4,1)S(1)} %get-tuple-element.22, pred[1024]{0:T(1024)(128)(4,1)S(1)} %get-tuple-element.23, pred[16]{0:T(512)(128)(4,1)S(1)} %broadcast_compare_fusion, ...), kind=kOutput, calls=%fused_computation | convolution fusion | flops 2163212288 | bytes 4204752 | tf_op jit(solution)/shard_map/dot_general | solution.py:378
  9.1 3.2 %collective-permute-start.3 = (bf16[4,128,640]{2,1,0:T(8,128)(2,1)S(1)}, bf16[4,128,640]{2,1,0:T(8,128)(2,1)}, u32[]{:S(2)}, u32[]{:S(2)}) collective-permute-start(bf16[4,128,640]{2,1,0:T(8,128)(2,1)S(1)} %pad_maximum_fusion), channel_id=1, source_target_pairs={{0,14},{2,0},{4,2},{6,4},{8,6},{10,8},{12,10},{14,12},{1,15},{3,1}... | collective-permute-start | bytes 1966088 | tf_op jit(solution)/shard_map/ppermute | solution.py:393
  12.3 40.1 %collective-permute-start.6 = (bf16[4,128,640]{2,1,0:T(8,128)(2,1)S(1)}, bf16[4,128,640]{2,1,0:T(8,128)(2,1)S(1)}, u32[]{:S(2)}, u32[]{:S(2)}) collective-permute-start(bf16[4,128,640]{2,1,0:T(8,128)(2,1)S(1)} %pad_maximum_fusion), channel_id=1, source_target_pairs={{0,2},{2,4},{4,6},{6,8},{8,10},{10,12},{12,14},{14,0},{1,3},{3,5},... | collective-permute-start | bytes 1966088 | tf_op jit(solution)/shard_map/ppermute | solution.py:392
  52.4 6.7 %collective-permute-done.3 = bf16[4,128,640]{2,1,0:T(8,128)(2,1)} collective-permute-done((bf16[4,128,640]{2,1,0:T(8,128)(2,1)S(1)}, bf16[4,128,640]{2,1,0:T(8,128)(2,1)}, u32[]{:S(2)}, u32[]{:S(2)}) %collective-permute-start.3) | collective-permute-done | bytes 655392 | tf_op jit(solution)/shard_map/ppermute | solution.py:393
  59.1 1.9 collective-permute-start.4
  61.0 5.2 %collective-permute-start.7 = (bf16[4,128,640]{2,1,0:T(8,128)(2,1)S(1)}, bf16[4,128,640]{2,1,0:T(8,128)(2,1)}, u32[]{:S(2)}, u32[]{:S(2)}) collective-permute-start(bf16[4,128,640]{2,1,0:T(8,128)(2,1)S(1)} %collective-permute-done.6), channel_id=1, source_target_pairs={{0,2},{2,4},{4,6},{6,8},{8,10},{10,12},{12,14},{14,0},{1,3},{3,5},... | collective-permute-start | bytes 1966088 | tf_op jit(solution)/shard_map/ppermute | solution.py:392
  66.2 13.5 %all-to-all-start = ((bf16[16,64,1024]{2,1,0:T(8,128)(2,1)}), bf16[16,64,1024]{2,1,0:T(8,128)(2,1)}, u32[]{:S(2)}, u32[]{:S(2)}) async-start(bf16[16,64,1024]{2,1,0:T(8,128)(2,1)} %select_convert_fusion), calls=%async_computation | async-start | bytes 4194304 | tf_op jit(solution)/shard_map/all_to_all | solution.py:357
  79.7 2.0 collective-permute-start.5
  81.7 5.2 %collective-permute-start.8 = (bf16[4,128,640]{2,1,0:T(8,128)(2,1)}, bf16[4,128,640]{2,1,0:T(8,128)(2,1)S(1)}, u32[]{:S(2)}, u32[]{:S(2)}) collective-permute-start(bf16[4,128,640]{2,1,0:T(8,128)(2,1)} %collective-permute-done.7), channel_id=1, source_target_pairs={{0,2},{2,4},{4,6},{6,8},{8,10},{10,12},{12,14},{14,0},{1,3},{3,5},... | collective-permute-start | bytes 1966088 | tf_op jit(solution)/shard_map/ppermute | solution.py:392
  86.8 0.9 bitcast_dynamic-update-slice_fusion.6
  87.8 2.0 bitcast_dynamic-update-slice_fusion.5
  89.8 8.1 %collective-permute-done.5 = bf16[4,128,640]{2,1,0:T(8,128)(2,1)S(1)} collective-permute-done((bf16[4,128,640]{2,1,0:T(8,128)(2,1)}, bf16[4,128,640]{2,1,0:T(8,128)(2,1)S(1)}, u32[]{:S(2)}, u32[]{:S(2)}) %collective-permute-start.5) | collective-permute-done | bytes 655392 | tf_op jit(solution)/shard_map/ppermute | solution.py:393
  97.9 2.0 collective-permute-start.10
  100.0 5.3 %collective-permute-start.9 = (bf16[2,128,640]{2,1,0:T(8,128)(2,1)S(1)}, bf16[2,128,640]{2,1,0:T(8,128)(2,1)S(1)}, u32[]{:S(2)}, u32[]{:S(2)}) collective-permute-start(bf16[2,128,640]{2,1,0:T(8,128)(2,1)S(1)} %slice.8), channel_id=1, source_target_pairs={{0,2},{2,4},{4,6},{6,8},{8,10},{10,12},{12,14},{14,0},{1,3},{3,5},... | collective-permute-start | bytes 983048 | tf_op jit(solution)/shard_map/ppermute | solution.py:397
  105.3 2.0 bitcast_dynamic-update-slice_fusion.4
  107.3 0.9 bitcast_dynamic-update-slice_fusion.3
  108.2 1.7 collective-permute-done.9
  109.8 1.0 fusion.7
  110.8 1.0 bitcast_dynamic-update-slice_fusion.2
  111.8 2.0 bitcast_dynamic-update-slice_fusion.1
  113.7 0.9 bitcast_dynamic-update-slice_fusion.w_own
  114.6 1.9 collective-permute-start.11
  116.6 1.2 copy.15
  117.8 2.4 %collective-permute-start.1 = (bf16[2,512,256]{2,1,0:T(8,128)(2,1)S(1)}, bf16[2,512,256]{2,1,0:T(8,128)(2,1)}, u32[]{:S(2)}, u32[]{:S(2)}) collective-permute-start(bf16[2,512,256]{2,1,0:T(8,128)(2,1)S(1)} %bitcast.30), channel_id=1, source_target_pairs={{0,1},{1,0},{2,3},{3,2},{4,5},{5,4},{6,7},{7,6},{8,9},{9,8},{10,11... | collective-permute-start | bytes 1572872 | tf_op jit(solution)/shard_map/ppermute | solution.py:354
  120.3 2.0 collective-permute-start.2
  122.3 2.4 %collective-permute-start = (bf16[1,512]{1,0:T(2,128)(2,1)S(1)}, bf16[1,512]{1,0:T(2,128)(2,1)S(1)}, u32[]{:S(2)}, u32[]{:S(2)}) collective-permute-start(bf16[1,512]{1,0:T(2,128)(2,1)S(1)} %broadcast_in_dim.111.gain_own), channel_id=1, source_target_pairs={{0,1},{1,0},{2,3},{3,2},{4,5},{5,4},{6,7},{7,6},{8,9},{9,8},{10,11... | collective-permute-start | bytes 3080 | tf_op jit(solution)/shard_map/ppermute | solution.py:354
  124.8 2.3 %collective-permute-done.gain_other = bf16[1,512]{1,0:T(2,128)(2,1)S(1)} collective-permute-done((bf16[1,512]{1,0:T(2,128)(2,1)S(1)}, bf16[1,512]{1,0:T(2,128)(2,1)S(1)}, u32[]{:S(2)}, u32[]{:S(2)}) %collective-permute-start) | collective-permute-done | bytes 1056 | tf_op jit(solution)/shard_map/ppermute | solution.py:354
  127.1 47.0 %all-to-all-done.x_hbm = bf16[16,64,1024]{2,1,0:T(8,128)(2,1)} async-done(((bf16[16,64,1024]{2,1,0:T(8,128)(2,1)}), bf16[16,64,1024]{2,1,0:T(8,128)(2,1)}, u32[]{:S(2)}, u32[]{:S(2)}) %all-to-all-start) | async-done | bytes 2097184 | tf_op jit(solution)/shard_map/all_to_all | solution.py:357
  174.0 1.0 copy-done.2
  175.1 10.4 %score_units.1 = f32[8,128]{1,0:T(8,128)S(1)} custom-call(s32[1]{0:T(128)} %bitcast.1.core_ref, bf16[1,512]{1,0:T(2,128)(2,1)S(1)} %broadcast_in_dim.111.gain_own, bf16[1,512]{1,0:T(2,128)(2,1)S(1)} %collective-permute-done.gain_other, bf16[1,1024]{1,0:T(2,128)(2,1)S(1)} %broadcast_in_dim.112.mlp_gain_ref, bf16[1,256]{1,0:T(2,128)(2,1)S(1)} %broadcast_in_dim.113.w_two_ref, ...), custom_call_target="tpu_custom_call" | custom-call | tf_op jit(solution)/shard_map/score_units/pallas_call | solution.py:300
  185.4 0.1 broadcast_in_dim.117
  185.5 0.6 broadcast_in_dim.118
  186.1 18.3 %all-to-all-start.1 = ((f32[32,1,64]{2,1,0:T(1,128)}), f32[32,1,64]{2,1,0:T(1,128)S(1)}, u32[]{:S(2)}, u32[]{:S(2)}) async-start(f32[32,1,64]{2,1,0:T(1,128)} %bitcast.15), calls=%async_computation.1 | async-start | bytes 32768 | tf_op jit(solution)/shard_map/all_to_all | solution.py:408
  204.4 11.8 %all-to-all-done.1 = f32[32,1,64]{2,1,0:T(1,128)S(1)} async-done(((f32[32,1,64]{2,1,0:T(1,128)}), f32[32,1,64]{2,1,0:T(1,128)S(1)}, u32[]{:S(2)}, u32[]{:S(2)}) %all-to-all-start.1) | async-done | bytes 8224 | tf_op jit(solution)/shard_map/all_to_all | solution.py:408
  216.2 0.5 broadcast.401
  216.7 0.7 reduce.3
  217.4 0.1 broadcast_in_dim.119
  217.5 0.1 select_reduce_fusion.1
  217.6 1.0 select_reduce_fusion
  (39 shorter events, 0.3 us)
Async XLA Ops:
  0.0 4.3 %copy-start = (bf16[16,64,1024]{2,1,0:T(8,128)(2,1)S(1)}, bf16[16,64,1024]{2,1,0:T(8,128)(2,1)}, u32[]{:S(2)}) copy-start(bf16[16,64,1024]{2,1,0:T(8,128)(2,1)} %param.12) | copy-start | bytes 6291460
  4.3 4.7 %copy-start.3 = (bf16[4,128,512]{2,1,0:T(8,128)(2,1)S(1)}, bf16[4,128,512]{2,1,0:T(8,128)(2,1)}, u32[]{:S(2)}) copy-start(bf16[4,128,512]{2,1,0:T(8,128)(2,1)} %param.18) | copy-start | bytes 1572868
  4.3 4.7 %copy-start.4 = (bf16[512,128]{1,0:T(8,128)(2,1)S(1)}, bf16[512,128]{1,0:T(8,128)(2,1)}, u32[]{:S(2)}) copy-start(bf16[512,128]{1,0:T(8,128)(2,1)} %param.20) | copy-start | bytes 393220
  9.1 50.0 %collective-permute-start.3 = (bf16[4,128,640]{2,1,0:T(8,128)(2,1)S(1)}, bf16[4,128,640]{2,1,0:T(8,128)(2,1)}, u32[]{:S(2)}, u32[]{:S(2)}) collective-permute-start(bf16[4,128,640]{2,1,0:T(8,128)(2,1)S(1)} %pad_maximum_fusion), channel_id=1, source_target_pairs={{0,14},{2,0},{4,2},{6,4},{8,6},{10,8},{12,10},{14,12},{1,15},{3,1}... | collective-permute-start | bytes 1966088 | tf_op jit(solution)/shard_map/ppermute | solution.py:393
  12.3 48.7 %collective-permute-start.6 = (bf16[4,128,640]{2,1,0:T(8,128)(2,1)S(1)}, bf16[4,128,640]{2,1,0:T(8,128)(2,1)S(1)}, u32[]{:S(2)}, u32[]{:S(2)}) collective-permute-start(bf16[4,128,640]{2,1,0:T(8,128)(2,1)S(1)} %pad_maximum_fusion), channel_id=1, source_target_pairs={{0,2},{2,4},{4,6},{6,8},{8,10},{10,12},{12,14},{14,0},{1,3},{3,5},... | collective-permute-start | bytes 1966088 | tf_op jit(solution)/shard_map/ppermute | solution.py:392
  59.1 20.6 %collective-permute-start.4 = (bf16[4,128,640]{2,1,0:T(8,128)(2,1)}, bf16[4,128,640]{2,1,0:T(8,128)(2,1)}, u32[]{:S(2)}, u32[]{:S(2)}) collective-permute-start(bf16[4,128,640]{2,1,0:T(8,128)(2,1)} %collective-permute-done.3), channel_id=1, source_target_pairs={{0,14},{2,0},{4,2},{6,4},{8,6},{10,8},{12,10},{14,12},{1,15},{3,1}... | collective-permute-start | bytes 1966088 | tf_op jit(solution)/shard_map/ppermute | solution.py:393
  61.0 20.6 %collective-permute-start.7 = (bf16[4,128,640]{2,1,0:T(8,128)(2,1)S(1)}, bf16[4,128,640]{2,1,0:T(8,128)(2,1)}, u32[]{:S(2)}, u32[]{:S(2)}) collective-permute-start(bf16[4,128,640]{2,1,0:T(8,128)(2,1)S(1)} %collective-permute-done.6), channel_id=1, source_target_pairs={{0,2},{2,4},{4,6},{6,8},{8,10},{10,12},{12,14},{14,0},{1,3},{3,5},... | collective-permute-start | bytes 1966088 | tf_op jit(solution)/shard_map/ppermute | solution.py:392
  66.2 107.8 %all-to-all-start = ((bf16[16,64,1024]{2,1,0:T(8,128)(2,1)}), bf16[16,64,1024]{2,1,0:T(8,128)(2,1)}, u32[]{:S(2)}, u32[]{:S(2)}) async-start(bf16[16,64,1024]{2,1,0:T(8,128)(2,1)} %select_convert_fusion), calls=%async_computation | async-start | bytes 4194304 | tf_op jit(solution)/shard_map/all_to_all | solution.py:357
  79.7 18.2 %collective-permute-start.5 = (bf16[4,128,640]{2,1,0:T(8,128)(2,1)}, bf16[4,128,640]{2,1,0:T(8,128)(2,1)S(1)}, u32[]{:S(2)}, u32[]{:S(2)}) collective-permute-start(bf16[4,128,640]{2,1,0:T(8,128)(2,1)} %collective-permute-done.4), channel_id=1, source_target_pairs={{0,14},{2,0},{4,2},{6,4},{8,6},{10,8},{12,10},{14,12},{1,15},{3,1}... | collective-permute-start | bytes 1966088 | tf_op jit(solution)/shard_map/ppermute | solution.py:393
  81.7 18.2 %collective-permute-start.8 = (bf16[4,128,640]{2,1,0:T(8,128)(2,1)}, bf16[4,128,640]{2,1,0:T(8,128)(2,1)S(1)}, u32[]{:S(2)}, u32[]{:S(2)}) collective-permute-start(bf16[4,128,640]{2,1,0:T(8,128)(2,1)} %collective-permute-done.7), channel_id=1, source_target_pairs={{0,2},{2,4},{4,6},{6,8},{8,10},{10,12},{12,14},{14,0},{1,3},{3,5},... | collective-permute-start | bytes 1966088 | tf_op jit(solution)/shard_map/ppermute | solution.py:392
  97.9 10.3 %collective-permute-start.10 = (bf16[2,128,640]{2,1,0:T(8,128)(2,1)S(1)}, bf16[2,128,640]{2,1,0:T(8,128)(2,1)S(1)}, u32[]{:S(2)}, u32[]{:S(2)}) collective-permute-start(bf16[2,128,640]{2,1,0:T(8,128)(2,1)S(1)} %slice.9), channel_id=1, source_target_pairs={{0,14},{2,0},{4,2},{6,4},{8,6},{10,8},{12,10},{14,12},{1,15},{3,1}... | collective-permute-start | bytes 983048 | tf_op jit(solution)/shard_map/ppermute | solution.py:398
  99.9 20.4 %copy-start.1 = (bf16[2,256,512]{2,1,0:T(8,128)(2,1)S(1)}, bf16[2,256,512]{2,1,0:T(8,128)(2,1)}, u32[]{:S(2)}) copy-start(bf16[2,256,512]{2,1,0:T(8,128)(2,1)} %v_own.1) | copy-start | bytes 1572868
  99.9 22.3 %copy-start.7 = (bf16[512]{0:T(512)(128)(2,1)S(1)}, bf16[512]{0:T(512)(128)(2,1)}, u32[]{:S(2)}) copy-start(bf16[512]{0:T(512)(128)(2,1)} %param.19) | copy-start | bytes 3076
  99.9 24.8 %copy-start.6 = (bf16[1024]{0:T(1024)(128)(2,1)S(1)}, bf16[1024]{0:T(1024)(128)(2,1)}, u32[]{:S(2)}) copy-start(bf16[1024]{0:T(1024)(128)(2,1)} %param.21) | copy-start | bytes 6148
  99.9 24.8 %copy-start.8 = (bf16[256]{0:T(256)(128)(2,1)S(1)}, bf16[256]{0:T(256)(128)(2,1)}, u32[]{:S(2)}) copy-start(bf16[256]{0:T(256)(128)(2,1)} %param.23) | copy-start | bytes 1540
  100.0 9.9 %collective-permute-start.9 = (bf16[2,128,640]{2,1,0:T(8,128)(2,1)S(1)}, bf16[2,128,640]{2,1,0:T(8,128)(2,1)S(1)}, u32[]{:S(2)}, u32[]{:S(2)}) collective-permute-start(bf16[2,128,640]{2,1,0:T(8,128)(2,1)S(1)} %slice.8), channel_id=1, source_target_pairs={{0,2},{2,4},{4,6},{6,8},{8,10},{10,12},{12,14},{14,0},{1,3},{3,5},... | collective-permute-start | bytes 983048 | tf_op jit(solution)/shard_map/ppermute | solution.py:397
  114.6 12.4 %collective-permute-start.11 = (bf16[8,4,128,640]{3,2,1,0:T(8,128)(2,1)}, bf16[8,4,128,640]{3,2,1,0:T(8,128)(2,1)}, u32[]{:S(2)}, u32[]{:S(2)}) collective-permute-start(bf16[8,4,128,640]{3,2,1,0:T(8,128)(2,1)} %bitcast_dynamic-update-slice_fusion.w_own), channel_id=1, source_target_pairs={{0,1},{1,0},{2,3},{3,2},{4,5},{5,4},{6,7},{7,6},{8,9},{9,8},{10,11... | collective-permute-start | bytes 15728648 | tf_op jit(solution)/shard_map/ppermute | solution.py:354
  117.8 9.2 %collective-permute-start.1 = (bf16[2,512,256]{2,1,0:T(8,128)(2,1)S(1)}, bf16[2,512,256]{2,1,0:T(8,128)(2,1)}, u32[]{:S(2)}, u32[]{:S(2)}) collective-permute-start(bf16[2,512,256]{2,1,0:T(8,128)(2,1)S(1)} %bitcast.30), channel_id=1, source_target_pairs={{0,1},{1,0},{2,3},{3,2},{4,5},{5,4},{6,7},{7,6},{8,9},{9,8},{10,11... | collective-permute-start | bytes 1572872 | tf_op jit(solution)/shard_map/ppermute | solution.py:354
  120.3 6.8 %collective-permute-start.2 = (bf16[2,256,512]{2,1,0:T(8,128)(2,1)S(1)}, bf16[2,256,512]{2,1,0:T(8,128)(2,1)}, u32[]{:S(2)}, u32[]{:S(2)}) collective-permute-start(bf16[2,256,512]{2,1,0:T(8,128)(2,1)S(1)} %copy-done.1), channel_id=1, source_target_pairs={{0,1},{1,0},{2,3},{3,2},{4,5},{5,4},{6,7},{7,6},{8,9},{9,8},{10,11... | collective-permute-start | bytes 1572872 | tf_op jit(solution)/shard_map/ppermute | solution.py:354
  122.3 4.8 %collective-permute-start = (bf16[1,512]{1,0:T(2,128)(2,1)S(1)}, bf16[1,512]{1,0:T(2,128)(2,1)S(1)}, u32[]{:S(2)}, u32[]{:S(2)}) collective-permute-start(bf16[1,512]{1,0:T(2,128)(2,1)S(1)} %broadcast_in_dim.111.gain_own), channel_id=1, source_target_pairs={{0,1},{1,0},{2,3},{3,2},{4,5},{5,4},{6,7},{7,6},{8,9},{9,8},{10,11... | collective-permute-start | bytes 3080 | tf_op jit(solution)/shard_map/ppermute | solution.py:354
  174.0 1.0 copy-start.2
  175.1 29.4 %copy-start.5 = (s32[16,1]{0,1:T(1,128)S(1)}, s32[16,1]{0,1:T(1,128)}, u32[]{:S(2)}) copy-start(s32[16,1]{0,1:T(1,128)} %param.13) | copy-start | bytes 196
  186.1 30.1 %all-to-all-start.1 = ((f32[32,1,64]{2,1,0:T(1,128)}), f32[32,1,64]{2,1,0:T(1,128)S(1)}, u32[]{:S(2)}, u32[]{:S(2)}) async-start(f32[32,1,64]{2,1,0:T(1,128)} %bitcast.15), calls=%async_computation.1 | async-start | bytes 32768 | tf_op jit(solution)/shard_map/all_to_all | solution.py:408

commit v9 on v8

--- a/solution.py
+++ b/solution.py
@@ -413,13 +413,12 @@
         tiled=True,
     ).reshape(peers, cores * block_width)
     row_scores = jnp.sum(jnp.where(goes[:, :, None], returned[:, None, :], 0.0), axis=0)
-    lane = jnp.where(
-        inside < block_fill[:, None], packed % cores * block_width + packed // cores, -1
-    )
+    lane = packed % cores * block_width + packed // cores
     wanted = lane[:, :, None] == lax.broadcasted_iota(
         jnp.int32, (blocks, block_width, cores * block_width), 2
     )
-    return jnp.sum(jnp.where(wanted, row_scores[:, None, :], 0.0), axis=2)
+    block_scores = jnp.sum(jnp.where(wanted, row_scores[:, None, :], 0.0), axis=2)
+    return jnp.where(inside < block_fill[:, None], block_scores, jnp.zeros_like(block_scores))
 
 
 def solution(mesh):

time: 221 us -> 220 us (level)
    unnamed x24 -> x26, local copies, waits for them, and re-layouts: 10.2 us -> 10.2 us
where the time goes in v9:
time: 220 us; the launch traced here: 218 us
  starting transfers between devices  105 us (48%)
  waiting for transfers between devices  77.5 us (35%)
  local copies, waits for them, and re-layouts  12.7 us (6%)
  Pallas kernels  10.4 us (5%)
  other arithmetic  7.11 us (3%)
  matrix products  4.68 us (2%)
    ppermute x3, starting transfers between devices, local(): from_below = lax.ppermute(from_below, 'routers', up)  50.4 us
    all_to_all x1, waiting for transfers between devices, exchanged(): return lax.all_to_all(x, 'users', split_axis=0, concat_axis=0, tiled=True)  46.9 us
    all_to_all x1, starting transfers between devices, local(): lax.all_to_all(back.reshape(peers * cores, block_width), ('users', 'heads...  18.3 us
    ppermute x3, waiting for transfers between devices, local(): from_above = lax.ppermute(from_above, 'routers', down)  14.8 us
    all_to_all x1, starting transfers between devices, exchanged(): return lax.all_to_all(x, 'users', split_axis=0, concat_axis=0, tiled=True)  13.5 us
    all_to_all x1, waiting for transfers between devices, local(): lax.all_to_all(back.reshape(peers * cores, block_width), ('users', 'heads...  11.8 us
    pallas_call x1, Pallas kernels, score_units(): pl.pallas_call(score_kernel, out_shape=jax.ShapeDtypeStruct((rows // lane...  10.4 us
    unnamed x26, local copies, waits for them, and re-layouts  10.2 us
  transfers between devices with their start and end apart: 14, of which 6 were waited for; matrix products, arithmetic and copies ran while one was open for 5% of the time, Pallas kernels for 0%

profile of v9, /device:TPU:78, one launch (start us, length us, event | category | flops | bytes accessed | tf_op | source)
XLA Modules:
  0.0 218.1 jit_solution(2089224348636885736)
XLA Ops:
  0.0 0.8 broadcast_compare_fusion.3
  0.8 0.9 select_reduce_fusion.4
  1.8 0.7 multiply_bitcast_fusion
  2.5 0.7 iota_compare_fusion.4
  3.2 0.1 fusion.9
  3.3 0.1 add.135
  3.5 0.1 add.139
  3.5 0.1 lt.70
  3.7 4.7 %select_convert_fusion = bf16[16,64,1024]{2,1,0:T(8,128)(2,1)} fusion(bf16[16]{0:T(256)(128)(2,1)S(1)} %convert_add_fusion, s32[16]{0:T(128)S(1)} %get-tuple-element.13, pred[1024]{0:T(1024)(128)(4,1)S(1)} %get-tuple-element.22, pred[1024]{0:T(1024)(128)(4,1)S(1)} %get-tuple-element.23, pred[16]{0:T(512)(128)(4,1)S(1)} %broadcast_compare_fusion, ...), kind=kOutput, calls=%fused_computation | convolution fusion | flops 2163212288 | bytes 4204752 | tf_op jit(solution)/shard_map/dot_general | solution.py:378
  8.4 3.2 %collective-permute-start.3 = (bf16[4,128,640]{2,1,0:T(8,128)(2,1)S(1)}, bf16[4,128,640]{2,1,0:T(8,128)(2,1)}, u32[]{:S(2)}, u32[]{:S(2)}) collective-permute-start(bf16[4,128,640]{2,1,0:T(8,128)(2,1)S(1)} %pad_maximum_fusion), channel_id=1, source_target_pairs={{0,14},{2,0},{4,2},{6,4},{8,6},{10,8},{12,10},{14,12},{1,15},{3,1}... | collective-permute-start | bytes 1966088 | tf_op jit(solution)/shard_map/ppermute | solution.py:393
  11.7 40.1 %collective-permute-start.6 = (bf16[4,128,640]{2,1,0:T(8,128)(2,1)S(1)}, bf16[4,128,640]{2,1,0:T(8,128)(2,1)S(1)}, u32[]{:S(2)}, u32[]{:S(2)}) collective-permute-start(bf16[4,128,640]{2,1,0:T(8,128)(2,1)S(1)} %pad_maximum_fusion), channel_id=1, source_target_pairs={{0,2},{2,4},{4,6},{6,8},{8,10},{10,12},{12,14},{14,0},{1,3},{3,5},... | collective-permute-start | bytes 1966088 | tf_op jit(solution)/shard_map/ppermute | solution.py:392
  51.7 6.7 %collective-permute-done.3 = bf16[4,128,640]{2,1,0:T(8,128)(2,1)} collective-permute-done((bf16[4,128,640]{2,1,0:T(8,128)(2,1)S(1)}, bf16[4,128,640]{2,1,0:T(8,128)(2,1)}, u32[]{:S(2)}, u32[]{:S(2)}) %collective-permute-start.3) | collective-permute-done | bytes 655392 | tf_op jit(solution)/shard_map/ppermute | solution.py:393
  58.4 1.9 collective-permute-start.4
  60.4 5.2 %collective-permute-start.7 = (bf16[4,128,640]{2,1,0:T(8,128)(2,1)S(1)}, bf16[4,128,640]{2,1,0:T(8,128)(2,1)}, u32[]{:S(2)}, u32[]{:S(2)}) collective-permute-start(bf16[4,128,640]{2,1,0:T(8,128)(2,1)S(1)} %collective-permute-done.6), channel_id=1, source_target_pairs={{0,2},{2,4},{4,6},{6,8},{8,10},{10,12},{12,14},{14,0},{1,3},{3,5},... | collective-permute-start | bytes 1966088 | tf_op jit(solution)/shard_map/ppermute | solution.py:392
  65.6 13.5 %all-to-all-start = ((bf16[16,64,1024]{2,1,0:T(8,128)(2,1)}), bf16[16,64,1024]{2,1,0:T(8,128)(2,1)}, u32[]{:S(2)}, u32[]{:S(2)}) async-start(bf16[16,64,1024]{2,1,0:T(8,128)(2,1)} %select_convert_fusion), calls=%async_computation | async-start | bytes 4194304 | tf_op jit(solution)/shard_map/all_to_all | solution.py:357
  79.0 2.0 collective-permute-start.5
  81.0 5.2 %collective-permute-start.8 = (bf16[4,128,640]{2,1,0:T(8,128)(2,1)}, bf16[4,128,640]{2,1,0:T(8,128)(2,1)S(1)}, u32[]{:S(2)}, u32[]{:S(2)}) collective-permute-start(bf16[4,128,640]{2,1,0:T(8,128)(2,1)} %collective-permute-done.7), channel_id=1, source_target_pairs={{0,2},{2,4},{4,6},{6,8},{8,10},{10,12},{12,14},{14,0},{1,3},{3,5},... | collective-permute-start | bytes 1966088 | tf_op jit(solution)/shard_map/ppermute | solution.py:392
  86.2 0.9 bitcast_dynamic-update-slice_fusion.6
  87.1 2.0 bitcast_dynamic-update-slice_fusion.5
  89.1 8.1 %collective-permute-done.5 = bf16[4,128,640]{2,1,0:T(8,128)(2,1)S(1)} collective-permute-done((bf16[4,128,640]{2,1,0:T(8,128)(2,1)}, bf16[4,128,640]{2,1,0:T(8,128)(2,1)S(1)}, u32[]{:S(2)}, u32[]{:S(2)}) %collective-permute-start.5) | collective-permute-done | bytes 655392 | tf_op jit(solution)/shard_map/ppermute | solution.py:393
  97.3 2.0 collective-permute-start.10
  99.3 5.3 %collective-permute-start.9 = (bf16[2,128,640]{2,1,0:T(8,128)(2,1)S(1)}, bf16[2,128,640]{2,1,0:T(8,128)(2,1)S(1)}, u32[]{:S(2)}, u32[]{:S(2)}) collective-permute-start(bf16[2,128,640]{2,1,0:T(8,128)(2,1)S(1)} %slice.8), channel_id=1, source_target_pairs={{0,2},{2,4},{4,6},{6,8},{8,10},{10,12},{12,14},{14,0},{1,3},{3,5},... | collective-permute-start | bytes 983048 | tf_op jit(solution)/shard_map/ppermute | solution.py:397
  104.6 2.0 bitcast_dynamic-update-slice_fusion.4
  106.6 0.9 bitcast_dynamic-update-slice_fusion.3
  107.5 1.7 collective-permute-done.9
  109.2 1.0 fusion.7
  110.2 1.0 bitcast_dynamic-update-slice_fusion.2
  111.1 2.0 bitcast_dynamic-update-slice_fusion.1
  113.1 0.9 bitcast_dynamic-update-slice_fusion.w_own
  114.0 1.9 collective-permute-start.11
  116.0 1.2 copy.15
  117.2 2.4 %collective-permute-start.1 = (bf16[2,512,256]{2,1,0:T(8,128)(2,1)S(1)}, bf16[2,512,256]{2,1,0:T(8,128)(2,1)}, u32[]{:S(2)}, u32[]{:S(2)}) collective-permute-start(bf16[2,512,256]{2,1,0:T(8,128)(2,1)S(1)} %bitcast.30), channel_id=1, source_target_pairs={{0,1},{1,0},{2,3},{3,2},{4,5},{5,4},{6,7},{7,6},{8,9},{9,8},{10,11... | collective-permute-start | bytes 1572872 | tf_op jit(solution)/shard_map/ppermute | solution.py:354
  119.7 2.0 collective-permute-start.2
  121.6 2.4 %collective-permute-start = (bf16[1,512]{1,0:T(2,128)(2,1)S(1)}, bf16[1,512]{1,0:T(2,128)(2,1)S(1)}, u32[]{:S(2)}, u32[]{:S(2)}) collective-permute-start(bf16[1,512]{1,0:T(2,128)(2,1)S(1)} %broadcast_in_dim.113.gain_own), channel_id=1, source_target_pairs={{0,1},{1,0},{2,3},{3,2},{4,5},{5,4},{6,7},{7,6},{8,9},{9,8},{10,11... | collective-permute-start | bytes 3080 | tf_op jit(solution)/shard_map/ppermute | solution.py:354
  124.1 2.3 %collective-permute-done.gain_other = bf16[1,512]{1,0:T(2,128)(2,1)S(1)} collective-permute-done((bf16[1,512]{1,0:T(2,128)(2,1)S(1)}, bf16[1,512]{1,0:T(2,128)(2,1)S(1)}, u32[]{:S(2)}, u32[]{:S(2)}) %collective-permute-start) | collective-permute-done | bytes 1056 | tf_op jit(solution)/shard_map/ppermute | solution.py:354
  126.4 46.9 %all-to-all-done.x_hbm = bf16[16,64,1024]{2,1,0:T(8,128)(2,1)} async-done(((bf16[16,64,1024]{2,1,0:T(8,128)(2,1)}), bf16[16,64,1024]{2,1,0:T(8,128)(2,1)}, u32[]{:S(2)}, u32[]{:S(2)}) %all-to-all-start) | async-done | bytes 2097184 | tf_op jit(solution)/shard_map/all_to_all | solution.py:357
  173.3 1.0 copy-done.2
  174.4 10.4 %score_units.1 = f32[8,128]{1,0:T(8,128)S(1)} custom-call(s32[1]{0:T(128)} %bitcast.1.core_ref, bf16[1,512]{1,0:T(2,128)(2,1)S(1)} %broadcast_in_dim.113.gain_own, bf16[1,512]{1,0:T(2,128)(2,1)S(1)} %collective-permute-done.gain_other, bf16[1,1024]{1,0:T(2,128)(2,1)S(1)} %broadcast_in_dim.114.mlp_gain_ref, bf16[1,256]{1,0:T(2,128)(2,1)S(1)} %broadcast_in_dim.115.w_two_ref, ...), custom_call_target="tpu_custom_call" | custom-call | tf_op jit(solution)/shard_map/score_units/pallas_call | solution.py:300
  184.8 0.1 broadcast_in_dim.119
  184.8 0.6 broadcast_in_dim.120
  185.5 18.3 %all-to-all-start.1 = ((f32[32,1,64]{2,1,0:T(1,128)}), f32[32,1,64]{2,1,0:T(1,128)S(1)}, u32[]{:S(2)}, u32[]{:S(2)}) async-start(f32[32,1,64]{2,1,0:T(1,128)} %bitcast.15), calls=%async_computation.1 | async-start | bytes 32768 | tf_op jit(solution)/shard_map/all_to_all | solution.py:408
  203.8 11.8 %all-to-all-done.1 = f32[32,1,64]{2,1,0:T(1,128)S(1)} async-done(((f32[32,1,64]{2,1,0:T(1,128)}), f32[32,1,64]{2,1,0:T(1,128)S(1)}, u32[]{:S(2)}, u32[]{:S(2)}) %all-to-all-start.1) | async-done | bytes 8224 | tf_op jit(solution)/shard_map/all_to_all | solution.py:408
  215.6 0.5 broadcast.386
  216.1 0.7 reduce.3
  216.8 0.1 broadcast_in_dim.121
  216.9 0.1 select_reduce_fusion.1
  217.0 0.4 select_reduce_fusion
  217.4 0.7 broadcast_select_fusion
  (42 shorter events, 0.3 us)
Async XLA Ops:
  0.0 3.6 %copy-start = (bf16[16,64,1024]{2,1,0:T(8,128)(2,1)S(1)}, bf16[16,64,1024]{2,1,0:T(8,128)(2,1)}, u32[]{:S(2)}) copy-start(bf16[16,64,1024]{2,1,0:T(8,128)(2,1)} %param.12) | copy-start | bytes 6291460
  3.6 4.7 %copy-start.3 = (bf16[4,128,512]{2,1,0:T(8,128)(2,1)S(1)}, bf16[4,128,512]{2,1,0:T(8,128)(2,1)}, u32[]{:S(2)}) copy-start(bf16[4,128,512]{2,1,0:T(8,128)(2,1)} %param.18) | copy-start | bytes 1572868
  3.7 4.7 %copy-start.4 = (bf16[512,128]{1,0:T(8,128)(2,1)S(1)}, bf16[512,128]{1,0:T(8,128)(2,1)}, u32[]{:S(2)}) copy-start(bf16[512,128]{1,0:T(8,128)(2,1)} %param.20) | copy-start | bytes 393220
  8.4 50.0 %collective-permute-start.3 = (bf16[4,128,640]{2,1,0:T(8,128)(2,1)S(1)}, bf16[4,128,640]{2,1,0:T(8,128)(2,1)}, u32[]{:S(2)}, u32[]{:S(2)}) collective-permute-start(bf16[4,128,640]{2,1,0:T(8,128)(2,1)S(1)} %pad_maximum_fusion), channel_id=1, source_target_pairs={{0,14},{2,0},{4,2},{6,4},{8,6},{10,8},{12,10},{14,12},{1,15},{3,1}... | collective-permute-start | bytes 1966088 | tf_op jit(solution)/shard_map/ppermute | solution.py:393
  11.7 48.7 %collective-permute-start.6 = (bf16[4,128,640]{2,1,0:T(8,128)(2,1)S(1)}, bf16[4,128,640]{2,1,0:T(8,128)(2,1)S(1)}, u32[]{:S(2)}, u32[]{:S(2)}) collective-permute-start(bf16[4,128,640]{2,1,0:T(8,128)(2,1)S(1)} %pad_maximum_fusion), channel_id=1, source_target_pairs={{0,2},{2,4},{4,6},{6,8},{8,10},{10,12},{12,14},{14,0},{1,3},{3,5},... | collective-permute-start | bytes 1966088 | tf_op jit(solution)/shard_map/ppermute | solution.py:392
  58.4 20.6 %collective-permute-start.4 = (bf16[4,128,640]{2,1,0:T(8,128)(2,1)}, bf16[4,128,640]{2,1,0:T(8,128)(2,1)}, u32[]{:S(2)}, u32[]{:S(2)}) collective-permute-start(bf16[4,128,640]{2,1,0:T(8,128)(2,1)} %collective-permute-done.3), channel_id=1, source_target_pairs={{0,14},{2,0},{4,2},{6,4},{8,6},{10,8},{12,10},{14,12},{1,15},{3,1}... | collective-permute-start | bytes 1966088 | tf_op jit(solution)/shard_map/ppermute | solution.py:393
  60.4 20.6 %collective-permute-start.7 = (bf16[4,128,640]{2,1,0:T(8,128)(2,1)S(1)}, bf16[4,128,640]{2,1,0:T(8,128)(2,1)}, u32[]{:S(2)}, u32[]{:S(2)}) collective-permute-start(bf16[4,128,640]{2,1,0:T(8,128)(2,1)S(1)} %collective-permute-done.6), channel_id=1, source_target_pairs={{0,2},{2,4},{4,6},{6,8},{8,10},{10,12},{12,14},{14,0},{1,3},{3,5},... | collective-permute-start | bytes 1966088 | tf_op jit(solution)/shard_map/ppermute | solution.py:392
  65.6 107.8 %all-to-all-start = ((bf16[16,64,1024]{2,1,0:T(8,128)(2,1)}), bf16[16,64,1024]{2,1,0:T(8,128)(2,1)}, u32[]{:S(2)}, u32[]{:S(2)}) async-start(bf16[16,64,1024]{2,1,0:T(8,128)(2,1)} %select_convert_fusion), calls=%async_computation | async-start | bytes 4194304 | tf_op jit(solution)/shard_map/all_to_all | solution.py:357
  79.0 18.2 %collective-permute-start.5 = (bf16[4,128,640]{2,1,0:T(8,128)(2,1)}, bf16[4,128,640]{2,1,0:T(8,128)(2,1)S(1)}, u32[]{:S(2)}, u32[]{:S(2)}) collective-permute-start(bf16[4,128,640]{2,1,0:T(8,128)(2,1)} %collective-permute-done.4), channel_id=1, source_target_pairs={{0,14},{2,0},{4,2},{6,4},{8,6},{10,8},{12,10},{14,12},{1,15},{3,1}... | collective-permute-start | bytes 1966088 | tf_op jit(solution)/shard_map/ppermute | solution.py:393
  81.0 18.2 %collective-permute-start.8 = (bf16[4,128,640]{2,1,0:T(8,128)(2,1)}, bf16[4,128,640]{2,1,0:T(8,128)(2,1)S(1)}, u32[]{:S(2)}, u32[]{:S(2)}) collective-permute-start(bf16[4,128,640]{2,1,0:T(8,128)(2,1)} %collective-permute-done.7), channel_id=1, source_target_pairs={{0,2},{2,4},{4,6},{6,8},{8,10},{10,12},{12,14},{14,0},{1,3},{3,5},... | collective-permute-start | bytes 1966088 | tf_op jit(solution)/shard_map/ppermute | solution.py:392
  97.3 10.2 %collective-permute-start.10 = (bf16[2,128,640]{2,1,0:T(8,128)(2,1)S(1)}, bf16[2,128,640]{2,1,0:T(8,128)(2,1)S(1)}, u32[]{:S(2)}, u32[]{:S(2)}) collective-permute-start(bf16[2,128,640]{2,1,0:T(8,128)(2,1)S(1)} %slice.9), channel_id=1, source_target_pairs={{0,14},{2,0},{4,2},{6,4},{8,6},{10,8},{12,10},{14,12},{1,15},{3,1}... | collective-permute-start | bytes 983048 | tf_op jit(solution)/shard_map/ppermute | solution.py:398
  99.3 20.4 %copy-start.1 = (bf16[2,256,512]{2,1,0:T(8,128)(2,1)S(1)}, bf16[2,256,512]{2,1,0:T(8,128)(2,1)}, u32[]{:S(2)}) copy-start(bf16[2,256,512]{2,1,0:T(8,128)(2,1)} %v_own.1) | copy-start | bytes 1572868
  99.3 22.3 %copy-start.8 = (bf16[512]{0:T(512)(128)(2,1)S(1)}, bf16[512]{0:T(512)(128)(2,1)}, u32[]{:S(2)}) copy-start(bf16[512]{0:T(512)(128)(2,1)} %param.19) | copy-start | bytes 3076
  99.3 24.8 %copy-start.7 = (bf16[1024]{0:T(1024)(128)(2,1)S(1)}, bf16[1024]{0:T(1024)(128)(2,1)}, u32[]{:S(2)}) copy-start(bf16[1024]{0:T(1024)(128)(2,1)} %param.21) | copy-start | bytes 6148
  99.3 24.8 %copy-start.9 = (bf16[256]{0:T(256)(128)(2,1)S(1)}, bf16[256]{0:T(256)(128)(2,1)}, u32[]{:S(2)}) copy-start(bf16[256]{0:T(256)(128)(2,1)} %param.23) | copy-start | bytes 1540
  99.3 9.9 %collective-permute-start.9 = (bf16[2,128,640]{2,1,0:T(8,128)(2,1)S(1)}, bf16[2,128,640]{2,1,0:T(8,128)(2,1)S(1)}, u32[]{:S(2)}, u32[]{:S(2)}) collective-permute-start(bf16[2,128,640]{2,1,0:T(8,128)(2,1)S(1)} %slice.8), channel_id=1, source_target_pairs={{0,2},{2,4},{4,6},{6,8},{8,10},{10,12},{12,14},{14,0},{1,3},{3,5},... | collective-permute-start | bytes 983048 | tf_op jit(solution)/shard_map/ppermute | solution.py:397
  114.0 12.4 %collective-permute-start.11 = (bf16[8,4,128,640]{3,2,1,0:T(8,128)(2,1)}, bf16[8,4,128,640]{3,2,1,0:T(8,128)(2,1)}, u32[]{:S(2)}, u32[]{:S(2)}) collective-permute-start(bf16[8,4,128,640]{3,2,1,0:T(8,128)(2,1)} %bitcast_dynamic-update-slice_fusion.w_own), channel_id=1, source_target_pairs={{0,1},{1,0},{2,3},{3,2},{4,5},{5,4},{6,7},{7,6},{8,9},{9,8},{10,11... | collective-permute-start | bytes 15728648 | tf_op jit(solution)/shard_map/ppermute | solution.py:354
  117.2 9.2 %collective-permute-start.1 = (bf16[2,512,256]{2,1,0:T(8,128)(2,1)S(1)}, bf16[2,512,256]{2,1,0:T(8,128)(2,1)}, u32[]{:S(2)}, u32[]{:S(2)}) collective-permute-start(bf16[2,512,256]{2,1,0:T(8,128)(2,1)S(1)} %bitcast.30), channel_id=1, source_target_pairs={{0,1},{1,0},{2,3},{3,2},{4,5},{5,4},{6,7},{7,6},{8,9},{9,8},{10,11... | collective-permute-start | bytes 1572872 | tf_op jit(solution)/shard_map/ppermute | solution.py:354
  119.7 6.8 %collective-permute-start.2 = (bf16[2,256,512]{2,1,0:T(8,128)(2,1)S(1)}, bf16[2,256,512]{2,1,0:T(8,128)(2,1)}, u32[]{:S(2)}, u32[]{:S(2)}) collective-permute-start(bf16[2,256,512]{2,1,0:T(8,128)(2,1)S(1)} %copy-done.1), channel_id=1, source_target_pairs={{0,1},{1,0},{2,3},{3,2},{4,5},{5,4},{6,7},{7,6},{8,9},{9,8},{10,11... | collective-permute-start | bytes 1572872 | tf_op jit(solution)/shard_map/ppermute | solution.py:354
  121.6 4.8 %collective-permute-start = (bf16[1,512]{1,0:T(2,128)(2,1)S(1)}, bf16[1,512]{1,0:T(2,128)(2,1)S(1)}, u32[]{:S(2)}, u32[]{:S(2)}) collective-permute-start(bf16[1,512]{1,0:T(2,128)(2,1)S(1)} %broadcast_in_dim.113.gain_own), channel_id=1, source_target_pairs={{0,1},{1,0},{2,3},{3,2},{4,5},{5,4},{6,7},{7,6},{8,9},{9,8},{10,11... | collective-permute-start | bytes 3080 | tf_op jit(solution)/shard_map/ppermute | solution.py:354
  173.3 1.0 copy-start.2
  174.4 29.4 %copy-start.5 = (s32[16,1]{0,1:T(1,128)S(1)}, s32[16,1]{0,1:T(1,128)}, u32[]{:S(2)}) copy-start(s32[16,1]{0,1:T(1,128)} %param.13) | copy-start | bytes 196
  174.4 43.0 %copy-start.6 = (s32[16]{0:T(128)S(1)}, s32[16]{0:T(128)}, u32[]{:S(2)}) copy-start(s32[16]{0:T(128)} %param.15) | copy-start | bytes 196
  185.5 30.1 %all-to-all-start.1 = ((f32[32,1,64]{2,1,0:T(1,128)}), f32[32,1,64]{2,1,0:T(1,128)S(1)}, u32[]{:S(2)}, u32[]{:S(2)}) async-start(f32[32,1,64]{2,1,0:T(1,128)} %bitcast.15), calls=%async_computation.1 | async-start | bytes 32768 | tf_op jit(solution)/shard_map/all_to_all | solution.py:408
